TPU v7x, 32 devices: a whole 2x2x4 slice. The times are simulated.
32 devices in a mesh: prow: 8 (over y, x, core), pcol: 4 (over z).
Axes of the slice: x: 2, y: 2, z: 4, core: 2. Of those that a mesh axis runs over, the one named last changes fastest.
Arguments:
- rhs: bfloat16 [128, 64, 256], P('prow'), may hold values from -6 to 6
- blocks: bfloat16 [128, 16, 256, 256], P('prow', 'pcol'), may hold values from -0.0625 to 0.0625
- inverses: bfloat16 [128, 256, 256], P('prow'), may hold values from -1 to 2.1, as said below
- columns: int32 [128, 16], P('prow', 'pcol'), may hold values from 0 to 127, as said below
- counts: int32 [128, 4], P('prow', 'pcol'), may hold values from 0 to 4, as said below
Outputs:
- solved: bfloat16 [128, 64, 256], P('prow')
Inputs may be any that keep to these rules, and one draw needn't show every extreme that they name: `columns`: slot c of array row o names a block row k (level order) of an earlier level than that of o, with (k // 8) % 4 == c // 4, or 0 where no such block row exists; only the first counts[o, c // 4] slots of a group are used. `counts`: 0 where the group has no earlier block row (level 0 in particular); otherwise 1 or more. `inverses`: each tile is the inverse of a lower triangular diagonal block, itself lower triangular.
All inputs are finite; a program needn't handle non-finite values.
Results may differ from a plain program's by a relative error of at most 0.0054.
Values may be sent and summed in bfloat16 or wider, within the bound.
No kernel may reach another device: no remote copies, remote signals or barrier semaphores. Data moves between devices by JAX's collectives and lax.ppermute only.
A program may use at most 64 MiB of HBM per device.

v0:
```python
import jax
import jax.numpy as jnp
from jax import lax
from jax.sharding import PartitionSpec as P

LEVELS = 8
LR = 2


def body(rhs, blocks, inverses, columns, counts):
    side_count = rhs.shape[1]
    block_size = rhs.shape[2]
    prow_count = lax.axis_size("prow")
    pcol_count = lax.axis_size("pcol")
    per_level = LR * prow_count
    slot_count = columns.shape[1]
    active_mask = (jnp.arange(slot_count, dtype=jnp.int32)[None, :] < counts).astype(jnp.bfloat16)
    store_rows = LEVELS * prow_count
    solved_store = jnp.zeros((store_rows, side_count, block_size), jnp.bfloat16)
    solution = jnp.zeros(rhs.shape, jnp.bfloat16)

    def advance(level_no, carry):
        solved_store, solution = carry
        first_row = level_no * LR
        column_ids = lax.dynamic_slice_in_dim(columns, first_row, LR, 0)
        active = lax.dynamic_slice_in_dim(active_mask, first_row, LR, 0)
        panels = lax.dynamic_slice_in_dim(blocks, first_row, LR, 0)
        right_side = lax.dynamic_slice_in_dim(rhs, first_row, LR, 0)
        inverse_tiles = lax.dynamic_slice_in_dim(inverses, first_row, LR, 0)
        store_ids = column_ids // per_level * prow_count + column_ids % prow_count
        gathered = jnp.take(solved_store, store_ids, axis=0) * active[:, :, None, None]
        update_sum = jnp.einsum(
            "scrj,scij->sri", gathered, panels, preferred_element_type=jnp.float32
        )
        which_half = (lax.axis_index("pcol") - level_no * LR) % pcol_count
        keep_half = (which_half < LR).astype(jnp.bfloat16)
        half_index = jnp.minimum(which_half, LR - 1)
        summed = lax.psum(update_sum, "pcol")
        residual = (right_side.astype(jnp.float32) - summed).astype(jnp.bfloat16)
        solved_now = jnp.einsum(
            "srb,sab->sra", residual, inverse_tiles, preferred_element_type=jnp.float32
        ).astype(jnp.bfloat16)
        payload = lax.dynamic_index_in_dim(solved_now, half_index, 0, keepdims=True) * keep_half
        level_block = lax.all_gather(payload[None], "prow", axis=0, tiled=True)
        column_block = level_block.reshape((prow_count, side_count, block_size))
        solved_store = lax.dynamic_update_slice_in_dim(
            solved_store, column_block, level_no * prow_count, 0
        )
        solution = lax.dynamic_update_slice_in_dim(solution, solved_now, first_row, 0)
        return (solved_store, solution)

    solved_store, solution = lax.fori_loop(0, LEVELS, advance, (solved_store, solution))
    return solution


def solution(mesh):
    placed = (
        P("prow", None, None),
        P("prow", "pcol", None, None),
        P("prow", None, None),
        P("prow", "pcol"),
        P("prow", "pcol"),
    )
    return jax.shard_map(
        body, mesh=mesh, in_specs=placed, out_specs=P("prow", None, None), check_vma=False
    )
```

profile of v0, /device:TPU:0, one launch (start us, length us, event | category | flops | bytes accessed | tf_op | source)
XLA Modules:
  0.0 398.1 jit_solution(2024207592908420231)
XLA Ops:
  8.3 382.1 %while.18 = (s32[]{:T(128)}, bf16[64,64,256]{2,1,0:T(8,128)(2,1)S(1)}, bf16[16,64,256]{2,1,0:T(8,128)(2,1)S(1)}, bf16[16,64,256]{2,1,0:T(8,128)(2,1)}, s32[16,4]...) while((s32[]{:T(128)}, ...), condition=%wide.region_2.3_spmd, body=%wide.region_0.2_spmd.sunk | while | flops 84329728 | bytes 4233478 | solution.py:52
  9.1 2.3 convolution_bitcast_fusion.2
  11.5 37.5 %all-reduce.2.cloned.1.call-done = f32[2,64,256]{2,1,0:T(8,128)} async-done(((f32[2,64,256]{2,1,0:T(8,128)}), f32[2,64,256]{2,1,0:T(8,128)}) %all-reduce.2.cloned.1.call-update) | async-done | bytes 131088 | tf_op jit(solution)/shard_map/while/body/eval_jaxpr/psum | solution.py:38
  49.0 1.3 constant_dynamic-update-slice_fusion.4
  50.2 9.2 %all-gather.2 = bf16[8,64,256]{2,1,0:T(8,128)(2,1)S(1)} all-gather(bf16[1,64,256]{2,1,0:T(8,128)(2,1)S(1)} %dynamic-slice_multiply_fusion.2), channel_id=2, replica_groups=mesh['prow'=8,'pcol'=4] {'prow'}, dimensions={0}, use_global_device_ids=true | all-gather | bytes 294912 | tf_op jit(solution)/shard_map/while/body/eval_jaxpr/all_gather | solution.py:44
  60.3 2.3 convolution_bitcast_fusion.2
  62.7 33.6 %all-reduce.2.cloned.1.call-done = f32[2,64,256]{2,1,0:T(8,128)} async-done(((f32[2,64,256]{2,1,0:T(8,128)}), f32[2,64,256]{2,1,0:T(8,128)}) %all-reduce.2.cloned.1.call-update) | async-done | bytes 131088 | tf_op jit(solution)/shard_map/while/body/eval_jaxpr/psum | solution.py:38
  96.2 1.3 constant_dynamic-update-slice_fusion.4
  97.5 9.2 %all-gather.2 = bf16[8,64,256]{2,1,0:T(8,128)(2,1)S(1)} all-gather(bf16[1,64,256]{2,1,0:T(8,128)(2,1)S(1)} %dynamic-slice_multiply_fusion.2), channel_id=2, replica_groups=mesh['prow'=8,'pcol'=4] {'prow'}, dimensions={0}, use_global_device_ids=true | all-gather | bytes 294912 | tf_op jit(solution)/shard_map/while/body/eval_jaxpr/all_gather | solution.py:44
  107.6 2.3 convolution_bitcast_fusion.2
  110.0 33.5 %all-reduce.2.cloned.1.call-done = f32[2,64,256]{2,1,0:T(8,128)} async-done(((f32[2,64,256]{2,1,0:T(8,128)}), f32[2,64,256]{2,1,0:T(8,128)}) %all-reduce.2.cloned.1.call-update) | async-done | bytes 131088 | tf_op jit(solution)/shard_map/while/body/eval_jaxpr/psum | solution.py:38
  143.5 1.3 constant_dynamic-update-slice_fusion.4
  144.8 9.2 %all-gather.2 = bf16[8,64,256]{2,1,0:T(8,128)(2,1)S(1)} all-gather(bf16[1,64,256]{2,1,0:T(8,128)(2,1)S(1)} %dynamic-slice_multiply_fusion.2), channel_id=2, replica_groups=mesh['prow'=8,'pcol'=4] {'prow'}, dimensions={0}, use_global_device_ids=true | all-gather | bytes 294912 | tf_op jit(solution)/shard_map/while/body/eval_jaxpr/all_gather | solution.py:44
  154.8 2.3 convolution_bitcast_fusion.2
  157.2 33.5 %all-reduce.2.cloned.1.call-done = f32[2,64,256]{2,1,0:T(8,128)} async-done(((f32[2,64,256]{2,1,0:T(8,128)}), f32[2,64,256]{2,1,0:T(8,128)}) %all-reduce.2.cloned.1.call-update) | async-done | bytes 131088 | tf_op jit(solution)/shard_map/while/body/eval_jaxpr/psum | solution.py:38
  190.8 1.3 constant_dynamic-update-slice_fusion.4
  192.1 9.2 %all-gather.2 = bf16[8,64,256]{2,1,0:T(8,128)(2,1)S(1)} all-gather(bf16[1,64,256]{2,1,0:T(8,128)(2,1)S(1)} %dynamic-slice_multiply_fusion.2), channel_id=2, replica_groups=mesh['prow'=8,'pcol'=4] {'prow'}, dimensions={0}, use_global_device_ids=true | all-gather | bytes 294912 | tf_op jit(solution)/shard_map/while/body/eval_jaxpr/all_gather | solution.py:44
  202.1 2.3 convolution_bitcast_fusion.2
  204.5 33.5 %all-reduce.2.cloned.1.call-done = f32[2,64,256]{2,1,0:T(8,128)} async-done(((f32[2,64,256]{2,1,0:T(8,128)}), f32[2,64,256]{2,1,0:T(8,128)}) %all-reduce.2.cloned.1.call-update) | async-done | bytes 131088 | tf_op jit(solution)/shard_map/while/body/eval_jaxpr/psum | solution.py:38
  238.1 1.3 constant_dynamic-update-slice_fusion.4
  239.3 9.2 %all-gather.2 = bf16[8,64,256]{2,1,0:T(8,128)(2,1)S(1)} all-gather(bf16[1,64,256]{2,1,0:T(8,128)(2,1)S(1)} %dynamic-slice_multiply_fusion.2), channel_id=2, replica_groups=mesh['prow'=8,'pcol'=4] {'prow'}, dimensions={0}, use_global_device_ids=true | all-gather | bytes 294912 | tf_op jit(solution)/shard_map/while/body/eval_jaxpr/all_gather | solution.py:44
  249.4 2.3 convolution_bitcast_fusion.2
  251.8 33.5 %all-reduce.2.cloned.1.call-done = f32[2,64,256]{2,1,0:T(8,128)} async-done(((f32[2,64,256]{2,1,0:T(8,128)}), f32[2,64,256]{2,1,0:T(8,128)}) %all-reduce.2.cloned.1.call-update) | async-done | bytes 131088 | tf_op jit(solution)/shard_map/while/body/eval_jaxpr/psum | solution.py:38
  285.3 1.3 constant_dynamic-update-slice_fusion.4
  286.6 9.2 %all-gather.2 = bf16[8,64,256]{2,1,0:T(8,128)(2,1)S(1)} all-gather(bf16[1,64,256]{2,1,0:T(8,128)(2,1)S(1)} %dynamic-slice_multiply_fusion.2), channel_id=2, replica_groups=mesh['prow'=8,'pcol'=4] {'prow'}, dimensions={0}, use_global_device_ids=true | all-gather | bytes 294912 | tf_op jit(solution)/shard_map/while/body/eval_jaxpr/all_gather | solution.py:44
  296.7 2.3 convolution_bitcast_fusion.2
  299.1 33.5 %all-reduce.2.cloned.1.call-done = f32[2,64,256]{2,1,0:T(8,128)} async-done(((f32[2,64,256]{2,1,0:T(8,128)}), f32[2,64,256]{2,1,0:T(8,128)}) %all-reduce.2.cloned.1.call-update) | async-done | bytes 131088 | tf_op jit(solution)/shard_map/while/body/eval_jaxpr/psum | solution.py:38
  332.6 1.3 constant_dynamic-update-slice_fusion.4
  333.9 9.2 %all-gather.2 = bf16[8,64,256]{2,1,0:T(8,128)(2,1)S(1)} all-gather(bf16[1,64,256]{2,1,0:T(8,128)(2,1)S(1)} %dynamic-slice_multiply_fusion.2), channel_id=2, replica_groups=mesh['prow'=8,'pcol'=4] {'prow'}, dimensions={0}, use_global_device_ids=true | all-gather | bytes 294912 | tf_op jit(solution)/shard_map/while/body/eval_jaxpr/all_gather | solution.py:44
  343.9 2.3 convolution_bitcast_fusion.2
  346.4 33.5 %all-reduce.2.cloned.1.call-done = f32[2,64,256]{2,1,0:T(8,128)} async-done(((f32[2,64,256]{2,1,0:T(8,128)}), f32[2,64,256]{2,1,0:T(8,128)}) %all-reduce.2.cloned.1.call-update) | async-done | bytes 131088 | tf_op jit(solution)/shard_map/while/body/eval_jaxpr/psum | solution.py:38
  381.2 9.2 %all-gather.2 = bf16[8,64,256]{2,1,0:T(8,128)(2,1)S(1)} all-gather(bf16[1,64,256]{2,1,0:T(8,128)(2,1)S(1)} %dynamic-slice_multiply_fusion.2), channel_id=2, replica_groups=mesh['prow'=8,'pcol'=4] {'prow'}, dimensions={0}, use_global_device_ids=true | all-gather | bytes 294912 | tf_op jit(solution)/shard_map/while/body/eval_jaxpr/all_gather | solution.py:44
  (79 shorter events, 10.1 us)
Async XLA Ops:
  8.3 40.6 %all-reduce.2.cloned.1.call-start = ((), (), s32[]{:S(2)}) async-start(), calls=%async_computation | async-start | bytes 262144 | tf_op jit(solution)/shard_map/while/body/eval_jaxpr/psum | solution.py:38
  59.5 36.7 %all-reduce.2.cloned.1.call-start = ((), (), s32[]{:S(2)}) async-start(), calls=%async_computation | async-start | bytes 262144 | tf_op jit(solution)/shard_map/while/body/eval_jaxpr/psum | solution.py:38
  106.8 36.7 %all-reduce.2.cloned.1.call-start = ((), (), s32[]{:S(2)}) async-start(), calls=%async_computation | async-start | bytes 262144 | tf_op jit(solution)/shard_map/while/body/eval_jaxpr/psum | solution.py:38
  154.1 36.7 %all-reduce.2.cloned.1.call-start = ((), (), s32[]{:S(2)}) async-start(), calls=%async_computation | async-start | bytes 262144 | tf_op jit(solution)/shard_map/while/body/eval_jaxpr/psum | solution.py:38
  201.4 36.7 %all-reduce.2.cloned.1.call-start = ((), (), s32[]{:S(2)}) async-start(), calls=%async_computation | async-start | bytes 262144 | tf_op jit(solution)/shard_map/while/body/eval_jaxpr/psum | solution.py:38
  248.6 36.7 %all-reduce.2.cloned.1.call-start = ((), (), s32[]{:S(2)}) async-start(), calls=%async_computation | async-start | bytes 262144 | tf_op jit(solution)/shard_map/while/body/eval_jaxpr/psum | solution.py:38
  295.9 36.7 %all-reduce.2.cloned.1.call-start = ((), (), s32[]{:S(2)}) async-start(), calls=%async_computation | async-start | bytes 262144 | tf_op jit(solution)/shard_map/while/body/eval_jaxpr/psum | solution.py:38
  343.2 36.7 %all-reduce.2.cloned.1.call-start = ((), (), s32[]{:S(2)}) async-start(), calls=%async_computation | async-start | bytes 262144 | tf_op jit(solution)/shard_map/while/body/eval_jaxpr/psum | solution.py:38
  390.4 0.8 copy-start
Sparse Core Ops, SparseCore 0:
  11.6 37.3 all-reduce.1
  62.8 33.4 all-reduce.1
  110.1 33.4 all-reduce.1
  157.3 33.4 all-reduce.1
  204.6 33.4 all-reduce.1
  251.9 33.4 all-reduce.1
  299.2 33.4 all-reduce.1
  346.4 33.4 all-reduce.1
where the time goes:
time: 399 us; the launch traced here: 398 us
  waiting for transfers between devices  272 us (68%)
  blocking collectives  74 us (19%)
  matrix products  28.7 us (7%)
  between operations  13.4 us (3%)
  local copies, waits for them, and re-layouts  7.25 us (2%)
    psum x8, waiting for transfers between devices, advance(): summed = lax.psum(update_sum, 'pcol')  272 us
    all_gather x8, blocking collectives, advance(): level_block = lax.all_gather(payload[None], 'prow', axis=0, tiled=True)  74 us
    dot_general x8, matrix products, advance(): jnp.einsum('scrj,scij->sri', gathered, panels, preferred_element_type=jnp...  18.7 us
    dot_general x8, matrix products, advance(): jnp.einsum('srb,sab->sra', residual, inverse_tiles, preferred_element_typ...  10 us
  transfers between devices with their start and end apart: 8, of which 8 were waited for; matrix products, arithmetic and copies ran while one was open for 0% of the time, Pallas kernels for 0%

commit v1 on v0

v1 whole, which is shorter than its diff:
```python
import functools

import jax
import jax.numpy as jnp
from jax import lax
from jax.experimental import pallas as pl
from jax.experimental.pallas import tpu as pltpu
from jax.sharding import PartitionSpec as P

LEVELS = 8
LR = 2
BF16 = jnp.bfloat16
F32 = jnp.float32
VM = pl.BlockSpec(memory_space=pltpu.VMEM)
SM = pl.BlockSpec(memory_space=pltpu.SMEM)


def dot_t(left, right):
    return lax.dot_general(left, right, (((1,), (1,)), ((), ())), preferred_element_type=F32)


def role(level):
    return lax.rem(lax.axis_index("pcol") + 2 * LEVELS * LR * lax.axis_size("pcol") - level * LR, lax.axis_size("pcol"))


def call(body, outs, ins, specs=None, aliases=None):
    return pl.pallas_call(
        body,
        out_shape=outs,
        in_specs=specs or [VM] * len(ins),
        out_specs=[VM] * len(outs),
        input_output_aliases=aliases or {},
    )(*ins)


def spread(store, pieces, level, local):
    rows = 2 * len(pieces)

    def body(*refs):
        out = refs[-1]
        out[...] = refs[0][...]

        @pl.when(role(level) < LR)
        def _():
            for j, piece in enumerate(refs[1:-1]):
                out[pl.ds(local * rows + 2 * j, 2)] = piece[...]

    return call(body, [jax.ShapeDtypeStruct(store.shape, store.dtype)], [store, *pieces])[0]


def partials(level, newest, table, store, own, other, kinds):
    slots = own.shape[1]
    shape = (2, store.shape[1], store.shape[2])

    def row_sum(table_ref, store_ref, own_ref, other_ref, row, pair):
        blocks_ref = other_ref if pair else own_ref
        total = None
        for j in range(slots):
            at = table_ref[level * LR + row, pair * slots + j]
            part = dot_t(store_ref[at], blocks_ref[row, j])
            total = part if total is None else total + part
        return total

    def body(table_ref, store_ref, own_ref, other_ref, *outs):
        place = role(newest) if newest is not None else 0

        def work():
            for out, (turn, kind) in zip(outs, kinds):
                row = lax.rem(place + turn, LR) if newest is not None else turn
                for pair in range(2):
                    out[pair] = row_sum(table_ref, store_ref, own_ref, other_ref, row, pair).astype(kind)

        if newest is None:
            work()
        else:
            pl.when(place < LR)(work)

    outs = [jax.ShapeDtypeStruct(shape, kind) for _, kind in kinds]
    return call(body, outs, [table, store, own, other], specs=[SM, VM, VM, VM])


def solve(level, rhs_own, rhs_other, inv_own, inv_other, terms):
    def body(ro, rp, io, ip, *refs):
        *terms_refs, out = refs
        place = role(level)

        @pl.when(place < LR)
        def _():
            for pair in range(2):
                r_ref, i_ref = (rp, ip) if pair else (ro, io)
                rest = r_ref[place].astype(F32)
                for term in terms_refs:
                    rest = rest - term[pair].astype(F32)
                out[pair] = dot_t(rest.astype(BF16), i_ref[place]).astype(BF16)

    shape = jax.ShapeDtypeStruct((2,) + rhs_own.shape[1:], BF16)
    return call(body, [shape], [rhs_own, rhs_other, inv_own, inv_other, *terms])[0]


def solve_first(rhs, inv, half):
    def body(r, i, keep, send):
        place = role(0)
        core = lax.rem(lax.axis_index("prow"), 2)

        @pl.when(place < LR)
        def _():
            tile = i[place]
            for out, part in ((keep, core), (send, 1 - core)):
                out[...] = dot_t(r[place, pl.ds(pl.multiple_of(part * half, half), half)], tile).astype(BF16)

    shape = jax.ShapeDtypeStruct((half, rhs.shape[2]), BF16)
    return call(body, [shape, shape], [rhs, inv])


def solve_last(rhs_own, rhs_other, inv_own, inv_other, parts):
    count = len(parts)

    def body(ro, rp, io, ip, *refs):
        own, other, held = refs[-3:]
        me = lax.axis_index("pcol")
        for k in range(count):
            held[jnp.bitwise_xor(me, k)] = refs[k][...]
        for pair in range(2):
            r_ref, i_ref, out = (rp, ip, other) if pair else (ro, io, own)
            for row in range(LR):
                rest = r_ref[row].astype(F32)
                for k in range(count):
                    rest = rest - held[k, row, pair].astype(F32)
                out[row] = dot_t(rest.astype(BF16), i_ref[row]).astype(BF16)

    shape = jax.ShapeDtypeStruct(rhs_own.shape, BF16)
    return pl.pallas_call(
        body,
        out_shape=[shape, shape],
        in_specs=[VM] * (4 + count),
        out_specs=[VM, VM],
        scratch_shapes=[pltpu.VMEM((count,) + parts[0].shape, BF16)],
    )(rhs_own, rhs_other, inv_own, inv_other, *parts)


def body(rhs, blocks, inverses, columns, counts):
    rows, sides, size = rhs.shape
    slots = columns.shape[1]
    half = sides // 2
    prow_count = lax.axis_size("prow")
    pcol_count = lax.axis_size("pcol")
    groups = pcol_count // LR
    locals_count = rows // pcol_count
    me = lax.axis_index("prow")
    core = me % 2

    def prow_swap(x, k):
        return lax.ppermute(x, "prow", [(i, i ^ k) for i in range(prow_count)])

    def pcol_swap(x, k):
        return lax.ppermute(x, "pcol", [(i, i ^ k) for i in range(pcol_count)])

    def between(x, first, second, turn):
        pairs = []
        for a in range(LR):
            s, d = (first * LR + a) % pcol_count, (second * LR + (a + turn) % LR) % pcol_count
            pairs += [(s, d), (d, s)]
        return lax.ppermute(x, "pcol", sorted(set(pairs)))

    keep, send = solve_first(rhs[:LR], inverses[:LR], half)
    solved = [jnp.stack([keep, prow_swap(send, 1)])]

    live = jnp.arange(slots, dtype=jnp.int32)[None, :] < counts
    coded = jnp.where(live, columns, -1)
    coded = jnp.concatenate([coded, prow_swap(coded, 1)], axis=1)
    zero_row = locals_count * prow_count
    at = coded // prow_count // pcol_count * prow_count + ((coded % prow_count) ^ me)
    table = jnp.where(coded < 0, zero_row, at)
    halves = rhs.reshape(rows, 2, half, size)
    mine = lax.dynamic_index_in_dim(halves, core, 1, keepdims=False)
    theirs = prow_swap(lax.dynamic_index_in_dim(halves, 1 - core, 1, keepdims=False), 1)
    near = prow_swap(blocks[LR:2 * LR], 1)
    far = prow_swap(blocks, 1)
    inverses_other = prow_swap(inverses, 1)

    def own_blocks(level):
        return blocks[level * LR:(level + 1) * LR]

    def other_blocks(level):
        return near if level == 1 else far[level * LR:(level + 1) * LR]

    def level_of(x, level):
        return x[level * LR:(level + 1) * LR]

    store = jnp.zeros((zero_row + 1, half, size), BF16)
    waiting = {level: [] for level in range(LEVELS)}
    for level in range(1, LEVELS):
        newest = level - 1
        y = solved[newest]
        pieces = [y] + [prow_swap(y, k) for k in range(2, prow_count, 2)]
        store = spread(store, pieces, newest, newest * LR // pcol_count)
        if level == LEVELS - 1:
            parts = partials(level, None, table, store, own_blocks(level), other_blocks(level), [(0, BF16), (1, BF16)])
            whole = jnp.stack(parts)
            final = [whole] + [pcol_swap(whole, k) for k in range(1, pcol_count)]
            own, other = solve_last(level_of(mine, level), level_of(theirs, level), level_of(inverses, level),
                                    level_of(inverses_other, level), final)
            break
        straight, crossed = partials(level, newest, table, store, own_blocks(level), other_blocks(level), [(0, BF16), (1, BF16)])
        terms = [between(straight, newest, level, 0), between(crossed, newest, level, 1)]
        for ahead in range(1, groups):
            later = level + ahead
            if later >= LEVELS - 1:
                continue
            mine_next = ahead == groups - 1
            kinds = [(0, F32 if mine_next else BF16), (1, BF16)]
            a, b = partials(later, newest, table, store, own_blocks(later), other_blocks(later), kinds)
            if mine_next:
                waiting[later] += [a, between(b, newest, newest, 1)]
            else:
                waiting[later] += [between(a, newest, later, 0), between(b, newest, later, 1)]
        solved.append(solve(level, level_of(mine, level), level_of(theirs, level), level_of(inverses, level),
                            level_of(inverses_other, level), terms + waiting[level]))

    group = lax.axis_index("pcol") // LR
    done = LEVELS - 1
    cycles = -(-done // groups)
    held = []
    for i in range(cycles):
        pick = solved[min(i * groups, done - 1)]
        for g in range(1, groups):
            pick = jnp.where(group == g, solved[min(i * groups + g, done - 1)], pick)
        held.append(pick)
    held = jnp.stack(held)
    held = jnp.stack([held[:, 0], prow_swap(held[:, 1], 1)], axis=1)
    spread_rows = [held] + [pcol_swap(held, k) for k in range(1, pcol_count)]
    swapped = prow_swap(other, 1)

    def assemble(*refs):
        *sources, own_ref, swapped_ref, out = refs
        col = lax.axis_index("pcol")
        my_core = lax.rem(lax.axis_index("prow"), 2)
        mine_at = pl.ds(pl.multiple_of(my_core * half, half), half)
        theirs_at = pl.ds(pl.multiple_of((1 - my_core) * half, half), half)
        for k, source in enumerate(sources):
            for i in range(cycles):
                row = i * pcol_count + jnp.bitwise_xor(col, k)
                out[row, mine_at] = source[i, 0]
                out[row, theirs_at] = source[i, 1]
        for s in range(LR):
            out[done * LR + s, mine_at] = own_ref[s]
            out[done * LR + s, theirs_at] = swapped_ref[s]

    return call(assemble, [jax.ShapeDtypeStruct(rhs.shape, BF16)], [*spread_rows, own, swapped])[0]


def solution(mesh):
    placed = (
        P("prow", None, None),
        P("prow", "pcol", None, None),
        P("prow", None, None),
        P("prow", "pcol"),
        P("prow", "pcol"),
    )
    return jax.shard_map(
        body, mesh=mesh, in_specs=placed, out_specs=P("prow", None, None), check_vma=False
    )
```

time: 399 us -> 220 us (0.55)
  waiting for transfers between devices: 272 us -> 47.4 us
  blocking collectives: 74 us -> 0 us
  starting transfers between devices: 0.33 us -> 74.2 us
  Pallas kernels: 0 us -> 63.4 us
  matrix products: 28.7 us -> 0 us
  local copies, waits for them, and re-layouts: 7.25 us -> 29.9 us
  between operations: 13.4 us -> 0.49 us
    psum x8 -> x0, waiting for transfers between devices: 272 us -> none  [advance(): summed = lax.psum(update_sum, 'pcol')]
    ppermute x0 -> x52, starting transfers between devices: none -> 74.2 us  [the longest x17 34.8 us: between(): return lax.ppermute(x, 'pcol', sorted(set(pairs)))]
    all_gather x8 -> x0, blocking collectives: 74 us -> none  [advance(): level_block = lax.all_gather(payload[None], 'prow', axis=0, tiled=True)]
    pallas_call x0 -> x28, Pallas kernels: none -> 63.4 us  [the longest x27 61.4 us: call(): pl.pallas_call(body, out_shape=outs, in_specs=specs or [VM] * len(ins), o...]
    ppermute x0 -> x52, waiting for transfers between devices: none -> 47.4 us  [the longest x17 20.2 us: between(): return lax.ppermute(x, 'pcol', sorted(set(pairs)))]
    dot_general x16 -> x0, matrix products: 28.7 us -> none  [the longest x8 18.7 us: advance(): jnp.einsum('scrj,scij->sri', gathered, panels, preferred_element_type=jnp...]
    slice x0 -> x8, local copies, waits for them, and re-layouts: none -> 17.5 us  [the longest x1 5.92 us: own_blocks(): return blocks[level * LR:(level + 1) * LR]]
    unnamed x2 -> x117, local copies, waits for them, and re-layouts: 0.79 us -> 11.5 us
  transfers between devices with their start and end apart: 8 -> 52, of which waited for: 8 -> 23; matrix products, arithmetic and copies ran while one was open for 0% -> 7% of each run, Pallas kernels for 0% -> 21%
where the time goes in v1:
time: 220 us; the launch traced here: 219 us
  starting transfers between devices  74.2 us (34%)
  Pallas kernels  63.4 us (29%)
  waiting for transfers between devices  47.4 us (22%)
  local copies, waits for them, and re-layouts  29.9 us (14%)
  other arithmetic  3.11 us (1%)
    pallas_call x27, Pallas kernels, call(): pl.pallas_call(body, out_shape=outs, in_specs=specs or [VM] * len(ins), o...  61.4 us
    ppermute x17, starting transfers between devices, between(): return lax.ppermute(x, 'pcol', sorted(set(pairs)))  34.8 us
    ppermute x29, starting transfers between devices, prow_swap(): return lax.ppermute(x, 'prow', [(i, i ^ k) for i in range(prow_count)])  30.5 us
    ppermute x17, waiting for transfers between devices, between(): return lax.ppermute(x, 'pcol', sorted(set(pairs)))  20.2 us
    ppermute x29, waiting for transfers between devices, prow_swap(): return lax.ppermute(x, 'prow', [(i, i ^ k) for i in range(prow_count)])  17.6 us
    unnamed x117, local copies, waits for them, and re-layouts  11.5 us
    ppermute x6, waiting for transfers between devices, pcol_swap(): return lax.ppermute(x, 'pcol', [(i, i ^ k) for i in range(pcol_count)])  9.54 us
    ppermute x6, starting transfers between devices, pcol_swap(): return lax.ppermute(x, 'pcol', [(i, i ^ k) for i in range(pcol_count)])  8.9 us
  transfers between devices with their start and end apart: 52, of which 23 were waited for; matrix products, arithmetic and copies ran while one was open for 7% of the time, Pallas kernels for 21%

profile of v1, /device:TPU:0, one launch (start us, length us, event | category | flops | bytes accessed | tf_op | source)
XLA Modules:
  0.0 218.5 jit_solution(6162896453693654014)
XLA Ops:
  0.7 5.9 %fusion.10 = (bf16[2,4,256,256]{3,2,1,0:T(8,128)(2,1)}, bf16[2,4,256,256]{3,2,1,0:T(8,128)(2,1)}, bf16[2,4,256,256]{3,2,1,0:T(8,128)(2,1)}, bf16[2,4,256,256]{3,...) fusion(bf16[16,4,256,256]{3,2,1,0:T(8,128)(2,1)} %param.6), kind=kLoop, calls=%fused_computation.40 | loop fusion | bytes 14680064 | tf_op jit(solution)/shard_map/slice | solution.py:182
  11.6 6.6 %collective-permute-done.3 = bf16[32,256]{1,0:T(8,128)(2,1)S(1)} collective-permute-done((bf16[32,256]{1,0:T(8,128)(2,1)}, bf16[32,256]{1,0:T(8,128)(2,1)S(1)}, u32[]{:S(2)}, u32[]{:S(2)}) %collective-permute-start.3) | collective-permute-done | bytes 16416 | tf_op jit(solution)/shard_map/ppermute | solution.py:153
  18.9 3.8 %collective-permute-start.6 = (bf16[2,32,256]{2,1,0:T(8,128)(2,1)S(1)}, bf16[2,32,256]{2,1,0:T(8,128)(2,1)S(1)}, u32[]{:S(2)}, u32[]{:S(2)}) collective-permute-start(bf16[2,32,256]{2,1,0:T(8,128)(2,1)S(1)} %pad_maximum_fusion.3.refs_1_), channel_id=1, source_target_pairs={{0,24},{4,28},{8,16},{12,20},{16,8},{20,12},{24,0},{28,4},{1,25},{... | collective-permute-start | bytes 98312 | tf_op jit(solution)/shard_map/ppermute | solution.py:153
  36.0 3.1 %shard_map.57 = (bf16[2,32,256]{2,1,0:T(8,128)(2,1)}, bf16[2,32,256]{2,1,0:T(8,128)(2,1)}) custom-call(s32[16,8]{1,0:T(8,128)} %fusion.3.table_ref, bf16[33,32,256]{2,1,0:T(8,128)(2,1)} %shard_map.56.store_ref.refs_0_, bf16[2,4,256,256]{3,2,1,0:T(8,128)(2,1)} %copy-done, bf16[2,4,256,256]{3,2,1,0:T(8,128)(2,1)} %collective-permute-done.7.other_ref), custom_call_target="tpu_custom_call" | custom-call | tf_op jit(solution)/shard_map/pallas_call | solution.py:27
  39.1 2.3 %collective-permute-start.8 = (bf16[2,32,256]{2,1,0:T(8,128)(2,1)}, bf16[2,32,256]{2,1,0:T(8,128)(2,1)S(1)}, u32[]{:S(2)}, u32[]{:S(2)}) collective-permute-start(bf16[2,32,256]{2,1,0:T(8,128)(2,1)} %get-tuple-element.35), channel_id=1, source_target_pairs={{0,2},{1,3},{2,0},{3,1},{4,6},{5,7},{6,4},{7,5},{8,10},{9,11},{10,... | collective-permute-start | bytes 98312 | tf_op jit(solution)/shard_map/ppermute | solution.py:163
  41.4 2.1 collective-permute-start.9
  43.5 2.7 %fusion.11 = (bf16[2,256,256]{2,1,0:T(8,128)(2,1)}, bf16[2,256,256]{2,1,0:T(8,128)(2,1)}, bf16[2,256,256]{2,1,0:T(8,128)(2,1)}, bf16[2,256,256]{2,1,0:T(8,128)(2...) fusion(bf16[16,256,256]{2,1,0:T(8,128)(2,1)} %collective-permute-done.1), kind=kLoop, calls=%fused_computation.41 | loop fusion | bytes 3670016 | tf_op jit(solution)/shard_map/slice | solution.py:188
  49.6 2.4 %collective-permute-start.12 = (bf16[2,32,256]{2,1,0:T(8,128)(2,1)}, bf16[2,32,256]{2,1,0:T(8,128)(2,1)S(1)}, u32[]{:S(2)}, u32[]{:S(2)}) collective-permute-start(bf16[2,32,256]{2,1,0:T(8,128)(2,1)} %shard_map.58.refs_1_), channel_id=1, source_target_pairs={{0,24},{4,28},{8,16},{12,20},{16,8},{20,12},{24,0},{28,4},{1,25},{... | collective-permute-start | bytes 98312 | tf_op jit(solution)/shard_map/ppermute | solution.py:153
  59.4 5.5 %fusion.9 = (bf16[2,4,256,256]{3,2,1,0:T(8,128)(2,1)}, bf16[2,4,256,256]{3,2,1,0:T(8,128)(2,1)}, bf16[2,4,256,256]{3,2,1,0:T(8,128)(2,1)}, bf16[2,4,256,256]{3,2...) fusion(bf16[16,4,256,256]{3,2,1,0:T(8,128)(2,1)} %collective-permute-done.13), kind=kLoop, calls=%fused_computation.39 | loop fusion | bytes 12582912 | tf_op jit(solution)/shard_map/slice | solution.py:185
  64.8 3.1 %shard_map.61 = (f32[2,32,256]{2,1,0:T(8,128)}, bf16[2,32,256]{2,1,0:T(8,128)(2,1)}) custom-call(s32[16,8]{1,0:T(8,128)} %fusion.3.table_ref, bf16[33,32,256]{2,1,0:T(8,128)(2,1)} %shard_map.56.store_ref.refs_0_, bf16[2,4,256,256]{3,2,1,0:T(8,128)(2,1)} %get-tuple-element.71.own_ref, bf16[2,4,256,256]{3,2,1,0:T(8,128)(2,1)} %get-tuple-element.66.other_ref), custom_call_target="tpu_custom_call" | custom-call | tf_op jit(solution)/shard_map/pallas_call | solution.py:27
  67.9 2.3 %shard_map.60 = (bf16[2,32,256]{2,1,0:T(8,128)(2,1)}, bf16[2,32,256]{2,1,0:T(8,128)(2,1)}) custom-call(s32[16,8]{1,0:T(8,128)} %fusion.3.table_ref, bf16[33,32,256]{2,1,0:T(8,128)(2,1)} %shard_map.59.store_ref.refs_0_, bf16[2,4,256,256]{3,2,1,0:T(8,128)(2,1)} %get-tuple-element.71.own_ref, bf16[2,4,256,256]{3,2,1,0:T(8,128)(2,1)} %get-tuple-element.66.other_ref), custom_call_target="tpu_custom_call" | custom-call | tf_op jit(solution)/shard_map/pallas_call | solution.py:27
  72.3 4.4 %collective-permute-start.15 = (bf16[2,32,256]{2,1,0:T(8,128)(2,1)}, bf16[2,32,256]{2,1,0:T(8,128)(2,1)S(1)}, u32[]{:S(2)}, u32[]{:S(2)}) collective-permute-start(bf16[2,32,256]{2,1,0:T(8,128)(2,1)} %get-tuple-element.38), channel_id=1, source_target_pairs={{0,3},{1,2},{2,1},{3,0},{4,7},{5,6},{6,5},{7,4},{8,11},{9,10},{10,... | collective-permute-start | bytes 98312 | tf_op jit(solution)/shard_map/ppermute | solution.py:163
  85.1 2.4 %shard_map.65 = (f32[2,32,256]{2,1,0:T(8,128)}, bf16[2,32,256]{2,1,0:T(8,128)(2,1)}) custom-call(s32[16,8]{1,0:T(8,128)} %fusion.3.table_ref, bf16[33,32,256]{2,1,0:T(8,128)(2,1)} %shard_map.59.store_ref.refs_0_, bf16[2,4,256,256]{3,2,1,0:T(8,128)(2,1)} %get-tuple-element.70.own_ref, bf16[2,4,256,256]{3,2,1,0:T(8,128)(2,1)} %get-tuple-element.65.other_ref), custom_call_target="tpu_custom_call" | custom-call | tf_op jit(solution)/shard_map/pallas_call | solution.py:27
  91.3 3.1 %shard_map.64 = (bf16[2,32,256]{2,1,0:T(8,128)(2,1)}, bf16[2,32,256]{2,1,0:T(8,128)(2,1)}) custom-call(s32[16,8]{1,0:T(8,128)} %fusion.3.table_ref, bf16[33,32,256]{2,1,0:T(8,128)(2,1)} %shard_map.63.store_ref.refs_0_, bf16[2,4,256,256]{3,2,1,0:T(8,128)(2,1)} %get-tuple-element.70.own_ref, bf16[2,4,256,256]{3,2,1,0:T(8,128)(2,1)} %get-tuple-element.65.other_ref), custom_call_target="tpu_custom_call" | custom-call | tf_op jit(solution)/shard_map/pallas_call | solution.py:27
  94.4 5.1 %collective-permute-start.20 = (bf16[2,32,256]{2,1,0:T(8,128)(2,1)}, bf16[2,32,256]{2,1,0:T(8,128)(2,1)S(1)}, u32[]{:S(2)}, u32[]{:S(2)}) collective-permute-start(bf16[2,32,256]{2,1,0:T(8,128)(2,1)} %get-tuple-element.41), channel_id=1, source_target_pairs={{0,2},{1,3},{2,0},{3,1},{4,6},{5,7},{6,4},{7,5},{8,10},{9,11},{10,... | collective-permute-start | bytes 98312 | tf_op jit(solution)/shard_map/ppermute | solution.py:163
  99.5 2.1 collective-permute-done.20.refs_0_
  101.6 3.8 %collective-permute-done.21.refs_1_ = bf16[2,32,256]{2,1,0:T(8,128)(2,1)S(1)} collective-permute-done((bf16[2,32,256]{2,1,0:T(8,128)(2,1)}, bf16[2,32,256]{2,1,0:T(8,128)(2,1)S(1)}, u32[]{:S(2)}, u32[]{:S(2)}) %collective-permute-start.21) | collective-permute-done | bytes 32800 | tf_op jit(solution)/shard_map/ppermute | solution.py:163
  111.2 3.1 %shard_map.69 = (f32[2,32,256]{2,1,0:T(8,128)}, bf16[2,32,256]{2,1,0:T(8,128)(2,1)}) custom-call(s32[16,8]{1,0:T(8,128)} %fusion.3.table_ref, bf16[33,32,256]{2,1,0:T(8,128)(2,1)} %shard_map.63.store_ref.refs_0_, bf16[2,4,256,256]{3,2,1,0:T(8,128)(2,1)} %get-tuple-element.69.own_ref, bf16[2,4,256,256]{3,2,1,0:T(8,128)(2,1)} %get-tuple-element.64.other_ref), custom_call_target="tpu_custom_call" | custom-call | tf_op jit(solution)/shard_map/pallas_call | solution.py:27
  119.4 2.4 %shard_map.68 = (bf16[2,32,256]{2,1,0:T(8,128)(2,1)}, bf16[2,32,256]{2,1,0:T(8,128)(2,1)}) custom-call(s32[16,8]{1,0:T(8,128)} %fusion.3.table_ref, bf16[33,32,256]{2,1,0:T(8,128)(2,1)} %shard_map.67.store_ref.refs_0_, bf16[2,4,256,256]{3,2,1,0:T(8,128)(2,1)} %get-tuple-element.69.own_ref, bf16[2,4,256,256]{3,2,1,0:T(8,128)(2,1)} %get-tuple-element.64.other_ref), custom_call_target="tpu_custom_call" | custom-call | tf_op jit(solution)/shard_map/pallas_call | solution.py:27
  121.8 4.4 %collective-permute-start.27 = (bf16[2,32,256]{2,1,0:T(8,128)(2,1)}, bf16[2,32,256]{2,1,0:T(8,128)(2,1)S(1)}, u32[]{:S(2)}, u32[]{:S(2)}) collective-permute-start(bf16[2,32,256]{2,1,0:T(8,128)(2,1)} %get-tuple-element.46), channel_id=1, source_target_pairs={{0,3},{1,2},{2,1},{3,0},{4,7},{5,6},{6,5},{7,4},{8,11},{9,10},{10,... | collective-permute-start | bytes 98312 | tf_op jit(solution)/shard_map/ppermute | solution.py:163
  134.6 2.4 %shard_map.73 = (f32[2,32,256]{2,1,0:T(8,128)}, bf16[2,32,256]{2,1,0:T(8,128)(2,1)}) custom-call(s32[16,8]{1,0:T(8,128)} %fusion.3.table_ref, bf16[33,32,256]{2,1,0:T(8,128)(2,1)} %shard_map.67.store_ref.refs_0_, bf16[2,4,256,256]{3,2,1,0:T(8,128)(2,1)} %get-tuple-element.68.own_ref, bf16[2,4,256,256]{3,2,1,0:T(8,128)(2,1)} %get-tuple-element.63.other_ref), custom_call_target="tpu_custom_call" | custom-call | tf_op jit(solution)/shard_map/pallas_call | solution.py:27
  140.8 3.1 %shard_map.72 = (bf16[2,32,256]{2,1,0:T(8,128)(2,1)}, bf16[2,32,256]{2,1,0:T(8,128)(2,1)}) custom-call(s32[16,8]{1,0:T(8,128)} %fusion.3.table_ref, bf16[33,32,256]{2,1,0:T(8,128)(2,1)} %shard_map.71.store_ref.refs_0_, bf16[2,4,256,256]{3,2,1,0:T(8,128)(2,1)} %get-tuple-element.68.own_ref, bf16[2,4,256,256]{3,2,1,0:T(8,128)(2,1)} %get-tuple-element.63.other_ref), custom_call_target="tpu_custom_call" | custom-call | tf_op jit(solution)/shard_map/pallas_call | solution.py:27
  143.9 5.1 %collective-permute-start.32 = (bf16[2,32,256]{2,1,0:T(8,128)(2,1)}, bf16[2,32,256]{2,1,0:T(8,128)(2,1)S(1)}, u32[]{:S(2)}, u32[]{:S(2)}) collective-permute-start(bf16[2,32,256]{2,1,0:T(8,128)(2,1)} %get-tuple-element.49), channel_id=1, source_target_pairs={{0,2},{1,3},{2,0},{3,1},{4,6},{5,7},{6,4},{7,5},{8,10},{9,11},{10,... | collective-permute-start | bytes 98312 | tf_op jit(solution)/shard_map/ppermute | solution.py:163
  149.0 2.1 collective-permute-done.32.refs_0_
  151.1 3.8 %collective-permute-done.33.refs_1_ = bf16[2,32,256]{2,1,0:T(8,128)(2,1)S(1)} collective-permute-done((bf16[2,32,256]{2,1,0:T(8,128)(2,1)}, bf16[2,32,256]{2,1,0:T(8,128)(2,1)S(1)}, u32[]{:S(2)}, u32[]{:S(2)}) %collective-permute-start.33) | collective-permute-done | bytes 32800 | tf_op jit(solution)/shard_map/ppermute | solution.py:163
  160.8 3.1 %shard_map.77 = (f32[2,32,256]{2,1,0:T(8,128)}, bf16[2,32,256]{2,1,0:T(8,128)(2,1)}) custom-call(s32[16,8]{1,0:T(8,128)} %fusion.3.table_ref, bf16[33,32,256]{2,1,0:T(8,128)(2,1)} %shard_map.71.store_ref.refs_0_, bf16[2,4,256,256]{3,2,1,0:T(8,128)(2,1)} %get-tuple-element.73.own_ref, bf16[2,4,256,256]{3,2,1,0:T(8,128)(2,1)} %get-tuple-element.62.other_ref), custom_call_target="tpu_custom_call" | custom-call | tf_op jit(solution)/shard_map/pallas_call | solution.py:27
  169.0 2.4 %shard_map.76 = (bf16[2,32,256]{2,1,0:T(8,128)(2,1)}, bf16[2,32,256]{2,1,0:T(8,128)(2,1)}) custom-call(s32[16,8]{1,0:T(8,128)} %fusion.3.table_ref, bf16[33,32,256]{2,1,0:T(8,128)(2,1)} %shard_map.75.store_ref.refs_0_, bf16[2,4,256,256]{3,2,1,0:T(8,128)(2,1)} %get-tuple-element.73.own_ref, bf16[2,4,256,256]{3,2,1,0:T(8,128)(2,1)} %get-tuple-element.62.other_ref), custom_call_target="tpu_custom_call" | custom-call | tf_op jit(solution)/shard_map/pallas_call | solution.py:27
  171.3 4.4 %collective-permute-start.39 = (bf16[2,32,256]{2,1,0:T(8,128)(2,1)}, bf16[2,32,256]{2,1,0:T(8,128)(2,1)S(1)}, u32[]{:S(2)}, u32[]{:S(2)}) collective-permute-start(bf16[2,32,256]{2,1,0:T(8,128)(2,1)} %get-tuple-element.54), channel_id=1, source_target_pairs={{0,3},{1,2},{2,1},{3,0},{4,7},{5,6},{6,5},{7,4},{8,11},{9,10},{10,... | collective-permute-start | bytes 98312 | tf_op jit(solution)/shard_map/ppermute | solution.py:163
  189.4 3.0 %shard_map.80 = (bf16[2,32,256]{2,1,0:T(8,128)(2,1)}, bf16[2,32,256]{2,1,0:T(8,128)(2,1)}) custom-call(s32[16,8]{1,0:T(8,128)} %fusion.3.table_ref, bf16[33,32,256]{2,1,0:T(8,128)(2,1)} %shard_map.79.store_ref, bf16[2,4,256,256]{3,2,1,0:T(8,128)(2,1)} %get-tuple-element.67.own_ref, bf16[2,4,256,256]{3,2,1,0:T(8,128)(2,1)} %get-tuple-element.61.other_ref), custom_call_target="tpu_custom_call" | custom-call | tf_op jit(solution)/shard_map/pallas_call | solution.py:27
  193.3 3.3 %collective-permute-start.50 = (bf16[2,2,32,256]{3,2,1,0:T(8,128)(2,1)S(1)}, bf16[2,2,32,256]{3,2,1,0:T(8,128)(2,1)S(1)}, u32[]{:S(2)}, u32[]{:S(2)}) collective-permute-start(bf16[2,2,32,256]{3,2,1,0:T(8,128)(2,1)S(1)} %pad_maximum_fusion.2.refs_0_), channel_id=1, source_target_pairs={{0,3},{1,2},{2,1},{3,0},{4,7},{5,6},{6,5},{7,4},{8,11},{9,10},{10,... | collective-permute-start | bytes 196616 | tf_op jit(solution)/shard_map/ppermute | solution.py:156
  197.2 3.8 %collective-permute-start.42 = (bf16[4,2,32,256]{3,2,1,0:T(8,128)(2,1)S(1)}, bf16[4,2,32,256]{3,2,1,0:T(8,128)(2,1)S(1)}, u32[]{:S(2)}, u32[]{:S(2)}) collective-permute-start(bf16[4,2,32,256]{3,2,1,0:T(8,128)(2,1)S(1)} %pad_maximum_fusion.1.refs_0_), channel_id=1, source_target_pairs={{0,1},{1,0},{2,3},{3,2},{4,5},{5,4},{6,7},{7,6},{8,9},{9,8},{10,11... | collective-permute-start | bytes 393224 | tf_op jit(solution)/shard_map/ppermute | solution.py:156
  202.2 9.5 %collective-permute-done.49.refs_2_ = bf16[2,2,32,256]{3,2,1,0:T(8,128)(2,1)S(1)} collective-permute-done((bf16[2,2,32,256]{3,2,1,0:T(8,128)(2,1)S(1)}, bf16[2,2,32,256]{3,2,1,0:T(8,128)(2,1)S(1)}, u32[]{:S(2)}, u32[]{:S(2)}) %collective-permute-start.49) | collective-permute-done | bytes 65568 | tf_op jit(solution)/shard_map/ppermute | solution.py:156
  (236 shorter events, 101.5 us)
Async XLA Ops:
  0.0 59.3 %collective-permute-start.13 = (bf16[16,4,256,256]{3,2,1,0:T(8,128)(2,1)}, bf16[16,4,256,256]{3,2,1,0:T(8,128)(2,1)}, u32[]{:S(2)}, u32[]{:S(2)}) collective-permute-start(bf16[16,4,256,256]{3,2,1,0:T(8,128)(2,1)} %param.6), channel_id=1, source_target_pairs={{0,4},{4,0},{8,12},{12,8},{16,20},{20,16},{24,28},{28,24},{1,5},{5... | collective-permute-start | bytes 25165832 | tf_op jit(solution)/shard_map/ppermute | solution.py:153
  0.6 42.9 %collective-permute-start.1 = (bf16[16,256,256]{2,1,0:T(8,128)(2,1)}, bf16[16,256,256]{2,1,0:T(8,128)(2,1)}, u32[]{:S(2)}, u32[]{:S(2)}) collective-permute-start(bf16[16,256,256]{2,1,0:T(8,128)(2,1)} %param.7), channel_id=1, source_target_pairs={{0,4},{4,0},{8,12},{12,8},{16,20},{20,16},{24,28},{28,24},{1,5},{5... | collective-permute-start | bytes 6291464 | tf_op jit(solution)/shard_map/ppermute | solution.py:153
  6.6 29.4 %collective-permute-start.7 = (bf16[2,4,256,256]{3,2,1,0:T(8,128)(2,1)S(1)}, bf16[2,4,256,256]{3,2,1,0:T(8,128)(2,1)}, u32[]{:S(2)}, u32[]{:S(2)}) collective-permute-start(bf16[2,4,256,256]{3,2,1,0:T(8,128)(2,1)S(1)} %get-tuple-element.72.own_ref), channel_id=1, source_target_pairs={{0,4},{4,0},{8,12},{12,8},{16,20},{20,16},{24,28},{28,24},{1,5},{5... | collective-permute-start | bytes 3145736 | tf_op jit(solution)/shard_map/ppermute | solution.py:153
  10.9 7.3 %collective-permute-start.3 = (bf16[32,256]{1,0:T(8,128)(2,1)}, bf16[32,256]{1,0:T(8,128)(2,1)S(1)}, u32[]{:S(2)}, u32[]{:S(2)}) collective-permute-start(bf16[32,256]{1,0:T(8,128)(2,1)} %get-tuple-element.34), channel_id=1, source_target_pairs={{0,4},{4,0},{8,12},{12,8},{16,20},{20,16},{24,28},{28,24},{1,5},{5... | collective-permute-start | bytes 49160 | tf_op jit(solution)/shard_map/ppermute | solution.py:153
  11.1 11.7 %collective-permute-start.2 = (s32[16,4]{1,0:T(8,128)S(1)}, s32[16,4]{1,0:T(8,128)S(1)}, u32[]{:S(2)}, u32[]{:S(2)}) collective-permute-start(s32[16,4]{1,0:T(8,128)S(1)} %fusion.5), channel_id=1, source_target_pairs={{0,4},{4,0},{8,12},{12,8},{16,20},{20,16},{24,28},{28,24},{1,5},{5... | collective-permute-start | bytes 776 | tf_op jit(solution)/shard_map/ppermute | solution.py:153
  22.8 12.5 %collective-permute-start = (bf16[16,32,256]{2,1,0:T(8,128)(2,1)S(1)}, bf16[16,32,256]{2,1,0:T(8,128)(2,1)S(1)}, u32[]{:S(2)}, u32[]{:S(2)}) collective-permute-start(bf16[16,32,256]{2,1,0:T(8,128)(2,1)S(1)} %dynamic-slice_bitcast_fusion), channel_id=1, source_target_pairs={{0,4},{4,0},{8,12},{12,8},{16,20},{20,16},{24,28},{28,24},{1,5},{5... | collective-permute-start | bytes 786440 | tf_op jit(solution)/shard_map/ppermute | solution.py:153
  39.1 7.1 %collective-permute-start.8 = (bf16[2,32,256]{2,1,0:T(8,128)(2,1)}, bf16[2,32,256]{2,1,0:T(8,128)(2,1)S(1)}, u32[]{:S(2)}, u32[]{:S(2)}) collective-permute-start(bf16[2,32,256]{2,1,0:T(8,128)(2,1)} %get-tuple-element.35), channel_id=1, source_target_pairs={{0,2},{1,3},{2,0},{3,1},{4,6},{5,7},{6,4},{7,5},{8,10},{9,11},{10,... | collective-permute-start | bytes 98312 | tf_op jit(solution)/shard_map/ppermute | solution.py:163
  70.3 6.4 %collective-permute-start.16 = (bf16[2,32,256]{2,1,0:T(8,128)(2,1)}, bf16[2,32,256]{2,1,0:T(8,128)(2,1)S(1)}, u32[]{:S(2)}, u32[]{:S(2)}) collective-permute-start(bf16[2,32,256]{2,1,0:T(8,128)(2,1)} %get-tuple-element.40), channel_id=1, source_target_pairs={{0,1},{1,0},{4,5},{5,4},{8,9},{9,8},{12,13},{13,12},{16,17},{17,16... | collective-permute-start | bytes 98312 | tf_op jit(solution)/shard_map/ppermute | solution.py:163
  72.3 6.8 %collective-permute-start.15 = (bf16[2,32,256]{2,1,0:T(8,128)(2,1)}, bf16[2,32,256]{2,1,0:T(8,128)(2,1)S(1)}, u32[]{:S(2)}, u32[]{:S(2)}) collective-permute-start(bf16[2,32,256]{2,1,0:T(8,128)(2,1)} %get-tuple-element.38), channel_id=1, source_target_pairs={{0,3},{1,2},{2,1},{3,0},{4,7},{5,6},{6,5},{7,4},{8,11},{9,10},{10,... | collective-permute-start | bytes 98312 | tf_op jit(solution)/shard_map/ppermute | solution.py:163
  81.6 6.5 %collective-permute-start.19 = (bf16[2,32,256]{2,1,0:T(8,128)(2,1)}, bf16[2,32,256]{2,1,0:T(8,128)(2,1)S(1)}, u32[]{:S(2)}, u32[]{:S(2)}) collective-permute-start(bf16[2,32,256]{2,1,0:T(8,128)(2,1)} %shard_map.62.refs_1_), channel_id=1, source_target_pairs={{0,24},{4,28},{8,16},{12,20},{16,8},{20,12},{24,0},{28,4},{1,25},{... | collective-permute-start | bytes 98312 | tf_op jit(solution)/shard_map/ppermute | solution.py:153
  87.4 12.0 %collective-permute-start.22 = (bf16[2,32,256]{2,1,0:T(8,128)(2,1)}, bf16[2,32,256]{2,1,0:T(8,128)(2,1)S(1)}, u32[]{:S(2)}, u32[]{:S(2)}) collective-permute-start(bf16[2,32,256]{2,1,0:T(8,128)(2,1)} %get-tuple-element.44), channel_id=1, source_target_pairs={{2,3},{3,2},{6,7},{7,6},{10,11},{11,10},{14,15},{15,14},{18,19},{1... | collective-permute-start | bytes 98312 | tf_op jit(solution)/shard_map/ppermute | solution.py:163
  94.4 7.2 %collective-permute-start.20 = (bf16[2,32,256]{2,1,0:T(8,128)(2,1)}, bf16[2,32,256]{2,1,0:T(8,128)(2,1)S(1)}, u32[]{:S(2)}, u32[]{:S(2)}) collective-permute-start(bf16[2,32,256]{2,1,0:T(8,128)(2,1)} %get-tuple-element.41), channel_id=1, source_target_pairs={{0,2},{1,3},{2,0},{3,1},{4,6},{5,7},{6,4},{7,5},{8,10},{9,11},{10,... | collective-permute-start | bytes 98312 | tf_op jit(solution)/shard_map/ppermute | solution.py:163
  107.7 8.5 %collective-permute-start.25 = (bf16[2,32,256]{2,1,0:T(8,128)(2,1)}, bf16[2,32,256]{2,1,0:T(8,128)(2,1)S(1)}, u32[]{:S(2)}, u32[]{:S(2)}) collective-permute-start(bf16[2,32,256]{2,1,0:T(8,128)(2,1)} %shard_map.66.refs_1_), channel_id=1, source_target_pairs={{0,24},{4,28},{8,16},{12,20},{16,8},{20,12},{24,0},{28,4},{1,25},{... | collective-permute-start | bytes 98312 | tf_op jit(solution)/shard_map/ppermute | solution.py:153
  109.1 7.1 %collective-permute-start.24 = (bf16[2,32,256]{2,1,0:T(8,128)(2,1)}, bf16[2,32,256]{2,1,0:T(8,128)(2,1)S(1)}, u32[]{:S(2)}, u32[]{:S(2)}) collective-permute-start(bf16[2,32,256]{2,1,0:T(8,128)(2,1)} %shard_map.66.refs_1_), channel_id=1, source_target_pairs={{0,16},{4,20},{8,24},{12,28},{16,0},{20,4},{24,8},{28,12},{1,17},{... | collective-permute-start | bytes 98312 | tf_op jit(solution)/shard_map/ppermute | solution.py:153
  109.7 6.6 %collective-permute-start.23 = (bf16[2,32,256]{2,1,0:T(8,128)(2,1)}, bf16[2,32,256]{2,1,0:T(8,128)(2,1)S(1)}, u32[]{:S(2)}, u32[]{:S(2)}) collective-permute-start(bf16[2,32,256]{2,1,0:T(8,128)(2,1)} %shard_map.66.refs_1_), channel_id=1, source_target_pairs={{0,8},{4,12},{8,0},{12,4},{16,24},{20,28},{24,16},{28,20},{1,9},{5... | collective-permute-start | bytes 98312 | tf_op jit(solution)/shard_map/ppermute | solution.py:153
  114.3 11.8 %collective-permute-start.28 = (bf16[2,32,256]{2,1,0:T(8,128)(2,1)}, bf16[2,32,256]{2,1,0:T(8,128)(2,1)S(1)}, u32[]{:S(2)}, u32[]{:S(2)}) collective-permute-start(bf16[2,32,256]{2,1,0:T(8,128)(2,1)} %get-tuple-element.48), channel_id=1, source_target_pairs={{0,1},{1,0},{4,5},{5,4},{8,9},{9,8},{12,13},{13,12},{16,17},{17,16... | collective-permute-start | bytes 98312 | tf_op jit(solution)/shard_map/ppermute | solution.py:163
  121.8 6.8 %collective-permute-start.27 = (bf16[2,32,256]{2,1,0:T(8,128)(2,1)}, bf16[2,32,256]{2,1,0:T(8,128)(2,1)S(1)}, u32[]{:S(2)}, u32[]{:S(2)}) collective-permute-start(bf16[2,32,256]{2,1,0:T(8,128)(2,1)} %get-tuple-element.46), channel_id=1, source_target_pairs={{0,3},{1,2},{2,1},{3,0},{4,7},{5,6},{6,5},{7,4},{8,11},{9,10},{10,... | collective-permute-start | bytes 98312 | tf_op jit(solution)/shard_map/ppermute | solution.py:163
  131.1 6.5 %collective-permute-start.31 = (bf16[2,32,256]{2,1,0:T(8,128)(2,1)}, bf16[2,32,256]{2,1,0:T(8,128)(2,1)S(1)}, u32[]{:S(2)}, u32[]{:S(2)}) collective-permute-start(bf16[2,32,256]{2,1,0:T(8,128)(2,1)} %shard_map.70.refs_1_), channel_id=1, source_target_pairs={{0,24},{4,28},{8,16},{12,20},{16,8},{20,12},{24,0},{28,4},{1,25},{... | collective-permute-start | bytes 98312 | tf_op jit(solution)/shard_map/ppermute | solution.py:153
  137.0 12.1 %collective-permute-start.34 = (bf16[2,32,256]{2,1,0:T(8,128)(2,1)}, bf16[2,32,256]{2,1,0:T(8,128)(2,1)S(1)}, u32[]{:S(2)}, u32[]{:S(2)}) collective-permute-start(bf16[2,32,256]{2,1,0:T(8,128)(2,1)} %get-tuple-element.52), channel_id=1, source_target_pairs={{2,3},{3,2},{6,7},{7,6},{10,11},{11,10},{14,15},{15,14},{18,19},{1... | collective-permute-start | bytes 98312 | tf_op jit(solution)/shard_map/ppermute | solution.py:163
  143.9 7.2 %collective-permute-start.32 = (bf16[2,32,256]{2,1,0:T(8,128)(2,1)}, bf16[2,32,256]{2,1,0:T(8,128)(2,1)S(1)}, u32[]{:S(2)}, u32[]{:S(2)}) collective-permute-start(bf16[2,32,256]{2,1,0:T(8,128)(2,1)} %get-tuple-element.49), channel_id=1, source_target_pairs={{0,2},{1,3},{2,0},{3,1},{4,6},{5,7},{6,4},{7,5},{8,10},{9,11},{10,... | collective-permute-start | bytes 98312 | tf_op jit(solution)/shard_map/ppermute | solution.py:163
  157.2 8.5 %collective-permute-start.37 = (bf16[2,32,256]{2,1,0:T(8,128)(2,1)}, bf16[2,32,256]{2,1,0:T(8,128)(2,1)S(1)}, u32[]{:S(2)}, u32[]{:S(2)}) collective-permute-start(bf16[2,32,256]{2,1,0:T(8,128)(2,1)} %shard_map.74.refs_1_), channel_id=1, source_target_pairs={{0,24},{4,28},{8,16},{12,20},{16,8},{20,12},{24,0},{28,4},{1,25},{... | collective-permute-start | bytes 98312 | tf_op jit(solution)/shard_map/ppermute | solution.py:153
  158.7 7.1 %collective-permute-start.36 = (bf16[2,32,256]{2,1,0:T(8,128)(2,1)}, bf16[2,32,256]{2,1,0:T(8,128)(2,1)S(1)}, u32[]{:S(2)}, u32[]{:S(2)}) collective-permute-start(bf16[2,32,256]{2,1,0:T(8,128)(2,1)} %shard_map.74.refs_1_), channel_id=1, source_target_pairs={{0,16},{4,20},{8,24},{12,28},{16,0},{20,4},{24,8},{28,12},{1,17},{... | collective-permute-start | bytes 98312 | tf_op jit(solution)/shard_map/ppermute | solution.py:153
  159.2 6.6 %collective-permute-start.35 = (bf16[2,32,256]{2,1,0:T(8,128)(2,1)}, bf16[2,32,256]{2,1,0:T(8,128)(2,1)S(1)}, u32[]{:S(2)}, u32[]{:S(2)}) collective-permute-start(bf16[2,32,256]{2,1,0:T(8,128)(2,1)} %shard_map.74.refs_1_), channel_id=1, source_target_pairs={{0,8},{4,12},{8,0},{12,4},{16,24},{20,28},{24,16},{28,20},{1,9},{5... | collective-permute-start | bytes 98312 | tf_op jit(solution)/shard_map/ppermute | solution.py:153
  163.9 11.9 %collective-permute-start.40 = (bf16[2,32,256]{2,1,0:T(8,128)(2,1)}, bf16[2,32,256]{2,1,0:T(8,128)(2,1)S(1)}, u32[]{:S(2)}, u32[]{:S(2)}) collective-permute-start(bf16[2,32,256]{2,1,0:T(8,128)(2,1)} %get-tuple-element.56), channel_id=1, source_target_pairs={{0,1},{1,0},{4,5},{5,4},{8,9},{9,8},{12,13},{13,12},{16,17},{17,16... | collective-permute-start | bytes 98312 | tf_op jit(solution)/shard_map/ppermute | solution.py:163
  171.3 6.8 %collective-permute-start.39 = (bf16[2,32,256]{2,1,0:T(8,128)(2,1)}, bf16[2,32,256]{2,1,0:T(8,128)(2,1)S(1)}, u32[]{:S(2)}, u32[]{:S(2)}) collective-permute-start(bf16[2,32,256]{2,1,0:T(8,128)(2,1)} %get-tuple-element.54), channel_id=1, source_target_pairs={{0,3},{1,2},{2,1},{3,0},{4,7},{5,6},{6,5},{7,4},{8,11},{9,10},{10,... | collective-permute-start | bytes 98312 | tf_op jit(solution)/shard_map/ppermute | solution.py:163
  185.0 11.6 %collective-permute-start.41 = (bf16[4,32,256]{2,1,0:T(8,128)(2,1)S(1)}, bf16[4,32,256]{2,1,0:T(8,128)(2,1)S(1)}, u32[]{:S(2)}, u32[]{:S(2)}) collective-permute-start(bf16[4,32,256]{2,1,0:T(8,128)(2,1)S(1)} %get-tuple-element.104), channel_id=1, source_target_pairs={{0,4},{4,0},{8,12},{12,8},{16,20},{20,16},{24,28},{28,24},{1,5},{5... | collective-permute-start | bytes 196616 | tf_op jit(solution)/shard_map/ppermute | solution.py:153
  193.3 7.8 %collective-permute-start.50 = (bf16[2,2,32,256]{3,2,1,0:T(8,128)(2,1)S(1)}, bf16[2,2,32,256]{3,2,1,0:T(8,128)(2,1)S(1)}, u32[]{:S(2)}, u32[]{:S(2)}) collective-permute-start(bf16[2,2,32,256]{3,2,1,0:T(8,128)(2,1)S(1)} %pad_maximum_fusion.2.refs_0_), channel_id=1, source_target_pairs={{0,3},{1,2},{2,1},{3,0},{4,7},{5,6},{6,5},{7,4},{8,11},{9,10},{10,... | collective-permute-start | bytes 196616 | tf_op jit(solution)/shard_map/ppermute | solution.py:156
  196.6 19.2 %collective-permute-start.44 = (bf16[4,2,32,256]{3,2,1,0:T(8,128)(2,1)S(1)}, bf16[4,2,32,256]{3,2,1,0:T(8,128)(2,1)S(1)}, u32[]{:S(2)}, u32[]{:S(2)}) collective-permute-start(bf16[4,2,32,256]{3,2,1,0:T(8,128)(2,1)S(1)} %pad_maximum_fusion.1.refs_0_), channel_id=1, source_target_pairs={{0,3},{1,2},{2,1},{3,0},{4,7},{5,6},{6,5},{7,4},{8,11},{9,10},{10,... | collective-permute-start | bytes 393224 | tf_op jit(solution)/shard_map/ppermute | solution.py:156
  197.2 18.6 %collective-permute-start.43 = (bf16[4,2,32,256]{3,2,1,0:T(8,128)(2,1)S(1)}, bf16[4,2,32,256]{3,2,1,0:T(8,128)(2,1)S(1)}, u32[]{:S(2)}, u32[]{:S(2)}) collective-permute-start(bf16[4,2,32,256]{3,2,1,0:T(8,128)(2,1)S(1)} %pad_maximum_fusion.1.refs_0_), channel_id=1, source_target_pairs={{0,2},{1,3},{2,0},{3,1},{4,6},{5,7},{6,4},{7,5},{8,10},{9,11},{10,... | collective-permute-start | bytes 393224 | tf_op jit(solution)/shard_map/ppermute | solution.py:156
  197.2 18.6 %collective-permute-start.42 = (bf16[4,2,32,256]{3,2,1,0:T(8,128)(2,1)S(1)}, bf16[4,2,32,256]{3,2,1,0:T(8,128)(2,1)S(1)}, u32[]{:S(2)}, u32[]{:S(2)}) collective-permute-start(bf16[4,2,32,256]{3,2,1,0:T(8,128)(2,1)S(1)} %pad_maximum_fusion.1.refs_0_), channel_id=1, source_target_pairs={{0,1},{1,0},{2,3},{3,2},{4,5},{5,4},{6,7},{7,6},{8,9},{9,8},{10,11... | collective-permute-start | bytes 393224 | tf_op jit(solution)/shard_map/ppermute | solution.py:156
  201.1 10.7 %collective-permute-start.49 = (bf16[2,2,32,256]{3,2,1,0:T(8,128)(2,1)S(1)}, bf16[2,2,32,256]{3,2,1,0:T(8,128)(2,1)S(1)}, u32[]{:S(2)}, u32[]{:S(2)}) collective-permute-start(bf16[2,2,32,256]{3,2,1,0:T(8,128)(2,1)S(1)} %pad_maximum_fusion.2.refs_0_), channel_id=1, source_target_pairs={{0,2},{1,3},{2,0},{3,1},{4,6},{5,7},{6,4},{7,5},{8,10},{9,11},{10,... | collective-permute-start | bytes 196616 | tf_op jit(solution)/shard_map/ppermute | solution.py:156
  201.1 10.6 %collective-permute-start.48 = (bf16[2,2,32,256]{3,2,1,0:T(8,128)(2,1)S(1)}, bf16[2,2,32,256]{3,2,1,0:T(8,128)(2,1)S(1)}, u32[]{:S(2)}, u32[]{:S(2)}) collective-permute-start(bf16[2,2,32,256]{3,2,1,0:T(8,128)(2,1)S(1)} %pad_maximum_fusion.2.refs_0_), channel_id=1, source_target_pairs={{0,1},{1,0},{2,3},{3,2},{4,5},{5,4},{6,7},{7,6},{8,9},{9,8},{10,11... | collective-permute-start | bytes 196616 | tf_op jit(solution)/shard_map/ppermute | solution.py:156
  (78 other events, 571.2 us)

commit v2 on v0

v2 whole, which is shorter than its diff:
```python
import jax
import jax.numpy as jnp
from jax import lax
from jax.experimental import pallas as pl
from jax.experimental.pallas import tpu as pltpu
from jax.sharding import PartitionSpec as P


LEVELS = 8
LR = 2
BF16 = jnp.bfloat16
F32 = jnp.float32
LIMIT = 4 << 20
VM = pl.BlockSpec(memory_space=pltpu.VMEM)
HBM = pl.BlockSpec(memory_space=pltpu.HBM)
SM = pl.BlockSpec(memory_space=pltpu.SMEM)


def dot_t(left, right):
    return lax.dot_general(left, right, (((1,), (1,)), ((), ())), preferred_element_type=F32)


def role(level):
    return lax.rem(lax.axis_index("pcol") + 2 * LEVELS * LR * lax.axis_size("pcol") - level * LR, lax.axis_size("pcol"))


def call(body, outs, ins, specs=None, aliases=None, scratch=(), limit=LIMIT):
    specs = specs or [VM] * len(ins)
    ins = [pltpu.with_memory_space_constraint(x, spec.memory_space) for x, spec in zip(ins, specs)]
    return pl.pallas_call(
        body,
        out_shape=[pltpu.VMEM(shape, kind) for shape, kind in outs],
        in_specs=specs,
        out_specs=[VM] * len(outs),
        input_output_aliases=aliases or {},
        scratch_shapes=scratch,
        compiler_params=pltpu.CompilerParams(vmem_limit_bytes=limit),
    )(*ins)


def row_sum(table, store, own, other, level, row, pair):
    slots = own.shape[1] - 1
    total = None
    for j in range(slots):
        at = table[level * LR + row, pair * slots + j]
        part = dot_t(store[at], (other if pair else own)[row, j])
        total = part if total is None else total + part
    return total


def update(level, table, store, pieces, own, other):
    newest = level - 1
    last = level == LEVELS - 1
    base = newest * LR // lax.axis_size("pcol") * 2 * len(pieces)

    def body(table_ref, store_ref, own_ref, other_ref, *refs):
        pieces_refs, out, sums = refs[:len(pieces)], refs[len(pieces)], refs[len(pieces) + 1:]
        place = role(newest)

        @pl.when(place < LR)
        def _():
            for j, piece in enumerate(pieces_refs):
                out[pl.ds(base + 2 * j, 2)] = piece[...]
            if not last:
                add_rows(level, place, table_ref, out, own_ref, other_ref, sums)

        if last:
            add_rows(level, place, table_ref, out, own_ref, other_ref, sums)
        else:
            @pl.when(place >= LR)
            def _():
                for to in sums:
                    to[...] = pieces_refs[0][...]

    shape = (2,) + store.shape[1:]
    sums = [((LR,) + shape, BF16)] if last else [(shape, BF16), (shape, BF16)]
    return call(body, [(store.shape, BF16), *sums], [table, store, own, other, *pieces],
                specs=[SM] + [VM] * (3 + len(pieces)), aliases={1: 0})


def add_rows(level, place, table, store, own, other, sums):
    for turn in range(LR):
        row = turn if len(sums) == 1 else lax.rem(place + turn, LR)
        for pair in range(2):
            total = row_sum(table, store, own, other, level, row, pair)
            if len(sums) == 1:
                sums[0][turn, pair] = total.astype(BF16)
            else:
                sums[turn][pair] = total.astype(sums[turn].dtype)


def early(level, newest, table, store, own, other, kind, solved):
    def body(table_ref, store_ref, own_ref, other_ref, solved_ref, *sums):
        place = role(newest)

        @pl.when(place < LR)
        def _():
            add_rows(level, place, table_ref, store_ref, own_ref, other_ref, sums)

        @pl.when(place >= LR)
        def _():
            sums[1][...] = solved_ref[...]

    shape = (2,) + store.shape[1:]
    return call(body, [(shape, kind), (shape, BF16)], [table, store, own, other, solved], specs=[SM, VM, VM, VM, VM])


def solve(level, rhs_own, rhs_other, own, other, before, terms):
    def body(ro, rp, io, ip, old, *refs):
        *terms_refs, out = refs
        place = role(level)

        @pl.when(place < LR)
        def _():
            for pair in range(2):
                r_ref, i_ref = (rp, ip) if pair else (ro, io)
                rest = r_ref[level * LR + place].astype(F32)
                for term in terms_refs:
                    rest = rest - term[pair].astype(F32)
                out[pair] = dot_t(rest.astype(BF16), i_ref[place, i_ref.shape[1] - 1]).astype(BF16)

        @pl.when(place >= LR)
        def _():
            out[...] = old[...]

    return call(body, [(before.shape, BF16)], [rhs_own, rhs_other, own, other, before, *terms])[0]


def solve_first(rhs, inverses, half):
    def body(r, i, keep, send, side, tile, sems):
        place = role(0)
        core = lax.rem(lax.axis_index("prow"), 2)
        at = lax.rem(place, LR)
        copies = [pltpu.make_async_copy(r.at[at], side, sems.at[0]), pltpu.make_async_copy(i.at[at], tile, sems.at[1])]
        for copy in copies:
            copy.start()
        for copy in copies:
            copy.wait()
        for out, part in ((keep, core), (send, 1 - core)):
            out[...] = dot_t(side[pl.ds(pl.multiple_of(part * half, half), half)], tile[...]).astype(BF16)

    size = rhs.shape[2]
    shape = ((half, size), BF16)
    return call(body, [shape, shape], [rhs, inverses], specs=[HBM] * 2,
                scratch=[pltpu.VMEM(rhs.shape[1:], BF16), pltpu.VMEM((size, size), BF16), pltpu.SemaphoreType.DMA((2,))])


def join(a, b):
    def body(x, y, out):
        out[0] = x[...]
        out[1] = y[...]

    return call(body, [((2,) + a.shape, BF16)], [a, b])[0]


def stage(level, inverses, blocks, after=()):
    slots = blocks.shape[1]
    rows = pl.ds(level * LR, LR)

    def body(i, b, *refs):
        out, sems = refs[-2:]
        copies = [pltpu.make_async_copy(b.at[rows], out.at[:, pl.ds(0, slots)], sems.at[0]),
                  pltpu.make_async_copy(i.at[rows], out.at[:, slots], sems.at[1])]
        for copy in copies:
            copy.start()
        for copy in copies:
            copy.wait()

    return call(body, [((LR, slots + 1) + blocks.shape[2:], BF16)], [inverses, blocks, *after],
                specs=[HBM] * 2 + [VM] * len(after), scratch=[pltpu.SemaphoreType.DMA((2,))])[0]


def halves(rhs, half):
    def body(r, mine, give, sems):
        core = lax.rem(lax.axis_index("prow"), 2)
        copies = []
        for k, (out, part) in enumerate(((mine, core), (give, 1 - core))):
            copies.append(pltpu.make_async_copy(r.at[:, pl.ds(pl.multiple_of(part * half, half), half)], out, sems.at[k]))
        for copy in copies:
            copy.start()
        for copy in copies:
            copy.wait()

    shape = ((rhs.shape[0], half, rhs.shape[2]), BF16)
    return call(body, [shape, shape], [rhs], specs=[HBM], scratch=[pltpu.SemaphoreType.DMA((2,))])


def zeros(shape):
    def body(out):
        out[...] = jnp.zeros(shape, BF16)

    return call(body, [(shape, BF16)], [])[0]


def to_scalars(table):
    def body(x, out):
        for i in range(table.shape[0]):
            for j in range(table.shape[1]):
                out[i, j] = x[i, j]

    return pl.pallas_call(body, out_shape=pltpu.SMEM(table.shape, jnp.int32), in_specs=[SM], out_specs=SM)(table)


def place_rows(found, col, write):
    for level, ref, away in found:
        source = jnp.bitwise_xor(col, away)
        count = lax.axis_size("pcol")
        place = lax.rem(source + 2 * LEVELS * LR * count - level * LR, count)

        @pl.when(place < LR)
        def _():
            write(level * LR + place, ref)


def pack(found, levels, half, size):
    first = levels[0] * LR

    def body(*refs):
        *sources, out = refs

        def write(row, ref):
            out[row - first] = ref[1]

        place_rows([(level, ref, away) for (level, _, away), ref in zip(found, sources)], lax.axis_index("pcol"), write)

    return call(body, [((len(levels) * LR, half, size), BF16)], [x for _, x, _ in found])[0]


def solve_last(rhs_own, rhs_other, own_tiles, other_tiles, parts, found, first):
    count = len(parts)
    half, size = rhs_own.shape[1:]

    def body(ro, rp, io, ip, *refs):
        parts_refs, sources, (own, send, held) = refs[:count], refs[count:-3], refs[-3:]
        col = lax.axis_index("pcol")
        for k in range(count):
            held[jnp.bitwise_xor(col, k)] = parts_refs[k][...]
        for pair in range(2):
            r_ref, i_ref = (rp, ip) if pair else (ro, io)
            for row in range(LR):
                rest = r_ref[(LEVELS - 1) * LR + row].astype(F32)
                for k in range(count):
                    rest = rest - held[k, row, pair].astype(F32)
                done = dot_t(rest.astype(BF16), i_ref[row, i_ref.shape[1] - 1]).astype(BF16)
                if pair:
                    send[(LEVELS - 1 - first) * LR + row] = done
                else:
                    own[row] = done

        def write(row, ref):
            send[row - first * LR] = ref[1]

        place_rows([(level, ref, away) for (level, _, away), ref in zip(found, sources)], col, write)

    outs = [((LR, half, size), BF16), (((LEVELS - first) * LR, half, size), BF16)]
    return call(body, outs, [rhs_own, rhs_other, own_tiles, other_tiles, *parts, *[x for _, x, _ in found]],
                scratch=[pltpu.VMEM((count,) + parts[0].shape, BF16)])


def assemble(found, swapped, own, shape):
    half = shape[1] // 2

    def body(*refs):
        sources, swaps, own_ref, out = refs[:len(found)], refs[len(found):-2], refs[-2], refs[-1]
        col = lax.axis_index("pcol")
        core = lax.rem(lax.axis_index("prow"), 2)
        mine_at = pl.ds(pl.multiple_of(core * half, half), half)
        theirs_at = pl.ds(pl.multiple_of((1 - core) * half, half), half)

        def write(row, ref):
            out[row, mine_at] = ref[0]

        place_rows([(level, ref, away) for (level, _, away), ref in zip(found, sources)], col, write)
        row = 0
        for ref in swaps:
            for i in range(ref.shape[0]):
                out[row, theirs_at] = ref[i]
                row += 1
        for i in range(LR):
            out[(LEVELS - 1) * LR + i, mine_at] = own_ref[i]

    return call(body, [(shape, BF16)], [*[x for _, x, _ in found], *swapped, own])[0]


def body(rhs, blocks, inverses, columns, counts):
    rows, sides, size = rhs.shape
    slots = columns.shape[1]
    half = sides // 2
    prow_count = lax.axis_size("prow")
    pcol_count = lax.axis_size("pcol")
    groups = pcol_count // LR
    paired = groups == 2
    me = lax.axis_index("prow")

    def prow_swap(x, k):
        return lax.ppermute(x, "prow", [(i, i ^ k) for i in range(prow_count)])

    def pcol_swap(x, k):
        return lax.ppermute(x, "pcol", [(i, i ^ k) for i in range(pcol_count)])

    def between(x, first, second, turn):
        pairs = []
        for a in range(LR):
            s, d = (first * LR + a) % pcol_count, (second * LR + (a + turn) % LR) % pcol_count
            pairs += [(s, d), (d, s)]
        return lax.ppermute(x, "pcol", sorted(set(pairs)))

    def share(x):
        return [x] + [pcol_swap(x, k) for k in range(1, pcol_count)]

    keep, send = solve_first(rhs, inverses, half)
    solved = [join(keep, prow_swap(send, 1))]
    held = {1: stage(1, inverses, blocks)}
    other = {1: prow_swap(held[1], 1)}
    live = jnp.arange(slots, dtype=jnp.int32)[None, :] < counts
    coded = jnp.where(live, columns, -1)
    coded = jnp.concatenate([coded, prow_swap(coded, 1)], axis=1)
    zero_row = rows // pcol_count * prow_count
    at = coded // prow_count // pcol_count * prow_count + ((coded % prow_count) ^ me)
    table = to_scalars(jnp.where(coded < 0, zero_row, at))
    mine, give = halves(rhs, half)
    theirs = prow_swap(give, 1)

    store = zeros((zero_row + 1, half, size))
    waiting = {level: [] for level in range(LEVELS)}
    found = []
    for level in range(1, LEVELS):
        newest = level - 1
        last = level == LEVELS - 1
        y = solved[newest]
        pieces = [y] + [prow_swap(y, k) for k in range(2, prow_count, 2)]
        if last:
            late = [newest - g for g in range(groups)] if paired else list(range(newest, -1, -1))
            rest = [(late[:groups], y)] if paired else [([i], solved[i]) for i in late]
            spread = [(y, share(y))] if paired else [(solved[i], share(solved[i])) for i in late]
            for (levels, _), (_, copies) in zip(rest, spread):
                found += [(i, copy, k) for i in levels for k, copy in enumerate(copies)]
        store, *sums = update(level, table, store, pieces, held[level], other[level])
        if last:
            parts = share(sums[0])
            break
        terms = [between(sums[0], newest, level, 0)]
        terms.append(between(sums[1], newest, level, 1))
        reach = level + groups
        for later in [reach] if level > 1 else range(2, reach + 1):
            if later < LEVELS:
                held[later] = stage(later, inverses, blocks, sums)
                other[later] = prow_swap(held[later], 1)
        traded = None
        for ahead in range(1, groups):
            later = level + ahead
            if later >= LEVELS - 1:
                continue
            own_pair = ahead == groups - 1
            a, b = early(later, newest, table, store, held[later], other[later], F32 if own_pair else BF16, y)
            if paired:
                traded = pcol_swap(b, 1)
                waiting[later] += [a, traded]
            elif own_pair:
                waiting[later] += [a, between(b, newest, newest, 1)]
            else:
                waiting[later] += [between(a, newest, later, 0), between(b, newest, later, 1)]
        if paired and level > 1:
            if traded is None:
                traded = pcol_swap(y, 1)
            found += [(level - 2, y, 0), (level - 2, traded, 1)]
            found += [(level - 2, terms[0], 2), (level - 2, terms[1], 3)]
        solved.append(solve(level, mine, theirs, held[level], other[level], y, terms + waiting[level]))

    first = min(late)
    swapped = [prow_swap(pack([f for f in found if f[0] < first], list(range(first)), half, size), 1)] if first else []
    own, send = solve_last(mine, theirs, held[LEVELS - 1], other[LEVELS - 1], parts,
                           [f for f in found if f[0] >= first], first)
    return assemble(found, swapped + [prow_swap(send, 1)], own, rhs.shape)


def solution(mesh):
    placed = (
        P("prow", None, None),
        P("prow", "pcol", None, None),
        P("prow", None, None),
        P("prow", "pcol"),
        P("prow", "pcol"),
    )
    return jax.shard_map(
        body, mesh=mesh, in_specs=placed, out_specs=P("prow", None, None), check_vma=False
    )
```

time: 399 us -> 128 us (0.32)
  waiting for transfers between devices: 272 us -> 43.5 us
  blocking collectives: 74 us -> 0 us
  starting transfers between devices: 0.33 us -> 63.9 us
  matrix products: 28.7 us -> 0 us
  Pallas kernels: 0 us -> 18.2 us
  between operations: 13.4 us -> 0.32 us
  local copies, waits for them, and re-layouts: 7.25 us -> 0.89 us
    psum x8 -> x0, waiting for transfers between devices: 272 us -> none  [advance(): summed = lax.psum(update_sum, 'pcol')]
    all_gather x8 -> x0, blocking collectives: 74 us -> none  [advance(): level_block = lax.all_gather(payload[None], 'prow', axis=0, tiled=True)]
    ppermute x0 -> x57, starting transfers between devices: none -> 63.9 us  [the longest x33 27.6 us: prow_swap(): return lax.ppermute(x, 'prow', [(i, i ^ k) for i in range(prow_count)])]
    ppermute x0 -> x57, waiting for transfers between devices: none -> 43.5 us  [the longest x12 22 us: between(): return lax.ppermute(x, 'pcol', sorted(set(pairs)))]
    dot_general x16 -> x0, matrix products: 28.7 us -> none  [the longest x8 18.7 us: advance(): jnp.einsum('scrj,scij->sri', gathered, panels, preferred_element_type=jnp...]
    pallas_call x0 -> x33, Pallas kernels: none -> 18.2 us  [the longest x32 17.3 us: call(): pl.pallas_call(body, out_shape=[pltpu.VMEM(shape, kind) for shape, kind i...]
    gather x8 -> x0, local copies, waits for them, and re-layouts: 4.5 us -> none  [advance(): jnp.take(solved_store, store_ids, axis=0) * active[:, :, None, None]]
  transfers between devices with their start and end apart: 8 -> 57, of which waited for: 8 -> 29; matrix products, arithmetic and copies ran while one was open for 0% -> 1% of each run, Pallas kernels for 0% -> 12%
where the time goes in v2:
time: 128 us
  starting transfers between devices  63.9 us (50%)
  waiting for transfers between devices  43.5 us (34%)
  Pallas kernels  18.2 us (14%)
    ppermute x33, starting transfers between devices, prow_swap(): return lax.ppermute(x, 'prow', [(i, i ^ k) for i in range(prow_count)])  27.6 us
    ppermute x12, starting transfers between devices, between(): return lax.ppermute(x, 'pcol', sorted(set(pairs)))  24.8 us
    ppermute x12, waiting for transfers between devices, between(): return lax.ppermute(x, 'pcol', sorted(set(pairs)))  22 us
    ppermute x33, waiting for transfers between devices, prow_swap(): return lax.ppermute(x, 'prow', [(i, i ^ k) for i in range(prow_count)])  18.7 us
    pallas_call x32, Pallas kernels, call(): pl.pallas_call(body, out_shape=[pltpu.VMEM(shape, kind) for shape, kind i...  17.3 us
    ppermute x12, starting transfers between devices, pcol_swap(): return lax.ppermute(x, 'pcol', [(i, i ^ k) for i in range(pcol_count)])  11.6 us
    ppermute x12, waiting for transfers between devices, pcol_swap(): return lax.ppermute(x, 'pcol', [(i, i ^ k) for i in range(pcol_count)])  2.89 us
  transfers between devices with their start and end apart: 57, of which 29 were waited for; matrix products, arithmetic and copies ran while one was open for 1% of the time, Pallas kernels for 12%

profile of v2, /device:TPU:0, one launch (start us, length us, event | category | flops | bytes accessed | tf_op | source)
XLA Modules:
  0.0 127.7 jit_solution(10552108249244509400)
XLA Ops:
  4.6 2.8 %collective-permute-start.4 = (bf16[2,32,256]{2,1,0:T(8,128)(2,1)S(1)}, bf16[2,32,256]{2,1,0:T(8,128)(2,1)S(1)}, u32[]{:S(2)}, u32[]{:S(2)}) collective-permute-start(bf16[2,32,256]{2,1,0:T(8,128)(2,1)S(1)} %shard_map.58.refs_0_.old.solved_ref), channel_id=1, source_target_pairs={{0,8},{4,12},{8,0},{12,4},{16,24},{20,28},{24,16},{28,20},{1,9},{5... | collective-permute-start | bytes 98312 | tf_op jit(solution)/shard_map/ppermute | solution.py:296
  7.4 1.5 %collective-permute-start.5 = (bf16[2,32,256]{2,1,0:T(8,128)(2,1)S(1)}, bf16[2,32,256]{2,1,0:T(8,128)(2,1)S(1)}, u32[]{:S(2)}, u32[]{:S(2)}) collective-permute-start(bf16[2,32,256]{2,1,0:T(8,128)(2,1)S(1)} %shard_map.58.refs_0_.old.solved_ref), channel_id=1, source_target_pairs={{0,16},{4,20},{8,24},{12,28},{16,0},{20,4},{24,8},{28,12},{1,17},{... | collective-permute-start | bytes 98312 | tf_op jit(solution)/shard_map/ppermute | solution.py:296
  11.3 2.4 %collective-permute-done.6.refs_3_ = bf16[2,32,256]{2,1,0:T(8,128)(2,1)S(1)} collective-permute-done((bf16[2,32,256]{2,1,0:T(8,128)(2,1)S(1)}, bf16[2,32,256]{2,1,0:T(8,128)(2,1)S(1)}, u32[]{:S(2)}, u32[]{:S(2)}) %collective-permute-start.6) | collective-permute-done | bytes 32800 | tf_op jit(solution)/shard_map/ppermute | solution.py:296
  18.8 1.9 %collective-permute-start.7 = (bf16[2,32,256]{2,1,0:T(8,128)(2,1)S(1)}, bf16[2,32,256]{2,1,0:T(8,128)(2,1)S(1)}, u32[]{:S(2)}, u32[]{:S(2)}) collective-permute-start(bf16[2,32,256]{2,1,0:T(8,128)(2,1)S(1)} %get-tuple-element.44.refs_0_), channel_id=1, source_target_pairs={{0,2},{1,3},{2,0},{3,1},{4,6},{5,7},{6,4},{7,5},{8,10},{9,11},{10,... | collective-permute-start | bytes 98312 | tf_op jit(solution)/shard_map/ppermute | solution.py:306
  20.8 2.1 %collective-permute-start.8 = (bf16[2,32,256]{2,1,0:T(8,128)(2,1)S(1)}, bf16[2,32,256]{2,1,0:T(8,128)(2,1)S(1)}, u32[]{:S(2)}, u32[]{:S(2)}) collective-permute-start(bf16[2,32,256]{2,1,0:T(8,128)(2,1)S(1)} %get-tuple-element.45.refs_1_), channel_id=1, source_target_pairs={{0,3},{1,2},{2,1},{3,0},{4,7},{5,6},{6,5},{7,4},{8,11},{9,10},{10,... | collective-permute-start | bytes 98312 | tf_op jit(solution)/shard_map/ppermute | solution.py:306
  23.7 2.8 %collective-permute-done.8.refs_1_ = bf16[2,32,256]{2,1,0:T(8,128)(2,1)S(1)} collective-permute-done((bf16[2,32,256]{2,1,0:T(8,128)(2,1)S(1)}, bf16[2,32,256]{2,1,0:T(8,128)(2,1)S(1)}, u32[]{:S(2)}, u32[]{:S(2)}) %collective-permute-start.8) | collective-permute-done | bytes 32800 | tf_op jit(solution)/shard_map/ppermute | solution.py:306
  27.5 2.4 %collective-permute-start.12 = (bf16[2,32,256]{2,1,0:T(8,128)(2,1)S(1)}, bf16[2,32,256]{2,1,0:T(8,128)(2,1)S(1)}, u32[]{:S(2)}, u32[]{:S(2)}) collective-permute-start(bf16[2,32,256]{2,1,0:T(8,128)(2,1)S(1)} %shard_map.62.refs_0_.solved_ref.old), channel_id=1, source_target_pairs={{0,24},{4,28},{8,16},{12,20},{16,8},{20,12},{24,0},{28,4},{1,25},{... | collective-permute-start | bytes 98312 | tf_op jit(solution)/shard_map/ppermute | solution.py:296
  33.7 1.7 %collective-permute-start.15 = (bf16[2,32,256]{2,1,0:T(8,128)(2,1)S(1)}, bf16[2,32,256]{2,1,0:T(8,128)(2,1)S(1)}, u32[]{:S(2)}, u32[]{:S(2)}) collective-permute-start(bf16[2,32,256]{2,1,0:T(8,128)(2,1)S(1)} %get-tuple-element.49.refs_0_), channel_id=1, source_target_pairs={{0,2},{1,3},{2,0},{3,1},{4,6},{5,7},{6,4},{7,5},{8,10},{9,11},{10,... | collective-permute-start | bytes 98312 | tf_op jit(solution)/shard_map/ppermute | solution.py:306
  37.3 1.8 %collective-permute-done.15.refs_0_.refs_2_ = bf16[2,32,256]{2,1,0:T(8,128)(2,1)S(1)} collective-permute-done((bf16[2,32,256]{2,1,0:T(8,128)(2,1)S(1)}, bf16[2,32,256]{2,1,0:T(8,128)(2,1)S(1)}, u32[]{:S(2)}, u32[]{:S(2)}) %collective-permute-start.15) | collective-permute-done | bytes 32800 | tf_op jit(solution)/shard_map/ppermute | solution.py:306
  39.1 2.3 %collective-permute-done.16.refs_1_.refs_3_ = bf16[2,32,256]{2,1,0:T(8,128)(2,1)S(1)} collective-permute-done((bf16[2,32,256]{2,1,0:T(8,128)(2,1)S(1)}, bf16[2,32,256]{2,1,0:T(8,128)(2,1)S(1)}, u32[]{:S(2)}, u32[]{:S(2)}) %collective-permute-start.16) | collective-permute-done | bytes 32800 | tf_op jit(solution)/shard_map/ppermute | solution.py:306
  41.6 1.5 %collective-permute-start.18 = (bf16[2,32,256]{2,1,0:T(8,128)(2,1)S(1)}, bf16[2,32,256]{2,1,0:T(8,128)(2,1)S(1)}, u32[]{:S(2)}, u32[]{:S(2)}) collective-permute-start(bf16[2,32,256]{2,1,0:T(8,128)(2,1)S(1)} %shard_map.68.refs_0_.solved_ref.old.refs_4_), channel_id=1, source_target_pairs={{0,8},{4,12},{8,0},{12,4},{16,24},{20,28},{24,16},{28,20},{1,9},{5... | collective-permute-start | bytes 98312 | tf_op jit(solution)/shard_map/ppermute | solution.py:296
  43.1 1.5 %collective-permute-start.19 = (bf16[2,32,256]{2,1,0:T(8,128)(2,1)S(1)}, bf16[2,32,256]{2,1,0:T(8,128)(2,1)S(1)}, u32[]{:S(2)}, u32[]{:S(2)}) collective-permute-start(bf16[2,32,256]{2,1,0:T(8,128)(2,1)S(1)} %shard_map.68.refs_0_.solved_ref.old.refs_4_), channel_id=1, source_target_pairs={{0,16},{4,20},{8,24},{12,28},{16,0},{20,4},{24,8},{28,12},{1,17},{... | collective-permute-start | bytes 98312 | tf_op jit(solution)/shard_map/ppermute | solution.py:296
  47.2 2.3 %collective-permute-done.20.refs_3_ = bf16[2,32,256]{2,1,0:T(8,128)(2,1)S(1)} collective-permute-done((bf16[2,32,256]{2,1,0:T(8,128)(2,1)S(1)}, bf16[2,32,256]{2,1,0:T(8,128)(2,1)S(1)}, u32[]{:S(2)}, u32[]{:S(2)}) %collective-permute-start.20) | collective-permute-done | bytes 32800 | tf_op jit(solution)/shard_map/ppermute | solution.py:296
  53.0 3.0 %collective-permute-start.24 = (bf16[2,32,256]{2,1,0:T(8,128)(2,1)S(1)}, bf16[2,32,256]{2,1,0:T(8,128)(2,1)S(1)}, u32[]{:S(2)}, u32[]{:S(2)}) collective-permute-start(bf16[2,32,256]{2,1,0:T(8,128)(2,1)S(1)} %get-tuple-element.56.refs_1_), channel_id=1, source_target_pairs={{0,3},{1,2},{2,1},{3,0},{4,7},{5,6},{6,5},{7,4},{8,11},{9,10},{10,... | collective-permute-start | bytes 98312 | tf_op jit(solution)/shard_map/ppermute | solution.py:306
  56.6 2.1 %collective-permute-done.24.refs_1_.refs_7_ = bf16[2,32,256]{2,1,0:T(8,128)(2,1)S(1)} collective-permute-done((bf16[2,32,256]{2,1,0:T(8,128)(2,1)S(1)}, bf16[2,32,256]{2,1,0:T(8,128)(2,1)S(1)}, u32[]{:S(2)}, u32[]{:S(2)}) %collective-permute-start.24) | collective-permute-done | bytes 32800 | tf_op jit(solution)/shard_map/ppermute | solution.py:306
  59.8 2.4 %collective-permute-start.27 = (bf16[2,32,256]{2,1,0:T(8,128)(2,1)S(1)}, bf16[2,32,256]{2,1,0:T(8,128)(2,1)S(1)}, u32[]{:S(2)}, u32[]{:S(2)}) collective-permute-start(bf16[2,32,256]{2,1,0:T(8,128)(2,1)S(1)} %shard_map.72.refs_0_.solved_ref.old.refs_8_), channel_id=1, source_target_pairs={{0,24},{4,28},{8,16},{12,20},{16,8},{20,12},{24,0},{28,4},{1,25},{... | collective-permute-start | bytes 98312 | tf_op jit(solution)/shard_map/ppermute | solution.py:296
  66.0 4.4 %collective-permute-start.30 = (bf16[2,32,256]{2,1,0:T(8,128)(2,1)S(1)}, bf16[2,32,256]{2,1,0:T(8,128)(2,1)S(1)}, u32[]{:S(2)}, u32[]{:S(2)}) collective-permute-start(bf16[2,32,256]{2,1,0:T(8,128)(2,1)S(1)} %get-tuple-element.60.refs_0_), channel_id=1, source_target_pairs={{0,2},{1,3},{2,0},{3,1},{4,6},{5,7},{6,4},{7,5},{8,10},{9,11},{10,... | collective-permute-start | bytes 98312 | tf_op jit(solution)/shard_map/ppermute | solution.py:306
  70.5 2.6 %collective-permute-done.30.refs_0_.refs_10_ = bf16[2,32,256]{2,1,0:T(8,128)(2,1)S(1)} collective-permute-done((bf16[2,32,256]{2,1,0:T(8,128)(2,1)S(1)}, bf16[2,32,256]{2,1,0:T(8,128)(2,1)S(1)}, u32[]{:S(2)}, u32[]{:S(2)}) %collective-permute-start.30) | collective-permute-done | bytes 32800 | tf_op jit(solution)/shard_map/ppermute | solution.py:306
  73.1 3.1 %collective-permute-done.31.refs_1_.refs_11_ = bf16[2,32,256]{2,1,0:T(8,128)(2,1)S(1)} collective-permute-done((bf16[2,32,256]{2,1,0:T(8,128)(2,1)S(1)}, bf16[2,32,256]{2,1,0:T(8,128)(2,1)S(1)}, u32[]{:S(2)}, u32[]{:S(2)}) %collective-permute-start.31) | collective-permute-done | bytes 32800 | tf_op jit(solution)/shard_map/ppermute | solution.py:306
  77.9 1.5 %collective-permute-start.33 = (bf16[2,32,256]{2,1,0:T(8,128)(2,1)S(1)}, bf16[2,32,256]{2,1,0:T(8,128)(2,1)S(1)}, u32[]{:S(2)}, u32[]{:S(2)}) collective-permute-start(bf16[2,32,256]{2,1,0:T(8,128)(2,1)S(1)} %shard_map.76.refs_0_.solved_ref.old.refs_12_), channel_id=1, source_target_pairs={{0,16},{4,20},{8,24},{12,28},{16,0},{20,4},{24,8},{28,12},{1,17},{... | collective-permute-start | bytes 98312 | tf_op jit(solution)/shard_map/ppermute | solution.py:296
  82.0 2.3 %collective-permute-done.34.refs_3_ = bf16[2,32,256]{2,1,0:T(8,128)(2,1)S(1)} collective-permute-done((bf16[2,32,256]{2,1,0:T(8,128)(2,1)S(1)}, bf16[2,32,256]{2,1,0:T(8,128)(2,1)S(1)}, u32[]{:S(2)}, u32[]{:S(2)}) %collective-permute-start.34) | collective-permute-done | bytes 32800 | tf_op jit(solution)/shard_map/ppermute | solution.py:296
  86.5 4.3 %collective-permute-start.38 = (bf16[2,32,256]{2,1,0:T(8,128)(2,1)S(1)}, bf16[2,32,256]{2,1,0:T(8,128)(2,1)S(1)}, u32[]{:S(2)}, u32[]{:S(2)}) collective-permute-start(bf16[2,32,256]{2,1,0:T(8,128)(2,1)S(1)} %get-tuple-element.66.refs_1_), channel_id=1, source_target_pairs={{0,3},{1,2},{2,1},{3,0},{4,7},{5,6},{6,5},{7,4},{8,11},{9,10},{10,... | collective-permute-start | bytes 98312 | tf_op jit(solution)/shard_map/ppermute | solution.py:306
  91.4 1.6 %collective-permute-done.38.refs_1_.refs_15_ = bf16[2,32,256]{2,1,0:T(8,128)(2,1)S(1)} collective-permute-done((bf16[2,32,256]{2,1,0:T(8,128)(2,1)S(1)}, bf16[2,32,256]{2,1,0:T(8,128)(2,1)S(1)}, u32[]{:S(2)}, u32[]{:S(2)}) %collective-permute-start.38) | collective-permute-done | bytes 32800 | tf_op jit(solution)/shard_map/ppermute | solution.py:306
  94.1 2.4 %collective-permute-start.42 = (bf16[2,32,256]{2,1,0:T(8,128)(2,1)S(1)}, bf16[2,32,256]{2,1,0:T(8,128)(2,1)S(1)}, u32[]{:S(2)}, u32[]{:S(2)}) collective-permute-start(bf16[2,32,256]{2,1,0:T(8,128)(2,1)S(1)} %shard_map.80.refs_0_.old.refs_16_), channel_id=1, source_target_pairs={{0,24},{4,28},{8,16},{12,20},{16,8},{20,12},{24,0},{28,4},{1,25},{... | collective-permute-start | bytes 98312 | tf_op jit(solution)/shard_map/ppermute | solution.py:296
  98.9 2.6 %collective-permute-start.43 = (bf16[2,32,256]{2,1,0:T(8,128)(2,1)S(1)}, bf16[2,32,256]{2,1,0:T(8,128)(2,1)S(1)}, u32[]{:S(2)}, u32[]{:S(2)}) collective-permute-start(bf16[2,32,256]{2,1,0:T(8,128)(2,1)S(1)} %get-tuple-element.68), channel_id=1, source_target_pairs={{0,2},{1,3},{2,0},{3,1},{4,6},{5,7},{6,4},{7,5},{8,10},{9,11},{10,... | collective-permute-start | bytes 98312 | tf_op jit(solution)/shard_map/ppermute | solution.py:306
  101.5 1.8 %collective-permute-start.44 = (bf16[2,32,256]{2,1,0:T(8,128)(2,1)S(1)}, bf16[2,32,256]{2,1,0:T(8,128)(2,1)S(1)}, u32[]{:S(2)}, u32[]{:S(2)}) collective-permute-start(bf16[2,32,256]{2,1,0:T(8,128)(2,1)S(1)} %get-tuple-element.69), channel_id=1, source_target_pairs={{0,3},{1,2},{2,1},{3,0},{4,7},{5,6},{6,5},{7,4},{8,11},{9,10},{10,... | collective-permute-start | bytes 98312 | tf_op jit(solution)/shard_map/ppermute | solution.py:306
  103.9 3.5 %collective-permute-done.44.refs_1_.refs_19_ = bf16[2,32,256]{2,1,0:T(8,128)(2,1)S(1)} collective-permute-done((bf16[2,32,256]{2,1,0:T(8,128)(2,1)S(1)}, bf16[2,32,256]{2,1,0:T(8,128)(2,1)S(1)}, u32[]{:S(2)}, u32[]{:S(2)}) %collective-permute-start.44) | collective-permute-done | bytes 32800 | tf_op jit(solution)/shard_map/ppermute | solution.py:306
  109.0 2.1 %collective-permute-start.52 = (bf16[2,32,256]{2,1,0:T(8,128)(2,1)S(1)}, bf16[2,32,256]{2,1,0:T(8,128)(2,1)S(1)}, u32[]{:S(2)}, u32[]{:S(2)}) collective-permute-start(bf16[2,32,256]{2,1,0:T(8,128)(2,1)S(1)} %shard_map.82.refs_0_.refs_4_.refs_8_.refs_20_.refs_24_), channel_id=1, source_target_pairs={{0,24},{4,28},{8,16},{12,20},{16,8},{20,12},{24,0},{28,4},{1,25},{... | collective-permute-start | bytes 98312 | tf_op jit(solution)/shard_map/ppermute | solution.py:296
  114.5 2.0 %collective-permute-start.53 = (bf16[2,2,32,256]{3,2,1,0:T(8,128)(2,1)S(1)}, bf16[2,2,32,256]{3,2,1,0:T(8,128)(2,1)S(1)}, u32[]{:S(2)}, u32[]{:S(2)}) collective-permute-start(bf16[2,2,32,256]{3,2,1,0:T(8,128)(2,1)S(1)} %get-tuple-element.72.refs_0_), channel_id=1, source_target_pairs={{0,1},{1,0},{2,3},{3,2},{4,5},{5,4},{6,7},{7,6},{8,9},{9,8},{10,11... | collective-permute-start | bytes 196616 | tf_op jit(solution)/shard_map/ppermute | solution.py:299
  116.5 1.7 %collective-permute-start.54 = (bf16[2,2,32,256]{3,2,1,0:T(8,128)(2,1)S(1)}, bf16[2,2,32,256]{3,2,1,0:T(8,128)(2,1)S(1)}, u32[]{:S(2)}, u32[]{:S(2)}) collective-permute-start(bf16[2,2,32,256]{3,2,1,0:T(8,128)(2,1)S(1)} %get-tuple-element.72.refs_0_), channel_id=1, source_target_pairs={{0,2},{1,3},{2,0},{3,1},{4,6},{5,7},{6,4},{7,5},{8,10},{9,11},{10,... | collective-permute-start | bytes 196616 | tf_op jit(solution)/shard_map/ppermute | solution.py:299
  119.0 3.1 %collective-permute-start.47 = (bf16[2,32,256]{2,1,0:T(8,128)(2,1)S(1)}, bf16[2,32,256]{2,1,0:T(8,128)(2,1)S(1)}, u32[]{:S(2)}, u32[]{:S(2)}) collective-permute-start(bf16[2,32,256]{2,1,0:T(8,128)(2,1)S(1)} %shard_map.82.refs_0_.refs_4_.refs_8_.refs_20_.refs_24_), channel_id=1, source_target_pairs={{0,3},{1,2},{2,1},{3,0},{4,7},{5,6},{6,5},{7,4},{8,11},{9,10},{10,... | collective-permute-start | bytes 98312 | tf_op jit(solution)/shard_map/ppermute | solution.py:299
  122.1 2.9 %collective-permute-done.47.refs_7_.refs_11_.refs_23_.refs_27_ = bf16[2,32,256]{2,1,0:T(8,128)(2,1)S(1)} collective-permute-done((bf16[2,32,256]{2,1,0:T(8,128)(2,1)S(1)}, bf16[2,32,256]{2,1,0:T(8,128)(2,1)S(1)}, u32[]{:S(2)}, u32[]{:S(2)}) %collective-permute-start.47) | collective-permute-done | bytes 32800 | tf_op jit(solution)/shard_map/ppermute | solution.py:299
  (123 shorter events, 50.8 us)
Async XLA Ops:
  1.3 12.4 %collective-permute-start.1 = (bf16[2,5,256,256]{3,2,1,0:T(8,128)(2,1)S(1)}, bf16[2,5,256,256]{3,2,1,0:T(8,128)(2,1)S(1)}, u32[]{:S(2)}, u32[]{:S(2)}) collective-permute-start(bf16[2,5,256,256]{3,2,1,0:T(8,128)(2,1)S(1)} %shard_map.56.own_ref.io), channel_id=1, source_target_pairs={{0,4},{4,0},{8,12},{12,8},{16,20},{20,16},{24,28},{28,24},{1,5},{5... | collective-permute-start | bytes 3932168 | tf_op jit(solution)/shard_map/ppermute | solution.py:296
  3.3 5.7 %collective-permute-start.3 = (s32[16,4]{1,0:T(8,128)S(1)}, s32[16,4]{1,0:T(8,128)S(1)}, u32[]{:S(2)}, u32[]{:S(2)}) collective-permute-start(s32[16,4]{1,0:T(8,128)S(1)} %fusion.5), channel_id=1, source_target_pairs={{0,4},{4,0},{8,12},{12,8},{16,20},{20,16},{24,28},{28,24},{1,5},{5... | collective-permute-start | bytes 776 | tf_op jit(solution)/shard_map/ppermute | solution.py:296
  4.6 6.0 %collective-permute-start.4 = (bf16[2,32,256]{2,1,0:T(8,128)(2,1)S(1)}, bf16[2,32,256]{2,1,0:T(8,128)(2,1)S(1)}, u32[]{:S(2)}, u32[]{:S(2)}) collective-permute-start(bf16[2,32,256]{2,1,0:T(8,128)(2,1)S(1)} %shard_map.58.refs_0_.old.solved_ref), channel_id=1, source_target_pairs={{0,8},{4,12},{8,0},{12,4},{16,24},{20,28},{24,16},{28,20},{1,9},{5... | collective-permute-start | bytes 98312 | tf_op jit(solution)/shard_map/ppermute | solution.py:296
  15.8 14.2 %collective-permute-start.9 = (bf16[2,5,256,256]{3,2,1,0:T(8,128)(2,1)S(1)}, bf16[2,5,256,256]{3,2,1,0:T(8,128)(2,1)S(1)}, u32[]{:S(2)}, u32[]{:S(2)}) collective-permute-start(bf16[2,5,256,256]{3,2,1,0:T(8,128)(2,1)S(1)} %shard_map.63.own_ref.io), channel_id=1, source_target_pairs={{0,4},{4,0},{8,12},{12,8},{16,20},{20,16},{24,28},{28,24},{1,5},{5... | collective-permute-start | bytes 3932168 | tf_op jit(solution)/shard_map/ppermute | solution.py:296
  17.1 28.0 %collective-permute-start.13 = (bf16[2,5,256,256]{3,2,1,0:T(8,128)(2,1)S(1)}, bf16[2,5,256,256]{3,2,1,0:T(8,128)(2,1)S(1)}, u32[]{:S(2)}, u32[]{:S(2)}) collective-permute-start(bf16[2,5,256,256]{3,2,1,0:T(8,128)(2,1)S(1)} %shard_map.65.own_ref.io), channel_id=1, source_target_pairs={{0,4},{4,0},{8,12},{12,8},{16,20},{20,16},{24,28},{28,24},{1,5},{5... | collective-permute-start | bytes 3932168 | tf_op jit(solution)/shard_map/ppermute | solution.py:296
  20.8 5.7 %collective-permute-start.8 = (bf16[2,32,256]{2,1,0:T(8,128)(2,1)S(1)}, bf16[2,32,256]{2,1,0:T(8,128)(2,1)S(1)}, u32[]{:S(2)}, u32[]{:S(2)}) collective-permute-start(bf16[2,32,256]{2,1,0:T(8,128)(2,1)S(1)} %get-tuple-element.45.refs_1_), channel_id=1, source_target_pairs={{0,3},{1,2},{2,1},{3,0},{4,7},{5,6},{6,5},{7,4},{8,11},{9,10},{10,... | collective-permute-start | bytes 98312 | tf_op jit(solution)/shard_map/ppermute | solution.py:306
  33.6 28.6 %collective-permute-start.21 = (bf16[2,5,256,256]{3,2,1,0:T(8,128)(2,1)S(1)}, bf16[2,5,256,256]{3,2,1,0:T(8,128)(2,1)S(1)}, u32[]{:S(2)}, u32[]{:S(2)}) collective-permute-start(bf16[2,5,256,256]{3,2,1,0:T(8,128)(2,1)S(1)} %shard_map.70.own_ref.io), channel_id=1, source_target_pairs={{0,4},{4,0},{8,12},{12,8},{16,20},{20,16},{24,28},{28,24},{1,5},{5... | collective-permute-start | bytes 3932168 | tf_op jit(solution)/shard_map/ppermute | solution.py:296
  33.7 5.4 %collective-permute-start.15 = (bf16[2,32,256]{2,1,0:T(8,128)(2,1)S(1)}, bf16[2,32,256]{2,1,0:T(8,128)(2,1)S(1)}, u32[]{:S(2)}, u32[]{:S(2)}) collective-permute-start(bf16[2,32,256]{2,1,0:T(8,128)(2,1)S(1)} %get-tuple-element.49.refs_0_), channel_id=1, source_target_pairs={{0,2},{1,3},{2,0},{3,1},{4,6},{5,7},{6,4},{7,5},{8,10},{9,11},{10,... | collective-permute-start | bytes 98312 | tf_op jit(solution)/shard_map/ppermute | solution.py:306
  35.4 6.0 %collective-permute-start.16 = (bf16[2,32,256]{2,1,0:T(8,128)(2,1)S(1)}, bf16[2,32,256]{2,1,0:T(8,128)(2,1)S(1)}, u32[]{:S(2)}, u32[]{:S(2)}) collective-permute-start(bf16[2,32,256]{2,1,0:T(8,128)(2,1)S(1)} %get-tuple-element.50.refs_1_), channel_id=1, source_target_pairs={{0,3},{1,2},{2,1},{3,0},{4,7},{5,6},{6,5},{7,4},{8,11},{9,10},{10,... | collective-permute-start | bytes 98312 | tf_op jit(solution)/shard_map/ppermute | solution.py:306
  51.5 28.4 %collective-permute-start.28 = (bf16[2,5,256,256]{3,2,1,0:T(8,128)(2,1)S(1)}, bf16[2,5,256,256]{3,2,1,0:T(8,128)(2,1)S(1)}, u32[]{:S(2)}, u32[]{:S(2)}) collective-permute-start(bf16[2,5,256,256]{3,2,1,0:T(8,128)(2,1)S(1)} %shard_map.74.own_ref.io), channel_id=1, source_target_pairs={{0,4},{4,0},{8,12},{12,8},{16,20},{20,16},{24,28},{28,24},{1,5},{5... | collective-permute-start | bytes 3932168 | tf_op jit(solution)/shard_map/ppermute | solution.py:296
  51.6 5.0 %collective-permute-start.23 = (bf16[2,32,256]{2,1,0:T(8,128)(2,1)S(1)}, bf16[2,32,256]{2,1,0:T(8,128)(2,1)S(1)}, u32[]{:S(2)}, u32[]{:S(2)}) collective-permute-start(bf16[2,32,256]{2,1,0:T(8,128)(2,1)S(1)} %get-tuple-element.55.refs_0_), channel_id=1, source_target_pairs={{0,2},{1,3},{2,0},{3,1},{4,6},{5,7},{6,4},{7,5},{8,10},{9,11},{10,... | collective-permute-start | bytes 98312 | tf_op jit(solution)/shard_map/ppermute | solution.py:306
  53.0 5.7 %collective-permute-start.24 = (bf16[2,32,256]{2,1,0:T(8,128)(2,1)S(1)}, bf16[2,32,256]{2,1,0:T(8,128)(2,1)S(1)}, u32[]{:S(2)}, u32[]{:S(2)}) collective-permute-start(bf16[2,32,256]{2,1,0:T(8,128)(2,1)S(1)} %get-tuple-element.56.refs_1_), channel_id=1, source_target_pairs={{0,3},{1,2},{2,1},{3,0},{4,7},{5,6},{6,5},{7,4},{8,11},{9,10},{10,... | collective-permute-start | bytes 98312 | tf_op jit(solution)/shard_map/ppermute | solution.py:306
  65.9 30.6 %collective-permute-start.35 = (bf16[2,5,256,256]{3,2,1,0:T(8,128)(2,1)S(1)}, bf16[2,5,256,256]{3,2,1,0:T(8,128)(2,1)S(1)}, u32[]{:S(2)}, u32[]{:S(2)}) collective-permute-start(bf16[2,5,256,256]{3,2,1,0:T(8,128)(2,1)S(1)} %shard_map.78.own_ref.io), channel_id=1, source_target_pairs={{0,4},{4,0},{8,12},{12,8},{16,20},{20,16},{24,28},{28,24},{1,5},{5... | collective-permute-start | bytes 3932168 | tf_op jit(solution)/shard_map/ppermute | solution.py:296
  66.0 7.0 %collective-permute-start.30 = (bf16[2,32,256]{2,1,0:T(8,128)(2,1)S(1)}, bf16[2,32,256]{2,1,0:T(8,128)(2,1)S(1)}, u32[]{:S(2)}, u32[]{:S(2)}) collective-permute-start(bf16[2,32,256]{2,1,0:T(8,128)(2,1)S(1)} %get-tuple-element.60.refs_0_), channel_id=1, source_target_pairs={{0,2},{1,3},{2,0},{3,1},{4,6},{5,7},{6,4},{7,5},{8,10},{9,11},{10,... | collective-permute-start | bytes 98312 | tf_op jit(solution)/shard_map/ppermute | solution.py:306
  70.5 5.7 %collective-permute-start.31 = (bf16[2,32,256]{2,1,0:T(8,128)(2,1)S(1)}, bf16[2,32,256]{2,1,0:T(8,128)(2,1)S(1)}, u32[]{:S(2)}, u32[]{:S(2)}) collective-permute-start(bf16[2,32,256]{2,1,0:T(8,128)(2,1)S(1)} %get-tuple-element.61.refs_1_), channel_id=1, source_target_pairs={{0,3},{1,2},{2,1},{3,0},{4,7},{5,6},{6,5},{7,4},{8,11},{9,10},{10,... | collective-permute-start | bytes 98312 | tf_op jit(solution)/shard_map/ppermute | solution.py:306
  86.2 25.7 %collective-permute-start.49 = (bf16[2,5,256,256]{3,2,1,0:T(8,128)(2,1)S(1)}, bf16[2,5,256,256]{3,2,1,0:T(8,128)(2,1)S(1)}, u32[]{:S(2)}, u32[]{:S(2)}) collective-permute-start(bf16[2,5,256,256]{3,2,1,0:T(8,128)(2,1)S(1)} %shard_map.84.own_ref.io), channel_id=1, source_target_pairs={{0,4},{4,0},{8,12},{12,8},{16,20},{20,16},{24,28},{28,24},{1,5},{5... | collective-permute-start | bytes 3932168 | tf_op jit(solution)/shard_map/ppermute | solution.py:296
  86.4 5.0 %collective-permute-start.37 = (bf16[2,32,256]{2,1,0:T(8,128)(2,1)S(1)}, bf16[2,32,256]{2,1,0:T(8,128)(2,1)S(1)}, u32[]{:S(2)}, u32[]{:S(2)}) collective-permute-start(bf16[2,32,256]{2,1,0:T(8,128)(2,1)S(1)} %get-tuple-element.65.refs_0_), channel_id=1, source_target_pairs={{0,2},{1,3},{2,0},{3,1},{4,6},{5,7},{6,4},{7,5},{8,10},{9,11},{10,... | collective-permute-start | bytes 98312 | tf_op jit(solution)/shard_map/ppermute | solution.py:306
  86.5 6.5 %collective-permute-start.38 = (bf16[2,32,256]{2,1,0:T(8,128)(2,1)S(1)}, bf16[2,32,256]{2,1,0:T(8,128)(2,1)S(1)}, u32[]{:S(2)}, u32[]{:S(2)}) collective-permute-start(bf16[2,32,256]{2,1,0:T(8,128)(2,1)S(1)} %get-tuple-element.66.refs_1_), channel_id=1, source_target_pairs={{0,3},{1,2},{2,1},{3,0},{4,7},{5,6},{6,5},{7,4},{8,11},{9,10},{10,... | collective-permute-start | bytes 98312 | tf_op jit(solution)/shard_map/ppermute | solution.py:306
  93.0 4.9 %collective-permute-start.40 = (bf16[2,32,256]{2,1,0:T(8,128)(2,1)S(1)}, bf16[2,32,256]{2,1,0:T(8,128)(2,1)S(1)}, u32[]{:S(2)}, u32[]{:S(2)}) collective-permute-start(bf16[2,32,256]{2,1,0:T(8,128)(2,1)S(1)} %shard_map.80.refs_0_.old.refs_16_), channel_id=1, source_target_pairs={{0,8},{4,12},{8,0},{12,4},{16,24},{20,28},{24,16},{28,20},{1,9},{5... | collective-permute-start | bytes 98312 | tf_op jit(solution)/shard_map/ppermute | solution.py:296
  97.2 6.6 %collective-permute-start.36 = (bf16[2,32,256]{2,1,0:T(8,128)(2,1)S(1)}, bf16[2,32,256]{2,1,0:T(8,128)(2,1)S(1)}, u32[]{:S(2)}, u32[]{:S(2)}) collective-permute-start(bf16[2,32,256]{2,1,0:T(8,128)(2,1)S(1)} %get-tuple-element.64), channel_id=1, source_target_pairs={{0,1},{1,0},{2,3},{3,2},{4,5},{5,4},{6,7},{7,6},{8,9},{9,8},{10,11... | collective-permute-start | bytes 98312 | tf_op jit(solution)/shard_map/ppermute | solution.py:299
  98.9 5.0 %collective-permute-start.43 = (bf16[2,32,256]{2,1,0:T(8,128)(2,1)S(1)}, bf16[2,32,256]{2,1,0:T(8,128)(2,1)S(1)}, u32[]{:S(2)}, u32[]{:S(2)}) collective-permute-start(bf16[2,32,256]{2,1,0:T(8,128)(2,1)S(1)} %get-tuple-element.68), channel_id=1, source_target_pairs={{0,2},{1,3},{2,0},{3,1},{4,6},{5,7},{6,4},{7,5},{8,10},{9,11},{10,... | collective-permute-start | bytes 98312 | tf_op jit(solution)/shard_map/ppermute | solution.py:306
  101.5 5.9 %collective-permute-start.44 = (bf16[2,32,256]{2,1,0:T(8,128)(2,1)S(1)}, bf16[2,32,256]{2,1,0:T(8,128)(2,1)S(1)}, u32[]{:S(2)}, u32[]{:S(2)}) collective-permute-start(bf16[2,32,256]{2,1,0:T(8,128)(2,1)S(1)} %get-tuple-element.69), channel_id=1, source_target_pairs={{0,3},{1,2},{2,1},{3,0},{4,7},{5,6},{6,5},{7,4},{8,11},{9,10},{10,... | collective-permute-start | bytes 98312 | tf_op jit(solution)/shard_map/ppermute | solution.py:306
  103.4 7.8 %collective-permute-start.39 = (bf16[2,32,256]{2,1,0:T(8,128)(2,1)S(1)}, bf16[2,32,256]{2,1,0:T(8,128)(2,1)S(1)}, u32[]{:S(2)}, u32[]{:S(2)}) collective-permute-start(bf16[2,32,256]{2,1,0:T(8,128)(2,1)S(1)} %shard_map.80.refs_0_.old.refs_16_), channel_id=1, source_target_pairs={{0,1},{1,0},{2,3},{3,2},{4,5},{5,4},{6,7},{7,6},{8,9},{9,8},{10,11... | collective-permute-start | bytes 98312 | tf_op jit(solution)/shard_map/ppermute | solution.py:299
  107.6 5.7 %collective-permute-start.50 = (bf16[2,32,256]{2,1,0:T(8,128)(2,1)S(1)}, bf16[2,32,256]{2,1,0:T(8,128)(2,1)S(1)}, u32[]{:S(2)}, u32[]{:S(2)}) collective-permute-start(bf16[2,32,256]{2,1,0:T(8,128)(2,1)S(1)} %shard_map.82.refs_0_.refs_4_.refs_8_.refs_20_.refs_24_), channel_id=1, source_target_pairs={{0,8},{4,12},{8,0},{12,4},{16,24},{20,28},{24,16},{28,20},{1,9},{5... | collective-permute-start | bytes 98312 | tf_op jit(solution)/shard_map/ppermute | solution.py:296
  108.0 5.4 %collective-permute-start.51 = (bf16[2,32,256]{2,1,0:T(8,128)(2,1)S(1)}, bf16[2,32,256]{2,1,0:T(8,128)(2,1)S(1)}, u32[]{:S(2)}, u32[]{:S(2)}) collective-permute-start(bf16[2,32,256]{2,1,0:T(8,128)(2,1)S(1)} %shard_map.82.refs_0_.refs_4_.refs_8_.refs_20_.refs_24_), channel_id=1, source_target_pairs={{0,16},{4,20},{8,24},{12,28},{16,0},{20,4},{24,8},{28,12},{1,17},{... | collective-permute-start | bytes 98312 | tf_op jit(solution)/shard_map/ppermute | solution.py:296
  111.1 7.8 %collective-permute-start.45 = (bf16[2,32,256]{2,1,0:T(8,128)(2,1)S(1)}, bf16[2,32,256]{2,1,0:T(8,128)(2,1)S(1)}, u32[]{:S(2)}, u32[]{:S(2)}) collective-permute-start(bf16[2,32,256]{2,1,0:T(8,128)(2,1)S(1)} %shard_map.82.refs_0_.refs_4_.refs_8_.refs_20_.refs_24_), channel_id=1, source_target_pairs={{0,1},{1,0},{2,3},{3,2},{4,5},{5,4},{6,7},{7,6},{8,9},{9,8},{10,11... | collective-permute-start | bytes 98312 | tf_op jit(solution)/shard_map/ppermute | solution.py:299
  111.9 7.1 %collective-permute-start.46 = (bf16[2,32,256]{2,1,0:T(8,128)(2,1)S(1)}, bf16[2,32,256]{2,1,0:T(8,128)(2,1)S(1)}, u32[]{:S(2)}, u32[]{:S(2)}) collective-permute-start(bf16[2,32,256]{2,1,0:T(8,128)(2,1)S(1)} %shard_map.82.refs_0_.refs_4_.refs_8_.refs_20_.refs_24_), channel_id=1, source_target_pairs={{0,2},{1,3},{2,0},{3,1},{4,6},{5,7},{6,4},{7,5},{8,10},{9,11},{10,... | collective-permute-start | bytes 98312 | tf_op jit(solution)/shard_map/ppermute | solution.py:299
  114.5 10.4 %collective-permute-start.53 = (bf16[2,2,32,256]{3,2,1,0:T(8,128)(2,1)S(1)}, bf16[2,2,32,256]{3,2,1,0:T(8,128)(2,1)S(1)}, u32[]{:S(2)}, u32[]{:S(2)}) collective-permute-start(bf16[2,2,32,256]{3,2,1,0:T(8,128)(2,1)S(1)} %get-tuple-element.72.refs_0_), channel_id=1, source_target_pairs={{0,1},{1,0},{2,3},{3,2},{4,5},{5,4},{6,7},{7,6},{8,9},{9,8},{10,11... | collective-permute-start | bytes 196616 | tf_op jit(solution)/shard_map/ppermute | solution.py:299
  116.5 8.4 %collective-permute-start.54 = (bf16[2,2,32,256]{3,2,1,0:T(8,128)(2,1)S(1)}, bf16[2,2,32,256]{3,2,1,0:T(8,128)(2,1)S(1)}, u32[]{:S(2)}, u32[]{:S(2)}) collective-permute-start(bf16[2,2,32,256]{3,2,1,0:T(8,128)(2,1)S(1)} %get-tuple-element.72.refs_0_), channel_id=1, source_target_pairs={{0,2},{1,3},{2,0},{3,1},{4,6},{5,7},{6,4},{7,5},{8,10},{9,11},{10,... | collective-permute-start | bytes 196616 | tf_op jit(solution)/shard_map/ppermute | solution.py:299
  118.2 6.8 %collective-permute-start.55 = (bf16[2,2,32,256]{3,2,1,0:T(8,128)(2,1)S(1)}, bf16[2,2,32,256]{3,2,1,0:T(8,128)(2,1)S(1)}, u32[]{:S(2)}, u32[]{:S(2)}) collective-permute-start(bf16[2,2,32,256]{3,2,1,0:T(8,128)(2,1)S(1)} %get-tuple-element.72.refs_0_), channel_id=1, source_target_pairs={{0,3},{1,2},{2,1},{3,0},{4,7},{5,6},{6,5},{7,4},{8,11},{9,10},{10,... | collective-permute-start | bytes 196616 | tf_op jit(solution)/shard_map/ppermute | solution.py:299
  119.0 6.4 %collective-permute-start.48 = (bf16[10,32,256]{2,1,0:T(8,128)(2,1)S(1)}, bf16[10,32,256]{2,1,0:T(8,128)(2,1)S(1)}, u32[]{:S(2)}, u32[]{:S(2)}) collective-permute-start(bf16[10,32,256]{2,1,0:T(8,128)(2,1)S(1)} %shard_map.83), channel_id=1, source_target_pairs={{0,4},{4,0},{8,12},{12,8},{16,20},{20,16},{24,28},{28,24},{1,5},{5... | collective-permute-start | bytes 491528 | tf_op jit(solution)/shard_map/ppermute | solution.py:296
  119.0 6.0 %collective-permute-start.47 = (bf16[2,32,256]{2,1,0:T(8,128)(2,1)S(1)}, bf16[2,32,256]{2,1,0:T(8,128)(2,1)S(1)}, u32[]{:S(2)}, u32[]{:S(2)}) collective-permute-start(bf16[2,32,256]{2,1,0:T(8,128)(2,1)S(1)} %shard_map.82.refs_0_.refs_4_.refs_8_.refs_20_.refs_24_), channel_id=1, source_target_pairs={{0,3},{1,2},{2,1},{3,0},{4,7},{5,6},{6,5},{7,4},{8,11},{9,10},{10,... | collective-permute-start | bytes 98312 | tf_op jit(solution)/shard_map/ppermute | solution.py:299
  (27 other events, 108.3 us)

commit v3 on v2

--- a/solution.py
+++ b/solution.py
@@ -212,56 +212,57 @@
             write(level * LR + place, ref)
 
 
-def pack(found, levels, half, size):
-    first = levels[0] * LR
+def pack(found, late, first):
+    half, size = late[0].shape[1:]
 
     def body(*refs):
-        *sources, out = refs
+        sources, late_refs, out = refs[:len(found)], refs[len(found):-1], refs[-1]
 
         def write(row, ref):
-            out[row - first] = ref[1]
+            out[row] = ref[1]
 
         place_rows([(level, ref, away) for (level, _, away), ref in zip(found, sources)], lax.axis_index("pcol"), write)
-
-    return call(body, [((len(levels) * LR, half, size), BF16)], [x for _, x, _ in found])[0]
-
-
-def solve_last(rhs_own, rhs_other, own_tiles, other_tiles, parts, found, first):
+        for i, ref in enumerate(late_refs):
+            out[first * LR + i] = ref[1]
+
+    return call(body, [((first * LR + len(late), half, size), BF16)], [*[x for _, x, _ in found], *late])[0]
+
+
+def whole_rows(late, swapped, first):
+    def body(*refs):
+        late_refs, swapped_ref, outs = refs[:len(late)], refs[len(late)], refs[len(late) + 1:]
+        for i, (ref, out) in enumerate(zip(late_refs, outs)):
+            out[0] = ref[0]
+            out[1] = swapped_ref[first * LR + i]
+
+    return call(body, [(y.shape, BF16) for y in late], [*late, swapped])
+
+
+def solve_last(rhs_own, rhs_other, own_tiles, other_tiles, parts):
     count = len(parts)
-    half, size = rhs_own.shape[1:]
 
     def body(ro, rp, io, ip, *refs):
-        parts_refs, sources, (own, send, held) = refs[:count], refs[count:-3], refs[-3:]
+        *parts_refs, own, send, held = refs
         col = lax.axis_index("pcol")
         for k in range(count):
             held[jnp.bitwise_xor(col, k)] = parts_refs[k][...]
-        for pair in range(2):
-            r_ref, i_ref = (rp, ip) if pair else (ro, io)
+        for r_ref, i_ref, pair, out in ((rp, ip, 1, send), (ro, io, 0, own)):
             for row in range(LR):
                 rest = r_ref[(LEVELS - 1) * LR + row].astype(F32)
                 for k in range(count):
                     rest = rest - held[k, row, pair].astype(F32)
-                done = dot_t(rest.astype(BF16), i_ref[row, i_ref.shape[1] - 1]).astype(BF16)
-                if pair:
-                    send[(LEVELS - 1 - first) * LR + row] = done
-                else:
-                    own[row] = done
-
-        def write(row, ref):
-            send[row - first * LR] = ref[1]
-
-        place_rows([(level, ref, away) for (level, _, away), ref in zip(found, sources)], col, write)
-
-    outs = [((LR, half, size), BF16), (((LEVELS - first) * LR, half, size), BF16)]
-    return call(body, outs, [rhs_own, rhs_other, own_tiles, other_tiles, *parts, *[x for _, x, _ in found]],
+                out[row] = dot_t(rest.astype(BF16), i_ref[row, i_ref.shape[1] - 1]).astype(BF16)
+
+    shape = ((LR,) + rhs_own.shape[1:], BF16)
+    return call(body, [shape, shape], [rhs_own, rhs_other, own_tiles, other_tiles, *parts],
                 scratch=[pltpu.VMEM((count,) + parts[0].shape, BF16)])
 
 
-def assemble(found, swapped, own, shape):
+def assemble(found, late, swapped, own, last_swapped, shape, first):
     half = shape[1] // 2
 
     def body(*refs):
-        sources, swaps, own_ref, out = refs[:len(found)], refs[len(found):-2], refs[-2], refs[-1]
+        sources, (swapped_ref, own_ref, last_ref, out) = refs[:-4], refs[-4:]
         col = lax.axis_index("pcol")
         core = lax.rem(lax.axis_index("prow"), 2)
         mine_at = pl.ds(pl.multiple_of(core * half, half), half)
@@ -270,16 +271,20 @@
         def write(row, ref):
             out[row, mine_at] = ref[0]
 
+        def write_both(row, ref):
+            out[row, mine_at] = ref[0]
+            out[row, theirs_at] = ref[1]
+
         place_rows([(level, ref, away) for (level, _, away), ref in zip(found, sources)], col, write)
-        row = 0
-        for ref in swaps:
-            for i in range(ref.shape[0]):
-                out[row, theirs_at] = ref[i]
-                row += 1
+        place_rows([(level, ref, away) for (level, _, away), ref in zip(late, sources[len(found):])], col, write_both)
+        for row in range(first * LR):
+            out[row, theirs_at] = swapped_ref[row]
         for i in range(LR):
             out[(LEVELS - 1) * LR + i, mine_at] = own_ref[i]
-
-    return call(body, [(shape, BF16)], [*[x for _, x, _ in found], *swapped, own])[0]
+            out[(LEVELS - 1) * LR + i, theirs_at] = last_ref[i]
+
+    ins = [*[x for _, x, _ in found + late], swapped, own, last_swapped]
+    return call(body, [(shape, BF16)], ins)[0]
 
 
 def body(rhs, blocks, inverses, columns, counts):
@@ -328,17 +333,21 @@
         newest = level - 1
         last = level == LEVELS - 1
         y = solved[newest]
-        pieces = [y] + [prow_swap(y, k) for k in range(2, prow_count, 2)]
+        pieces = [y]
+        for k in range(2, prow_count, 2):
+            pieces.append(prow_swap(y, k))
         if last:
-            late = [newest - g for g in range(groups)] if paired else list(range(newest, -1, -1))
-            rest = [(late[:groups], y)] if paired else [([i], solved[i]) for i in late]
-            spread = [(y, share(y))] if paired else [(solved[i], share(solved[i])) for i in late]
-            for (levels, _), (_, copies) in zip(rest, spread):
-                found += [(i, copy, k) for i in levels for k, copy in enumerate(copies)]
+            late = [([newest - g for g in range(groups)], y)] if paired else [([i], x) for i, x in enumerate(solved)]
+            first = min(min(levels) for levels, _ in late)
+            swapped = prow_swap(pack(found, [x for _, x in late], first), 1)
         store, *sums = update(level, table, store, pieces, held[level], other[level])
         if last:
             parts = share(sums[0])
-            break
+            rows_late = whole_rows([x for _, x in late], swapped, first)
+            spread = [(i, copy, k) for (levels, _), x in zip(late, rows_late)
+                      for k, copy in enumerate(share(x)) for i in levels]
+            own, send = solve_last(mine, theirs, held[level], other[level], parts)
+            return assemble(found, spread, swapped, own, prow_swap(send, 1), rhs.shape, first)
         terms = [between(sums[0], newest, level, 0)]
         terms.append(between(sums[1], newest, level, 1))
         reach = level + groups
@@ -367,12 +376,6 @@
             found += [(level - 2, terms[0], 2), (level - 2, terms[1], 3)]
         solved.append(solve(level, mine, theirs, held[level], other[level], y, terms + waiting[level]))
 
-    first = min(late)
-    swapped = [prow_swap(pack([f for f in found if f[0] < first], list(range(first)), half, size), 1)] if first else []
-    own, send = solve_last(mine, theirs, held[LEVELS - 1], other[LEVELS - 1], parts,
-                           [f for f in found if f[0] >= first], first)
-    return assemble(found, swapped + [prow_swap(send, 1)], own, rhs.shape)
-
 
 def solution(mesh):
     placed = (

time: 128 us -> 135 us (1.055)
  waiting for transfers between devices: 43.5 us -> 50.8 us
    ppermute x12, waiting for transfers between devices: 2.89 us -> 8.07 us  [pcol_swap(): return lax.ppermute(x, 'pcol', [(i, i ^ k) for i in range(pcol_count)])]
    ppermute x33, waiting for transfers between devices: 18.7 us -> 20.8 us  [prow_swap(): return lax.ppermute(x, 'prow', [(i, i ^ k) for i in range(prow_count)])]
    pallas_call x32 -> x33, Pallas kernels: 17.3 us -> 17.4 us  [call(): pl.pallas_call(body, out_shape=[pltpu.VMEM(shape, kind) for shape, kind i...]
  transfers between devices with their start and end apart: 57 -> 57, of which waited for: 29 -> 33; matrix products, arithmetic and copies ran while one was open for 1% -> 1% of each run, Pallas kernels for 12% -> 11%
where the time goes in v3:
time: 135 us; the launch traced here: 134 us
  starting transfers between devices  63.3 us (47%)
  waiting for transfers between devices  50.8 us (38%)
  Pallas kernels  18.2 us (13%)
    ppermute x33, starting transfers between devices, prow_swap(): return lax.ppermute(x, 'prow', [(i, i ^ k) for i in range(prow_count)])  27.7 us
    ppermute x12, starting transfers between devices, between(): return lax.ppermute(x, 'pcol', sorted(set(pairs)))  24.8 us
    ppermute x12, waiting for transfers between devices, between(): return lax.ppermute(x, 'pcol', sorted(set(pairs)))  22 us
    ppermute x33, waiting for transfers between devices, prow_swap(): return lax.ppermute(x, 'prow', [(i, i ^ k) for i in range(prow_count)])  20.8 us
    pallas_call x33, Pallas kernels, call(): pl.pallas_call(body, out_shape=[pltpu.VMEM(shape, kind) for shape, kind i...  17.4 us
    ppermute x12, starting transfers between devices, pcol_swap(): return lax.ppermute(x, 'pcol', [(i, i ^ k) for i in range(pcol_count)])  10.8 us
    ppermute x12, waiting for transfers between devices, pcol_swap(): return lax.ppermute(x, 'pcol', [(i, i ^ k) for i in range(pcol_count)])  8.07 us
  transfers between devices with their start and end apart: 57, of which 33 were waited for; matrix products, arithmetic and copies ran while one was open for 1% of the time, Pallas kernels for 11%

profile of v3, /device:TPU:0, one launch (start us, length us, event | category | flops | bytes accessed | tf_op | source)
XLA Modules:
  0.0 134.3 jit_solution(16179981016590963581)
XLA Ops:
  4.6 2.8 %collective-permute-start.4 = (bf16[2,32,256]{2,1,0:T(8,128)(2,1)S(1)}, bf16[2,32,256]{2,1,0:T(8,128)(2,1)S(1)}, u32[]{:S(2)}, u32[]{:S(2)}) collective-permute-start(bf16[2,32,256]{2,1,0:T(8,128)(2,1)S(1)} %shard_map.58.refs_0_.old.solved_ref), channel_id=1, source_target_pairs={{0,8},{4,12},{8,0},{12,4},{16,24},{20,28},{24,16},{28,20},{1,9},{5... | collective-permute-start | bytes 98312 | tf_op jit(solution)/shard_map/ppermute | solution.py:301
  11.3 2.4 %collective-permute-done.6.refs_3_ = bf16[2,32,256]{2,1,0:T(8,128)(2,1)S(1)} collective-permute-done((bf16[2,32,256]{2,1,0:T(8,128)(2,1)S(1)}, bf16[2,32,256]{2,1,0:T(8,128)(2,1)S(1)}, u32[]{:S(2)}, u32[]{:S(2)}) %collective-permute-start.6) | collective-permute-done | bytes 32800 | tf_op jit(solution)/shard_map/ppermute | solution.py:301
  18.8 1.9 %collective-permute-start.7 = (bf16[2,32,256]{2,1,0:T(8,128)(2,1)S(1)}, bf16[2,32,256]{2,1,0:T(8,128)(2,1)S(1)}, u32[]{:S(2)}, u32[]{:S(2)}) collective-permute-start(bf16[2,32,256]{2,1,0:T(8,128)(2,1)S(1)} %get-tuple-element.44.refs_0_), channel_id=1, source_target_pairs={{0,2},{1,3},{2,0},{3,1},{4,6},{5,7},{6,4},{7,5},{8,10},{9,11},{10,... | collective-permute-start | bytes 98312 | tf_op jit(solution)/shard_map/ppermute | solution.py:311
  20.8 2.1 %collective-permute-start.8 = (bf16[2,32,256]{2,1,0:T(8,128)(2,1)S(1)}, bf16[2,32,256]{2,1,0:T(8,128)(2,1)S(1)}, u32[]{:S(2)}, u32[]{:S(2)}) collective-permute-start(bf16[2,32,256]{2,1,0:T(8,128)(2,1)S(1)} %get-tuple-element.45.refs_1_), channel_id=1, source_target_pairs={{0,3},{1,2},{2,1},{3,0},{4,7},{5,6},{6,5},{7,4},{8,11},{9,10},{10,... | collective-permute-start | bytes 98312 | tf_op jit(solution)/shard_map/ppermute | solution.py:311
  23.7 2.8 %collective-permute-done.8.refs_1_ = bf16[2,32,256]{2,1,0:T(8,128)(2,1)S(1)} collective-permute-done((bf16[2,32,256]{2,1,0:T(8,128)(2,1)S(1)}, bf16[2,32,256]{2,1,0:T(8,128)(2,1)S(1)}, u32[]{:S(2)}, u32[]{:S(2)}) %collective-permute-start.8) | collective-permute-done | bytes 32800 | tf_op jit(solution)/shard_map/ppermute | solution.py:311
  27.5 2.4 %collective-permute-start.12 = (bf16[2,32,256]{2,1,0:T(8,128)(2,1)S(1)}, bf16[2,32,256]{2,1,0:T(8,128)(2,1)S(1)}, u32[]{:S(2)}, u32[]{:S(2)}) collective-permute-start(bf16[2,32,256]{2,1,0:T(8,128)(2,1)S(1)} %shard_map.62.refs_0_.solved_ref.old), channel_id=1, source_target_pairs={{0,24},{4,28},{8,16},{12,20},{16,8},{20,12},{24,0},{28,4},{1,25},{... | collective-permute-start | bytes 98312 | tf_op jit(solution)/shard_map/ppermute | solution.py:301
  33.7 1.7 %collective-permute-start.15 = (bf16[2,32,256]{2,1,0:T(8,128)(2,1)S(1)}, bf16[2,32,256]{2,1,0:T(8,128)(2,1)S(1)}, u32[]{:S(2)}, u32[]{:S(2)}) collective-permute-start(bf16[2,32,256]{2,1,0:T(8,128)(2,1)S(1)} %get-tuple-element.49.refs_0_), channel_id=1, source_target_pairs={{0,2},{1,3},{2,0},{3,1},{4,6},{5,7},{6,4},{7,5},{8,10},{9,11},{10,... | collective-permute-start | bytes 98312 | tf_op jit(solution)/shard_map/ppermute | solution.py:311
  37.3 1.8 %collective-permute-done.15.refs_0_.refs_2_ = bf16[2,32,256]{2,1,0:T(8,128)(2,1)S(1)} collective-permute-done((bf16[2,32,256]{2,1,0:T(8,128)(2,1)S(1)}, bf16[2,32,256]{2,1,0:T(8,128)(2,1)S(1)}, u32[]{:S(2)}, u32[]{:S(2)}) %collective-permute-start.15) | collective-permute-done | bytes 32800 | tf_op jit(solution)/shard_map/ppermute | solution.py:311
  39.1 2.3 %collective-permute-done.16.refs_1_.refs_3_ = bf16[2,32,256]{2,1,0:T(8,128)(2,1)S(1)} collective-permute-done((bf16[2,32,256]{2,1,0:T(8,128)(2,1)S(1)}, bf16[2,32,256]{2,1,0:T(8,128)(2,1)S(1)}, u32[]{:S(2)}, u32[]{:S(2)}) %collective-permute-start.16) | collective-permute-done | bytes 32800 | tf_op jit(solution)/shard_map/ppermute | solution.py:311
  47.2 2.3 %collective-permute-done.20.refs_3_ = bf16[2,32,256]{2,1,0:T(8,128)(2,1)S(1)} collective-permute-done((bf16[2,32,256]{2,1,0:T(8,128)(2,1)S(1)}, bf16[2,32,256]{2,1,0:T(8,128)(2,1)S(1)}, u32[]{:S(2)}, u32[]{:S(2)}) %collective-permute-start.20) | collective-permute-done | bytes 32800 | tf_op jit(solution)/shard_map/ppermute | solution.py:301
  53.0 3.0 %collective-permute-start.24 = (bf16[2,32,256]{2,1,0:T(8,128)(2,1)S(1)}, bf16[2,32,256]{2,1,0:T(8,128)(2,1)S(1)}, u32[]{:S(2)}, u32[]{:S(2)}) collective-permute-start(bf16[2,32,256]{2,1,0:T(8,128)(2,1)S(1)} %get-tuple-element.56.refs_1_), channel_id=1, source_target_pairs={{0,3},{1,2},{2,1},{3,0},{4,7},{5,6},{6,5},{7,4},{8,11},{9,10},{10,... | collective-permute-start | bytes 98312 | tf_op jit(solution)/shard_map/ppermute | solution.py:311
  56.6 2.1 %collective-permute-done.24.refs_1_.refs_7_ = bf16[2,32,256]{2,1,0:T(8,128)(2,1)S(1)} collective-permute-done((bf16[2,32,256]{2,1,0:T(8,128)(2,1)S(1)}, bf16[2,32,256]{2,1,0:T(8,128)(2,1)S(1)}, u32[]{:S(2)}, u32[]{:S(2)}) %collective-permute-start.24) | collective-permute-done | bytes 32800 | tf_op jit(solution)/shard_map/ppermute | solution.py:311
  59.8 2.4 %collective-permute-start.27 = (bf16[2,32,256]{2,1,0:T(8,128)(2,1)S(1)}, bf16[2,32,256]{2,1,0:T(8,128)(2,1)S(1)}, u32[]{:S(2)}, u32[]{:S(2)}) collective-permute-start(bf16[2,32,256]{2,1,0:T(8,128)(2,1)S(1)} %shard_map.72.refs_0_.solved_ref.old.refs_8_), channel_id=1, source_target_pairs={{0,24},{4,28},{8,16},{12,20},{16,8},{20,12},{24,0},{28,4},{1,25},{... | collective-permute-start | bytes 98312 | tf_op jit(solution)/shard_map/ppermute | solution.py:301
  66.0 4.4 %collective-permute-start.30 = (bf16[2,32,256]{2,1,0:T(8,128)(2,1)S(1)}, bf16[2,32,256]{2,1,0:T(8,128)(2,1)S(1)}, u32[]{:S(2)}, u32[]{:S(2)}) collective-permute-start(bf16[2,32,256]{2,1,0:T(8,128)(2,1)S(1)} %get-tuple-element.60.refs_0_), channel_id=1, source_target_pairs={{0,2},{1,3},{2,0},{3,1},{4,6},{5,7},{6,4},{7,5},{8,10},{9,11},{10,... | collective-permute-start | bytes 98312 | tf_op jit(solution)/shard_map/ppermute | solution.py:311
  70.5 2.6 %collective-permute-done.30.refs_0_.refs_10_ = bf16[2,32,256]{2,1,0:T(8,128)(2,1)S(1)} collective-permute-done((bf16[2,32,256]{2,1,0:T(8,128)(2,1)S(1)}, bf16[2,32,256]{2,1,0:T(8,128)(2,1)S(1)}, u32[]{:S(2)}, u32[]{:S(2)}) %collective-permute-start.30) | collective-permute-done | bytes 32800 | tf_op jit(solution)/shard_map/ppermute | solution.py:311
  73.1 3.1 %collective-permute-done.31.refs_1_.refs_11_ = bf16[2,32,256]{2,1,0:T(8,128)(2,1)S(1)} collective-permute-done((bf16[2,32,256]{2,1,0:T(8,128)(2,1)S(1)}, bf16[2,32,256]{2,1,0:T(8,128)(2,1)S(1)}, u32[]{:S(2)}, u32[]{:S(2)}) %collective-permute-start.31) | collective-permute-done | bytes 32800 | tf_op jit(solution)/shard_map/ppermute | solution.py:311
  82.0 2.3 %collective-permute-done.34.refs_3_ = bf16[2,32,256]{2,1,0:T(8,128)(2,1)S(1)} collective-permute-done((bf16[2,32,256]{2,1,0:T(8,128)(2,1)S(1)}, bf16[2,32,256]{2,1,0:T(8,128)(2,1)S(1)}, u32[]{:S(2)}, u32[]{:S(2)}) %collective-permute-start.34) | collective-permute-done | bytes 32800 | tf_op jit(solution)/shard_map/ppermute | solution.py:301
  86.5 4.3 %collective-permute-start.38 = (bf16[2,32,256]{2,1,0:T(8,128)(2,1)S(1)}, bf16[2,32,256]{2,1,0:T(8,128)(2,1)S(1)}, u32[]{:S(2)}, u32[]{:S(2)}) collective-permute-start(bf16[2,32,256]{2,1,0:T(8,128)(2,1)S(1)} %get-tuple-element.66.refs_1_), channel_id=1, source_target_pairs={{0,3},{1,2},{2,1},{3,0},{4,7},{5,6},{6,5},{7,4},{8,11},{9,10},{10,... | collective-permute-start | bytes 98312 | tf_op jit(solution)/shard_map/ppermute | solution.py:311
  91.4 1.6 %collective-permute-done.38.refs_1_.refs_15_ = bf16[2,32,256]{2,1,0:T(8,128)(2,1)S(1)} collective-permute-done((bf16[2,32,256]{2,1,0:T(8,128)(2,1)S(1)}, bf16[2,32,256]{2,1,0:T(8,128)(2,1)S(1)}, u32[]{:S(2)}, u32[]{:S(2)}) %collective-permute-start.38) | collective-permute-done | bytes 32800 | tf_op jit(solution)/shard_map/ppermute | solution.py:311
  94.1 2.4 %collective-permute-start.42 = (bf16[2,32,256]{2,1,0:T(8,128)(2,1)S(1)}, bf16[2,32,256]{2,1,0:T(8,128)(2,1)S(1)}, u32[]{:S(2)}, u32[]{:S(2)}) collective-permute-start(bf16[2,32,256]{2,1,0:T(8,128)(2,1)S(1)} %shard_map.80.refs_0_.old.refs_16_), channel_id=1, source_target_pairs={{0,24},{4,28},{8,16},{12,20},{16,8},{20,12},{24,0},{28,4},{1,25},{... | collective-permute-start | bytes 98312 | tf_op jit(solution)/shard_map/ppermute | solution.py:301
  98.9 2.6 %collective-permute-start.43 = (bf16[2,32,256]{2,1,0:T(8,128)(2,1)S(1)}, bf16[2,32,256]{2,1,0:T(8,128)(2,1)S(1)}, u32[]{:S(2)}, u32[]{:S(2)}) collective-permute-start(bf16[2,32,256]{2,1,0:T(8,128)(2,1)S(1)} %get-tuple-element.68), channel_id=1, source_target_pairs={{0,2},{1,3},{2,0},{3,1},{4,6},{5,7},{6,4},{7,5},{8,10},{9,11},{10,... | collective-permute-start | bytes 98312 | tf_op jit(solution)/shard_map/ppermute | solution.py:311
  101.5 1.8 %collective-permute-start.44 = (bf16[2,32,256]{2,1,0:T(8,128)(2,1)S(1)}, bf16[2,32,256]{2,1,0:T(8,128)(2,1)S(1)}, u32[]{:S(2)}, u32[]{:S(2)}) collective-permute-start(bf16[2,32,256]{2,1,0:T(8,128)(2,1)S(1)} %get-tuple-element.69), channel_id=1, source_target_pairs={{0,3},{1,2},{2,1},{3,0},{4,7},{5,6},{6,5},{7,4},{8,11},{9,10},{10,... | collective-permute-start | bytes 98312 | tf_op jit(solution)/shard_map/ppermute | solution.py:311
  103.9 3.5 %collective-permute-done.44.refs_1_.refs_19_ = bf16[2,32,256]{2,1,0:T(8,128)(2,1)S(1)} collective-permute-done((bf16[2,32,256]{2,1,0:T(8,128)(2,1)S(1)}, bf16[2,32,256]{2,1,0:T(8,128)(2,1)S(1)}, u32[]{:S(2)}, u32[]{:S(2)}) %collective-permute-start.44) | collective-permute-done | bytes 32800 | tf_op jit(solution)/shard_map/ppermute | solution.py:311
  109.0 1.5 %collective-permute-start.51 = (bf16[2,32,256]{2,1,0:T(8,128)(2,1)S(1)}, bf16[2,32,256]{2,1,0:T(8,128)(2,1)S(1)}, u32[]{:S(2)}, u32[]{:S(2)}) collective-permute-start(bf16[2,32,256]{2,1,0:T(8,128)(2,1)S(1)} %shard_map.82.refs_20_.refs_0_), channel_id=1, source_target_pairs={{0,16},{4,20},{8,24},{12,28},{16,0},{20,4},{24,8},{28,12},{1,17},{... | collective-permute-start | bytes 98312 | tf_op jit(solution)/shard_map/ppermute | solution.py:301
  112.9 2.4 %collective-permute-done.52.refs_3_ = bf16[2,32,256]{2,1,0:T(8,128)(2,1)S(1)} collective-permute-done((bf16[2,32,256]{2,1,0:T(8,128)(2,1)S(1)}, bf16[2,32,256]{2,1,0:T(8,128)(2,1)S(1)}, u32[]{:S(2)}, u32[]{:S(2)}) %collective-permute-start.52) | collective-permute-done | bytes 32800 | tf_op jit(solution)/shard_map/ppermute | solution.py:301
  116.8 1.6 %collective-permute-start.54 = (bf16[2,2,32,256]{3,2,1,0:T(8,128)(2,1)S(1)}, bf16[2,2,32,256]{3,2,1,0:T(8,128)(2,1)S(1)}, u32[]{:S(2)}, u32[]{:S(2)}) collective-permute-start(bf16[2,2,32,256]{3,2,1,0:T(8,128)(2,1)S(1)} %get-tuple-element.72.refs_0_), channel_id=1, source_target_pairs={{0,2},{1,3},{2,0},{3,1},{4,6},{5,7},{6,4},{7,5},{8,10},{9,11},{10,... | collective-permute-start | bytes 196616 | tf_op jit(solution)/shard_map/ppermute | solution.py:304
  118.5 2.0 %collective-permute-start.55 = (bf16[2,2,32,256]{3,2,1,0:T(8,128)(2,1)S(1)}, bf16[2,2,32,256]{3,2,1,0:T(8,128)(2,1)S(1)}, u32[]{:S(2)}, u32[]{:S(2)}) collective-permute-start(bf16[2,2,32,256]{3,2,1,0:T(8,128)(2,1)S(1)} %get-tuple-element.72.refs_0_), channel_id=1, source_target_pairs={{0,3},{1,2},{2,1},{3,0},{4,7},{5,6},{6,5},{7,4},{8,11},{9,10},{10,... | collective-permute-start | bytes 196616 | tf_op jit(solution)/shard_map/ppermute | solution.py:304
  120.5 2.8 %collective-permute-done.54.refs_2_ = bf16[2,2,32,256]{3,2,1,0:T(8,128)(2,1)S(1)} collective-permute-done((bf16[2,2,32,256]{3,2,1,0:T(8,128)(2,1)S(1)}, bf16[2,2,32,256]{3,2,1,0:T(8,128)(2,1)S(1)}, u32[]{:S(2)}, u32[]{:S(2)}) %collective-permute-start.54) | collective-permute-done | bytes 65568 | tf_op jit(solution)/shard_map/ppermute | solution.py:304
  125.6 2.0 %collective-permute-start.47 = (bf16[2,32,256]{2,1,0:T(8,128)(2,1)S(1)}, bf16[2,32,256]{2,1,0:T(8,128)(2,1)S(1)}, u32[]{:S(2)}, u32[]{:S(2)}) collective-permute-start(bf16[2,32,256]{2,1,0:T(8,128)(2,1)S(1)} %shard_map.84.refs_20_.refs_21_), channel_id=1, source_target_pairs={{0,2},{1,3},{2,0},{3,1},{4,6},{5,7},{6,4},{7,5},{8,10},{9,11},{10,... | collective-permute-start | bytes 98312 | tf_op jit(solution)/shard_map/ppermute | solution.py:304
  127.6 1.8 %collective-permute-start.48 = (bf16[2,32,256]{2,1,0:T(8,128)(2,1)S(1)}, bf16[2,32,256]{2,1,0:T(8,128)(2,1)S(1)}, u32[]{:S(2)}, u32[]{:S(2)}) collective-permute-start(bf16[2,32,256]{2,1,0:T(8,128)(2,1)S(1)} %shard_map.84.refs_20_.refs_21_), channel_id=1, source_target_pairs={{0,3},{1,2},{2,1},{3,0},{4,7},{5,6},{6,5},{7,4},{8,11},{9,10},{10,... | collective-permute-start | bytes 98312 | tf_op jit(solution)/shard_map/ppermute | solution.py:304
  129.4 1.9 %collective-permute-done.47.refs_24_.refs_25_ = bf16[2,32,256]{2,1,0:T(8,128)(2,1)S(1)} collective-permute-done((bf16[2,32,256]{2,1,0:T(8,128)(2,1)S(1)}, bf16[2,32,256]{2,1,0:T(8,128)(2,1)S(1)}, u32[]{:S(2)}, u32[]{:S(2)}) %collective-permute-start.47) | collective-permute-done | bytes 32800 | tf_op jit(solution)/shard_map/ppermute | solution.py:304
  131.4 1.9 %collective-permute-done.48.refs_26_.refs_27_ = bf16[2,32,256]{2,1,0:T(8,128)(2,1)S(1)} collective-permute-done((bf16[2,32,256]{2,1,0:T(8,128)(2,1)S(1)}, bf16[2,32,256]{2,1,0:T(8,128)(2,1)S(1)}, u32[]{:S(2)}, u32[]{:S(2)}) %collective-permute-start.48) | collective-permute-done | bytes 32800 | tf_op jit(solution)/shard_map/ppermute | solution.py:304
  (124 shorter events, 57.2 us)
Async XLA Ops:
  1.3 12.4 %collective-permute-start.1 = (bf16[2,5,256,256]{3,2,1,0:T(8,128)(2,1)S(1)}, bf16[2,5,256,256]{3,2,1,0:T(8,128)(2,1)S(1)}, u32[]{:S(2)}, u32[]{:S(2)}) collective-permute-start(bf16[2,5,256,256]{3,2,1,0:T(8,128)(2,1)S(1)} %shard_map.56.own_ref.io), channel_id=1, source_target_pairs={{0,4},{4,0},{8,12},{12,8},{16,20},{20,16},{24,28},{28,24},{1,5},{5... | collective-permute-start | bytes 3932168 | tf_op jit(solution)/shard_map/ppermute | solution.py:301
  3.3 5.7 %collective-permute-start.3 = (s32[16,4]{1,0:T(8,128)S(1)}, s32[16,4]{1,0:T(8,128)S(1)}, u32[]{:S(2)}, u32[]{:S(2)}) collective-permute-start(s32[16,4]{1,0:T(8,128)S(1)} %fusion.5), channel_id=1, source_target_pairs={{0,4},{4,0},{8,12},{12,8},{16,20},{20,16},{24,28},{28,24},{1,5},{5... | collective-permute-start | bytes 776 | tf_op jit(solution)/shard_map/ppermute | solution.py:301
  4.6 6.0 %collective-permute-start.4 = (bf16[2,32,256]{2,1,0:T(8,128)(2,1)S(1)}, bf16[2,32,256]{2,1,0:T(8,128)(2,1)S(1)}, u32[]{:S(2)}, u32[]{:S(2)}) collective-permute-start(bf16[2,32,256]{2,1,0:T(8,128)(2,1)S(1)} %shard_map.58.refs_0_.old.solved_ref), channel_id=1, source_target_pairs={{0,8},{4,12},{8,0},{12,4},{16,24},{20,28},{24,16},{28,20},{1,9},{5... | collective-permute-start | bytes 98312 | tf_op jit(solution)/shard_map/ppermute | solution.py:301
  8.9 4.8 %collective-permute-start.6 = (bf16[2,32,256]{2,1,0:T(8,128)(2,1)S(1)}, bf16[2,32,256]{2,1,0:T(8,128)(2,1)S(1)}, u32[]{:S(2)}, u32[]{:S(2)}) collective-permute-start(bf16[2,32,256]{2,1,0:T(8,128)(2,1)S(1)} %shard_map.58.refs_0_.old.solved_ref), channel_id=1, source_target_pairs={{0,24},{4,28},{8,16},{12,20},{16,8},{20,12},{24,0},{28,4},{1,25},{... | collective-permute-start | bytes 98312 | tf_op jit(solution)/shard_map/ppermute | solution.py:301
  15.8 14.2 %collective-permute-start.9 = (bf16[2,5,256,256]{3,2,1,0:T(8,128)(2,1)S(1)}, bf16[2,5,256,256]{3,2,1,0:T(8,128)(2,1)S(1)}, u32[]{:S(2)}, u32[]{:S(2)}) collective-permute-start(bf16[2,5,256,256]{3,2,1,0:T(8,128)(2,1)S(1)} %shard_map.63.own_ref.io), channel_id=1, source_target_pairs={{0,4},{4,0},{8,12},{12,8},{16,20},{20,16},{24,28},{28,24},{1,5},{5... | collective-permute-start | bytes 3932168 | tf_op jit(solution)/shard_map/ppermute | solution.py:301
  17.1 28.0 %collective-permute-start.13 = (bf16[2,5,256,256]{3,2,1,0:T(8,128)(2,1)S(1)}, bf16[2,5,256,256]{3,2,1,0:T(8,128)(2,1)S(1)}, u32[]{:S(2)}, u32[]{:S(2)}) collective-permute-start(bf16[2,5,256,256]{3,2,1,0:T(8,128)(2,1)S(1)} %shard_map.65.own_ref.io), channel_id=1, source_target_pairs={{0,4},{4,0},{8,12},{12,8},{16,20},{20,16},{24,28},{28,24},{1,5},{5... | collective-permute-start | bytes 3932168 | tf_op jit(solution)/shard_map/ppermute | solution.py:301
  18.8 4.9 %collective-permute-start.7 = (bf16[2,32,256]{2,1,0:T(8,128)(2,1)S(1)}, bf16[2,32,256]{2,1,0:T(8,128)(2,1)S(1)}, u32[]{:S(2)}, u32[]{:S(2)}) collective-permute-start(bf16[2,32,256]{2,1,0:T(8,128)(2,1)S(1)} %get-tuple-element.44.refs_0_), channel_id=1, source_target_pairs={{0,2},{1,3},{2,0},{3,1},{4,6},{5,7},{6,4},{7,5},{8,10},{9,11},{10,... | collective-permute-start | bytes 98312 | tf_op jit(solution)/shard_map/ppermute | solution.py:311
  20.8 5.7 %collective-permute-start.8 = (bf16[2,32,256]{2,1,0:T(8,128)(2,1)S(1)}, bf16[2,32,256]{2,1,0:T(8,128)(2,1)S(1)}, u32[]{:S(2)}, u32[]{:S(2)}) collective-permute-start(bf16[2,32,256]{2,1,0:T(8,128)(2,1)S(1)} %get-tuple-element.45.refs_1_), channel_id=1, source_target_pairs={{0,3},{1,2},{2,1},{3,0},{4,7},{5,6},{6,5},{7,4},{8,11},{9,10},{10,... | collective-permute-start | bytes 98312 | tf_op jit(solution)/shard_map/ppermute | solution.py:311
  27.5 4.8 %collective-permute-start.12 = (bf16[2,32,256]{2,1,0:T(8,128)(2,1)S(1)}, bf16[2,32,256]{2,1,0:T(8,128)(2,1)S(1)}, u32[]{:S(2)}, u32[]{:S(2)}) collective-permute-start(bf16[2,32,256]{2,1,0:T(8,128)(2,1)S(1)} %shard_map.62.refs_0_.solved_ref.old), channel_id=1, source_target_pairs={{0,24},{4,28},{8,16},{12,20},{16,8},{20,12},{24,0},{28,4},{1,25},{... | collective-permute-start | bytes 98312 | tf_op jit(solution)/shard_map/ppermute | solution.py:301
  33.6 28.6 %collective-permute-start.21 = (bf16[2,5,256,256]{3,2,1,0:T(8,128)(2,1)S(1)}, bf16[2,5,256,256]{3,2,1,0:T(8,128)(2,1)S(1)}, u32[]{:S(2)}, u32[]{:S(2)}) collective-permute-start(bf16[2,5,256,256]{3,2,1,0:T(8,128)(2,1)S(1)} %shard_map.70.own_ref.io), channel_id=1, source_target_pairs={{0,4},{4,0},{8,12},{12,8},{16,20},{20,16},{24,28},{28,24},{1,5},{5... | collective-permute-start | bytes 3932168 | tf_op jit(solution)/shard_map/ppermute | solution.py:301
  33.7 5.4 %collective-permute-start.15 = (bf16[2,32,256]{2,1,0:T(8,128)(2,1)S(1)}, bf16[2,32,256]{2,1,0:T(8,128)(2,1)S(1)}, u32[]{:S(2)}, u32[]{:S(2)}) collective-permute-start(bf16[2,32,256]{2,1,0:T(8,128)(2,1)S(1)} %get-tuple-element.49.refs_0_), channel_id=1, source_target_pairs={{0,2},{1,3},{2,0},{3,1},{4,6},{5,7},{6,4},{7,5},{8,10},{9,11},{10,... | collective-permute-start | bytes 98312 | tf_op jit(solution)/shard_map/ppermute | solution.py:311
  35.4 6.0 %collective-permute-start.16 = (bf16[2,32,256]{2,1,0:T(8,128)(2,1)S(1)}, bf16[2,32,256]{2,1,0:T(8,128)(2,1)S(1)}, u32[]{:S(2)}, u32[]{:S(2)}) collective-permute-start(bf16[2,32,256]{2,1,0:T(8,128)(2,1)S(1)} %get-tuple-element.50.refs_1_), channel_id=1, source_target_pairs={{0,3},{1,2},{2,1},{3,0},{4,7},{5,6},{6,5},{7,4},{8,11},{9,10},{10,... | collective-permute-start | bytes 98312 | tf_op jit(solution)/shard_map/ppermute | solution.py:311
  44.6 4.8 %collective-permute-start.20 = (bf16[2,32,256]{2,1,0:T(8,128)(2,1)S(1)}, bf16[2,32,256]{2,1,0:T(8,128)(2,1)S(1)}, u32[]{:S(2)}, u32[]{:S(2)}) collective-permute-start(bf16[2,32,256]{2,1,0:T(8,128)(2,1)S(1)} %shard_map.68.refs_0_.solved_ref.old.refs_4_), channel_id=1, source_target_pairs={{0,24},{4,28},{8,16},{12,20},{16,8},{20,12},{24,0},{28,4},{1,25},{... | collective-permute-start | bytes 98312 | tf_op jit(solution)/shard_map/ppermute | solution.py:301
  51.5 28.4 %collective-permute-start.28 = (bf16[2,5,256,256]{3,2,1,0:T(8,128)(2,1)S(1)}, bf16[2,5,256,256]{3,2,1,0:T(8,128)(2,1)S(1)}, u32[]{:S(2)}, u32[]{:S(2)}) collective-permute-start(bf16[2,5,256,256]{3,2,1,0:T(8,128)(2,1)S(1)} %shard_map.74.own_ref.io), channel_id=1, source_target_pairs={{0,4},{4,0},{8,12},{12,8},{16,20},{20,16},{24,28},{28,24},{1,5},{5... | collective-permute-start | bytes 3932168 | tf_op jit(solution)/shard_map/ppermute | solution.py:301
  51.6 5.0 %collective-permute-start.23 = (bf16[2,32,256]{2,1,0:T(8,128)(2,1)S(1)}, bf16[2,32,256]{2,1,0:T(8,128)(2,1)S(1)}, u32[]{:S(2)}, u32[]{:S(2)}) collective-permute-start(bf16[2,32,256]{2,1,0:T(8,128)(2,1)S(1)} %get-tuple-element.55.refs_0_), channel_id=1, source_target_pairs={{0,2},{1,3},{2,0},{3,1},{4,6},{5,7},{6,4},{7,5},{8,10},{9,11},{10,... | collective-permute-start | bytes 98312 | tf_op jit(solution)/shard_map/ppermute | solution.py:311
  53.0 5.7 %collective-permute-start.24 = (bf16[2,32,256]{2,1,0:T(8,128)(2,1)S(1)}, bf16[2,32,256]{2,1,0:T(8,128)(2,1)S(1)}, u32[]{:S(2)}, u32[]{:S(2)}) collective-permute-start(bf16[2,32,256]{2,1,0:T(8,128)(2,1)S(1)} %get-tuple-element.56.refs_1_), channel_id=1, source_target_pairs={{0,3},{1,2},{2,1},{3,0},{4,7},{5,6},{6,5},{7,4},{8,11},{9,10},{10,... | collective-permute-start | bytes 98312 | tf_op jit(solution)/shard_map/ppermute | solution.py:311
  65.9 30.6 %collective-permute-start.35 = (bf16[2,5,256,256]{3,2,1,0:T(8,128)(2,1)S(1)}, bf16[2,5,256,256]{3,2,1,0:T(8,128)(2,1)S(1)}, u32[]{:S(2)}, u32[]{:S(2)}) collective-permute-start(bf16[2,5,256,256]{3,2,1,0:T(8,128)(2,1)S(1)} %shard_map.78.own_ref.io), channel_id=1, source_target_pairs={{0,4},{4,0},{8,12},{12,8},{16,20},{20,16},{24,28},{28,24},{1,5},{5... | collective-permute-start | bytes 3932168 | tf_op jit(solution)/shard_map/ppermute | solution.py:301
  66.0 7.0 %collective-permute-start.30 = (bf16[2,32,256]{2,1,0:T(8,128)(2,1)S(1)}, bf16[2,32,256]{2,1,0:T(8,128)(2,1)S(1)}, u32[]{:S(2)}, u32[]{:S(2)}) collective-permute-start(bf16[2,32,256]{2,1,0:T(8,128)(2,1)S(1)} %get-tuple-element.60.refs_0_), channel_id=1, source_target_pairs={{0,2},{1,3},{2,0},{3,1},{4,6},{5,7},{6,4},{7,5},{8,10},{9,11},{10,... | collective-permute-start | bytes 98312 | tf_op jit(solution)/shard_map/ppermute | solution.py:311
  70.5 5.7 %collective-permute-start.31 = (bf16[2,32,256]{2,1,0:T(8,128)(2,1)S(1)}, bf16[2,32,256]{2,1,0:T(8,128)(2,1)S(1)}, u32[]{:S(2)}, u32[]{:S(2)}) collective-permute-start(bf16[2,32,256]{2,1,0:T(8,128)(2,1)S(1)} %get-tuple-element.61.refs_1_), channel_id=1, source_target_pairs={{0,3},{1,2},{2,1},{3,0},{4,7},{5,6},{6,5},{7,4},{8,11},{9,10},{10,... | collective-permute-start | bytes 98312 | tf_op jit(solution)/shard_map/ppermute | solution.py:311
  86.2 25.2 %collective-permute-start.49 = (bf16[2,5,256,256]{3,2,1,0:T(8,128)(2,1)S(1)}, bf16[2,5,256,256]{3,2,1,0:T(8,128)(2,1)S(1)}, u32[]{:S(2)}, u32[]{:S(2)}) collective-permute-start(bf16[2,5,256,256]{3,2,1,0:T(8,128)(2,1)S(1)} %shard_map.85.own_ref.io), channel_id=1, source_target_pairs={{0,4},{4,0},{8,12},{12,8},{16,20},{20,16},{24,28},{28,24},{1,5},{5... | collective-permute-start | bytes 3932168 | tf_op jit(solution)/shard_map/ppermute | solution.py:301
  86.4 5.0 %collective-permute-start.37 = (bf16[2,32,256]{2,1,0:T(8,128)(2,1)S(1)}, bf16[2,32,256]{2,1,0:T(8,128)(2,1)S(1)}, u32[]{:S(2)}, u32[]{:S(2)}) collective-permute-start(bf16[2,32,256]{2,1,0:T(8,128)(2,1)S(1)} %get-tuple-element.65.refs_0_), channel_id=1, source_target_pairs={{0,2},{1,3},{2,0},{3,1},{4,6},{5,7},{6,4},{7,5},{8,10},{9,11},{10,... | collective-permute-start | bytes 98312 | tf_op jit(solution)/shard_map/ppermute | solution.py:311
  86.5 6.5 %collective-permute-start.38 = (bf16[2,32,256]{2,1,0:T(8,128)(2,1)S(1)}, bf16[2,32,256]{2,1,0:T(8,128)(2,1)S(1)}, u32[]{:S(2)}, u32[]{:S(2)}) collective-permute-start(bf16[2,32,256]{2,1,0:T(8,128)(2,1)S(1)} %get-tuple-element.66.refs_1_), channel_id=1, source_target_pairs={{0,3},{1,2},{2,1},{3,0},{4,7},{5,6},{6,5},{7,4},{8,11},{9,10},{10,... | collective-permute-start | bytes 98312 | tf_op jit(solution)/shard_map/ppermute | solution.py:311
  93.0 4.9 %collective-permute-start.40 = (bf16[2,32,256]{2,1,0:T(8,128)(2,1)S(1)}, bf16[2,32,256]{2,1,0:T(8,128)(2,1)S(1)}, u32[]{:S(2)}, u32[]{:S(2)}) collective-permute-start(bf16[2,32,256]{2,1,0:T(8,128)(2,1)S(1)} %shard_map.80.refs_0_.old.refs_16_), channel_id=1, source_target_pairs={{0,8},{4,12},{8,0},{12,4},{16,24},{20,28},{24,16},{28,20},{1,9},{5... | collective-permute-start | bytes 98312 | tf_op jit(solution)/shard_map/ppermute | solution.py:301
  94.1 4.8 %collective-permute-start.42 = (bf16[2,32,256]{2,1,0:T(8,128)(2,1)S(1)}, bf16[2,32,256]{2,1,0:T(8,128)(2,1)S(1)}, u32[]{:S(2)}, u32[]{:S(2)}) collective-permute-start(bf16[2,32,256]{2,1,0:T(8,128)(2,1)S(1)} %shard_map.80.refs_0_.old.refs_16_), channel_id=1, source_target_pairs={{0,24},{4,28},{8,16},{12,20},{16,8},{20,12},{24,0},{28,4},{1,25},{... | collective-permute-start | bytes 98312 | tf_op jit(solution)/shard_map/ppermute | solution.py:301
  97.2 6.6 %collective-permute-start.36 = (bf16[2,32,256]{2,1,0:T(8,128)(2,1)S(1)}, bf16[2,32,256]{2,1,0:T(8,128)(2,1)S(1)}, u32[]{:S(2)}, u32[]{:S(2)}) collective-permute-start(bf16[2,32,256]{2,1,0:T(8,128)(2,1)S(1)} %get-tuple-element.64), channel_id=1, source_target_pairs={{0,1},{1,0},{2,3},{3,2},{4,5},{5,4},{6,7},{7,6},{8,9},{9,8},{10,11... | collective-permute-start | bytes 98312 | tf_op jit(solution)/shard_map/ppermute | solution.py:304
  98.9 5.0 %collective-permute-start.43 = (bf16[2,32,256]{2,1,0:T(8,128)(2,1)S(1)}, bf16[2,32,256]{2,1,0:T(8,128)(2,1)S(1)}, u32[]{:S(2)}, u32[]{:S(2)}) collective-permute-start(bf16[2,32,256]{2,1,0:T(8,128)(2,1)S(1)} %get-tuple-element.68), channel_id=1, source_target_pairs={{0,2},{1,3},{2,0},{3,1},{4,6},{5,7},{6,4},{7,5},{8,10},{9,11},{10,... | collective-permute-start | bytes 98312 | tf_op jit(solution)/shard_map/ppermute | solution.py:311
  101.5 5.9 %collective-permute-start.44 = (bf16[2,32,256]{2,1,0:T(8,128)(2,1)S(1)}, bf16[2,32,256]{2,1,0:T(8,128)(2,1)S(1)}, u32[]{:S(2)}, u32[]{:S(2)}) collective-permute-start(bf16[2,32,256]{2,1,0:T(8,128)(2,1)S(1)} %get-tuple-element.69), channel_id=1, source_target_pairs={{0,3},{1,2},{2,1},{3,0},{4,7},{5,6},{6,5},{7,4},{8,11},{9,10},{10,... | collective-permute-start | bytes 98312 | tf_op jit(solution)/shard_map/ppermute | solution.py:311
  107.8 17.2 %collective-permute-start.45 = (bf16[11,32,256]{2,1,0:T(8,128)(2,1)S(1)}, bf16[11,32,256]{2,1,0:T(8,128)(2,1)S(1)}, u32[]{:S(2)}, u32[]{:S(2)}) collective-permute-start(bf16[11,32,256]{2,1,0:T(8,128)(2,1)S(1)} %shard_map.83), channel_id=1, source_target_pairs={{0,4},{4,0},{8,12},{12,8},{16,20},{20,16},{24,28},{28,24},{1,5},{5... | collective-permute-start | bytes 540680 | tf_op jit(solution)/shard_map/ppermute | solution.py:301
  116.8 6.4 %collective-permute-start.54 = (bf16[2,2,32,256]{3,2,1,0:T(8,128)(2,1)S(1)}, bf16[2,2,32,256]{3,2,1,0:T(8,128)(2,1)S(1)}, u32[]{:S(2)}, u32[]{:S(2)}) collective-permute-start(bf16[2,2,32,256]{3,2,1,0:T(8,128)(2,1)S(1)} %get-tuple-element.72.refs_0_), channel_id=1, source_target_pairs={{0,2},{1,3},{2,0},{3,1},{4,6},{5,7},{6,4},{7,5},{8,10},{9,11},{10,... | collective-permute-start | bytes 196616 | tf_op jit(solution)/shard_map/ppermute | solution.py:304
  118.5 6.2 %collective-permute-start.55 = (bf16[2,2,32,256]{3,2,1,0:T(8,128)(2,1)S(1)}, bf16[2,2,32,256]{3,2,1,0:T(8,128)(2,1)S(1)}, u32[]{:S(2)}, u32[]{:S(2)}) collective-permute-start(bf16[2,2,32,256]{3,2,1,0:T(8,128)(2,1)S(1)} %get-tuple-element.72.refs_0_), channel_id=1, source_target_pairs={{0,3},{1,2},{2,1},{3,0},{4,7},{5,6},{6,5},{7,4},{8,11},{9,10},{10,... | collective-permute-start | bytes 196616 | tf_op jit(solution)/shard_map/ppermute | solution.py:304
  125.6 5.7 %collective-permute-start.47 = (bf16[2,32,256]{2,1,0:T(8,128)(2,1)S(1)}, bf16[2,32,256]{2,1,0:T(8,128)(2,1)S(1)}, u32[]{:S(2)}, u32[]{:S(2)}) collective-permute-start(bf16[2,32,256]{2,1,0:T(8,128)(2,1)S(1)} %shard_map.84.refs_20_.refs_21_), channel_id=1, source_target_pairs={{0,2},{1,3},{2,0},{3,1},{4,6},{5,7},{6,4},{7,5},{8,10},{9,11},{10,... | collective-permute-start | bytes 98312 | tf_op jit(solution)/shard_map/ppermute | solution.py:304
  127.6 5.7 %collective-permute-start.48 = (bf16[2,32,256]{2,1,0:T(8,128)(2,1)S(1)}, bf16[2,32,256]{2,1,0:T(8,128)(2,1)S(1)}, u32[]{:S(2)}, u32[]{:S(2)}) collective-permute-start(bf16[2,32,256]{2,1,0:T(8,128)(2,1)S(1)} %shard_map.84.refs_20_.refs_21_), channel_id=1, source_target_pairs={{0,3},{1,2},{2,1},{3,0},{4,7},{5,6},{6,5},{7,4},{8,11},{9,10},{10,... | collective-permute-start | bytes 98312 | tf_op jit(solution)/shard_map/ppermute | solution.py:304
  (27 other events, 108.4 us)

commit v4 on v3

--- a/solution.py
+++ b/solution.py
@@ -167,7 +167,7 @@
             copy.wait()
 
     return call(body, [((LR, slots + 1) + blocks.shape[2:], BF16)], [inverses, blocks, *after],
-                specs=[HBM] * 2 + [VM] * len(after), scratch=[pltpu.SemaphoreType.DMA((2,))])[0]
+                specs=[HBM] * 2 + [SM if x.dtype == jnp.int32 else VM for x in after], scratch=[pltpu.SemaphoreType.DMA((2,))])[0]
 
 
 def halves(rhs, half):
@@ -284,7 +284,9 @@
             out[(LEVELS - 1) * LR + i, theirs_at] = last_ref[i]
 
     ins = [*[x for _, x, _ in found + late], swapped, own, last_swapped]
-    return call(body, [(shape, BF16)], ins)[0]
+    ins = [pltpu.with_memory_space_constraint(x, pltpu.VMEM) for x in ins]
+    return pl.pallas_call(body, out_shape=jax.ShapeDtypeStruct(shape, BF16), in_specs=[VM] * len(ins), out_specs=VM,
+                          compiler_params=pltpu.CompilerParams(vmem_limit_bytes=LIMIT))(*ins)
 
 
 def body(rhs, blocks, inverses, columns, counts):
@@ -340,6 +342,13 @@
             late = [([newest - g for g in range(groups)], y)] if paired else [([i], x) for i, x in enumerate(solved)]
             first = min(min(levels) for levels, _ in late)
             swapped = prow_swap(pack(found, [x for _, x in late], first), 1)
+        if level == 1 and groups > 1:
+            held[2] = stage(2, inverses, blocks, (table,))
+            other[2] = prow_swap(held[2], 1)
+        if level == 2 and level + groups - 1 < LEVELS:
+            later = level + groups - 1
+            held[later] = stage(later, inverses, blocks, (y,))
+            other[later] = prow_swap(held[later], 1)
         store, *sums = update(level, table, store, pieces, held[level], other[level])
         if last:
             parts = share(sums[0])
@@ -351,7 +360,7 @@
         terms = [between(sums[0], newest, level, 0)]
         terms.append(between(sums[1], newest, level, 1))
         reach = level + groups
-        for later in [reach] if level > 1 else range(2, reach + 1):
+        for later in [reach] if level > 1 else range(3, reach):
             if later < LEVELS:
                 held[later] = stage(later, inverses, blocks, sums)
                 other[later] = prow_swap(held[later], 1)

time: 135 us -> 136 us (level)
  starting transfers between devices: 63.3 us -> 68 us
  waiting for transfers between devices: 50.8 us -> 47.7 us
    ppermute x12, waiting for transfers between devices: 8.07 us -> 4.57 us  [pcol_swap(): return lax.ppermute(x, 'pcol', [(i, i ^ k) for i in range(pcol_count)])]
    ppermute x33, starting transfers between devices: 27.7 us -> 30.7 us  [prow_swap(): return lax.ppermute(x, 'prow', [(i, i ^ k) for i in range(prow_count)])]
    ppermute x33, waiting for transfers between devices: 20.8 us -> 22.5 us  [prow_swap(): return lax.ppermute(x, 'prow', [(i, i ^ k) for i in range(prow_count)])]
    ppermute x12, starting transfers between devices: 24.8 us -> 26.3 us  [between(): return lax.ppermute(x, 'pcol', sorted(set(pairs)))]
    pallas_call x33 -> x32, Pallas kernels: 17.4 us -> 17.1 us  [call(): pl.pallas_call(body, out_shape=[pltpu.VMEM(shape, kind) for shape, kind i...]
  transfers between devices with their start and end apart: 57 -> 57, of which waited for: 33 -> 34; matrix products, arithmetic and copies ran while one was open for 1% -> 1% of each run, Pallas kernels for 11% -> 12%
where the time goes in v4:
time: 136 us
  starting transfers between devices  68 us (50%)
  waiting for transfers between devices  47.7 us (35%)
  Pallas kernels  19 us (14%)
    ppermute x33, starting transfers between devices, prow_swap(): return lax.ppermute(x, 'prow', [(i, i ^ k) for i in range(prow_count)])  30.7 us
    ppermute x12, starting transfers between devices, between(): return lax.ppermute(x, 'pcol', sorted(set(pairs)))  26.3 us
    ppermute x33, waiting for transfers between devices, prow_swap(): return lax.ppermute(x, 'prow', [(i, i ^ k) for i in range(prow_count)])  22.5 us
    ppermute x12, waiting for transfers between devices, between(): return lax.ppermute(x, 'pcol', sorted(set(pairs)))  20.7 us
    pallas_call x32, Pallas kernels, call(): pl.pallas_call(body, out_shape=[pltpu.VMEM(shape, kind) for shape, kind i...  17.1 us
    ppermute x12, starting transfers between devices, pcol_swap(): return lax.ppermute(x, 'pcol', [(i, i ^ k) for i in range(pcol_count)])  11 us
    ppermute x12, waiting for transfers between devices, pcol_swap(): return lax.ppermute(x, 'pcol', [(i, i ^ k) for i in range(pcol_count)])  4.57 us
  transfers between devices with their start and end apart: 57, of which 34 were waited for; matrix products, arithmetic and copies ran while one was open for 1% of the time, Pallas kernels for 12%

profile of v4, /device:TPU:0, one launch (start us, length us, event | category | flops | bytes accessed | tf_op | source)
XLA Modules:
  0.0 135.9 jit_solution(10973171338600443164)
XLA Ops:
  10.9 2.8 %collective-permute-start.4 = (bf16[2,32,256]{2,1,0:T(8,128)(2,1)S(1)}, bf16[2,32,256]{2,1,0:T(8,128)(2,1)S(1)}, u32[]{:S(2)}, u32[]{:S(2)}) collective-permute-start(bf16[2,32,256]{2,1,0:T(8,128)(2,1)S(1)} %shard_map.58.refs_0_.old.solved_ref), channel_id=1, source_target_pairs={{0,8},{4,12},{8,0},{12,4},{16,24},{20,28},{24,16},{28,20},{1,9},{5... | collective-permute-start | bytes 98312 | tf_op jit(solution)/shard_map/ppermute | solution.py:303
  15.7 3.0 %collective-permute-start.6 = (bf16[2,32,256]{2,1,0:T(8,128)(2,1)S(1)}, bf16[2,32,256]{2,1,0:T(8,128)(2,1)S(1)}, u32[]{:S(2)}, u32[]{:S(2)}) collective-permute-start(bf16[2,32,256]{2,1,0:T(8,128)(2,1)S(1)} %shard_map.58.refs_0_.old.solved_ref), channel_id=1, source_target_pairs={{0,24},{4,28},{8,16},{12,20},{16,8},{20,12},{24,0},{28,4},{1,25},{... | collective-permute-start | bytes 98312 | tf_op jit(solution)/shard_map/ppermute | solution.py:303
  18.7 1.8 %collective-permute-done.6.refs_3_ = bf16[2,32,256]{2,1,0:T(8,128)(2,1)S(1)} collective-permute-done((bf16[2,32,256]{2,1,0:T(8,128)(2,1)S(1)}, bf16[2,32,256]{2,1,0:T(8,128)(2,1)S(1)}, u32[]{:S(2)}, u32[]{:S(2)}) %collective-permute-start.6) | collective-permute-done | bytes 32800 | tf_op jit(solution)/shard_map/ppermute | solution.py:303
  21.3 2.4 %collective-permute-start.7 = (bf16[2,32,256]{2,1,0:T(8,128)(2,1)S(1)}, bf16[2,32,256]{2,1,0:T(8,128)(2,1)S(1)}, u32[]{:S(2)}, u32[]{:S(2)}) collective-permute-start(bf16[2,32,256]{2,1,0:T(8,128)(2,1)S(1)} %get-tuple-element.44), channel_id=1, source_target_pairs={{0,2},{1,3},{2,0},{3,1},{4,6},{5,7},{6,4},{7,5},{8,10},{9,11},{10,... | collective-permute-start | bytes 98312 | tf_op jit(solution)/shard_map/ppermute | solution.py:313
  23.7 2.0 %collective-permute-start.8 = (bf16[2,32,256]{2,1,0:T(8,128)(2,1)S(1)}, bf16[2,32,256]{2,1,0:T(8,128)(2,1)S(1)}, u32[]{:S(2)}, u32[]{:S(2)}) collective-permute-start(bf16[2,32,256]{2,1,0:T(8,128)(2,1)S(1)} %get-tuple-element.45), channel_id=1, source_target_pairs={{0,3},{1,2},{2,1},{3,0},{4,7},{5,6},{6,5},{7,4},{8,11},{9,10},{10,... | collective-permute-start | bytes 98312 | tf_op jit(solution)/shard_map/ppermute | solution.py:313
  26.4 3.1 %collective-permute-done.8.refs_1_ = bf16[2,32,256]{2,1,0:T(8,128)(2,1)S(1)} collective-permute-done((bf16[2,32,256]{2,1,0:T(8,128)(2,1)S(1)}, bf16[2,32,256]{2,1,0:T(8,128)(2,1)S(1)}, u32[]{:S(2)}, u32[]{:S(2)}) %collective-permute-start.8) | collective-permute-done | bytes 32800 | tf_op jit(solution)/shard_map/ppermute | solution.py:313
  30.8 1.6 %collective-permute-start.10 = (bf16[2,32,256]{2,1,0:T(8,128)(2,1)S(1)}, bf16[2,32,256]{2,1,0:T(8,128)(2,1)S(1)}, u32[]{:S(2)}, u32[]{:S(2)}) collective-permute-start(bf16[2,32,256]{2,1,0:T(8,128)(2,1)S(1)} %shard_map.62.refs_0_.solved_ref.old), channel_id=1, source_target_pairs={{0,8},{4,12},{8,0},{12,4},{16,24},{20,28},{24,16},{28,20},{1,9},{5... | collective-permute-start | bytes 98312 | tf_op jit(solution)/shard_map/ppermute | solution.py:303
  32.3 1.5 %collective-permute-start.11 = (bf16[2,32,256]{2,1,0:T(8,128)(2,1)S(1)}, bf16[2,32,256]{2,1,0:T(8,128)(2,1)S(1)}, u32[]{:S(2)}, u32[]{:S(2)}) collective-permute-start(bf16[2,32,256]{2,1,0:T(8,128)(2,1)S(1)} %shard_map.62.refs_0_.solved_ref.old), channel_id=1, source_target_pairs={{0,16},{4,20},{8,24},{12,28},{16,0},{20,4},{24,8},{28,12},{1,17},{... | collective-permute-start | bytes 98312 | tf_op jit(solution)/shard_map/ppermute | solution.py:303
  36.3 2.4 %collective-permute-done.12.refs_3_ = bf16[2,32,256]{2,1,0:T(8,128)(2,1)S(1)} collective-permute-done((bf16[2,32,256]{2,1,0:T(8,128)(2,1)S(1)}, bf16[2,32,256]{2,1,0:T(8,128)(2,1)S(1)}, u32[]{:S(2)}, u32[]{:S(2)}) %collective-permute-start.12) | collective-permute-done | bytes 32800 | tf_op jit(solution)/shard_map/ppermute | solution.py:303
  40.1 3.5 %collective-permute-start.15 = (bf16[2,32,256]{2,1,0:T(8,128)(2,1)S(1)}, bf16[2,32,256]{2,1,0:T(8,128)(2,1)S(1)}, u32[]{:S(2)}, u32[]{:S(2)}) collective-permute-start(bf16[2,32,256]{2,1,0:T(8,128)(2,1)S(1)} %get-tuple-element.49.refs_0_), channel_id=1, source_target_pairs={{0,2},{1,3},{2,0},{3,1},{4,6},{5,7},{6,4},{7,5},{8,10},{9,11},{10,... | collective-permute-start | bytes 98312 | tf_op jit(solution)/shard_map/ppermute | solution.py:313
  45.9 3.4 %collective-permute-done.16.refs_1_.refs_3_ = bf16[2,32,256]{2,1,0:T(8,128)(2,1)S(1)} collective-permute-done((bf16[2,32,256]{2,1,0:T(8,128)(2,1)S(1)}, bf16[2,32,256]{2,1,0:T(8,128)(2,1)S(1)}, u32[]{:S(2)}, u32[]{:S(2)}) %collective-permute-start.16) | collective-permute-done | bytes 32800 | tf_op jit(solution)/shard_map/ppermute | solution.py:313
  50.6 2.4 %collective-permute-start.20 = (bf16[2,32,256]{2,1,0:T(8,128)(2,1)S(1)}, bf16[2,32,256]{2,1,0:T(8,128)(2,1)S(1)}, u32[]{:S(2)}, u32[]{:S(2)}) collective-permute-start(bf16[2,32,256]{2,1,0:T(8,128)(2,1)S(1)} %shard_map.68.refs_0_.solved_ref.old.refs_4_), channel_id=1, source_target_pairs={{0,24},{4,28},{8,16},{12,20},{16,8},{20,12},{24,0},{28,4},{1,25},{... | collective-permute-start | bytes 98312 | tf_op jit(solution)/shard_map/ppermute | solution.py:303
  58.1 3.8 %collective-permute-start.24 = (bf16[2,32,256]{2,1,0:T(8,128)(2,1)S(1)}, bf16[2,32,256]{2,1,0:T(8,128)(2,1)S(1)}, u32[]{:S(2)}, u32[]{:S(2)}) collective-permute-start(bf16[2,32,256]{2,1,0:T(8,128)(2,1)S(1)} %get-tuple-element.56.refs_1_), channel_id=1, source_target_pairs={{0,3},{1,2},{2,1},{3,0},{4,7},{5,6},{6,5},{7,4},{8,11},{9,10},{10,... | collective-permute-start | bytes 98312 | tf_op jit(solution)/shard_map/ppermute | solution.py:313
  62.5 1.6 %collective-permute-done.24.refs_1_.refs_7_ = bf16[2,32,256]{2,1,0:T(8,128)(2,1)S(1)} collective-permute-done((bf16[2,32,256]{2,1,0:T(8,128)(2,1)S(1)}, bf16[2,32,256]{2,1,0:T(8,128)(2,1)S(1)}, u32[]{:S(2)}, u32[]{:S(2)}) %collective-permute-start.24) | collective-permute-done | bytes 32800 | tf_op jit(solution)/shard_map/ppermute | solution.py:313
  68.4 1.5 %collective-permute-done.26.refs_2_ = bf16[2,32,256]{2,1,0:T(8,128)(2,1)S(1)} collective-permute-done((bf16[2,32,256]{2,1,0:T(8,128)(2,1)S(1)}, bf16[2,32,256]{2,1,0:T(8,128)(2,1)S(1)}, u32[]{:S(2)}, u32[]{:S(2)}) %collective-permute-start.26) | collective-permute-done | bytes 32800 | tf_op jit(solution)/shard_map/ppermute | solution.py:303
  69.9 2.1 %collective-permute-done.27.refs_3_ = bf16[2,32,256]{2,1,0:T(8,128)(2,1)S(1)} collective-permute-done((bf16[2,32,256]{2,1,0:T(8,128)(2,1)S(1)}, bf16[2,32,256]{2,1,0:T(8,128)(2,1)S(1)}, u32[]{:S(2)}, u32[]{:S(2)}) %collective-permute-start.27) | collective-permute-done | bytes 32800 | tf_op jit(solution)/shard_map/ppermute | solution.py:303
  74.2 4.2 %collective-permute-start.30 = (bf16[2,32,256]{2,1,0:T(8,128)(2,1)S(1)}, bf16[2,32,256]{2,1,0:T(8,128)(2,1)S(1)}, u32[]{:S(2)}, u32[]{:S(2)}) collective-permute-start(bf16[2,32,256]{2,1,0:T(8,128)(2,1)S(1)} %get-tuple-element.60.refs_0_), channel_id=1, source_target_pairs={{0,2},{1,3},{2,0},{3,1},{4,6},{5,7},{6,4},{7,5},{8,10},{9,11},{10,... | collective-permute-start | bytes 98312 | tf_op jit(solution)/shard_map/ppermute | solution.py:313
  78.4 2.6 %collective-permute-done.30.refs_0_.refs_10_ = bf16[2,32,256]{2,1,0:T(8,128)(2,1)S(1)} collective-permute-done((bf16[2,32,256]{2,1,0:T(8,128)(2,1)S(1)}, bf16[2,32,256]{2,1,0:T(8,128)(2,1)S(1)}, u32[]{:S(2)}, u32[]{:S(2)}) %collective-permute-start.30) | collective-permute-done | bytes 32800 | tf_op jit(solution)/shard_map/ppermute | solution.py:313
  81.0 3.1 %collective-permute-done.31.refs_1_.refs_11_ = bf16[2,32,256]{2,1,0:T(8,128)(2,1)S(1)} collective-permute-done((bf16[2,32,256]{2,1,0:T(8,128)(2,1)S(1)}, bf16[2,32,256]{2,1,0:T(8,128)(2,1)S(1)}, u32[]{:S(2)}, u32[]{:S(2)}) %collective-permute-start.31) | collective-permute-done | bytes 32800 | tf_op jit(solution)/shard_map/ppermute | solution.py:313
  85.4 2.4 %collective-permute-start.34 = (bf16[2,32,256]{2,1,0:T(8,128)(2,1)S(1)}, bf16[2,32,256]{2,1,0:T(8,128)(2,1)S(1)}, u32[]{:S(2)}, u32[]{:S(2)}) collective-permute-start(bf16[2,32,256]{2,1,0:T(8,128)(2,1)S(1)} %shard_map.76.refs_0_.solved_ref.old.refs_12_), channel_id=1, source_target_pairs={{0,24},{4,28},{8,16},{12,20},{16,8},{20,12},{24,0},{28,4},{1,25},{... | collective-permute-start | bytes 98312 | tf_op jit(solution)/shard_map/ppermute | solution.py:303
  92.4 4.3 %collective-permute-start.38 = (bf16[2,32,256]{2,1,0:T(8,128)(2,1)S(1)}, bf16[2,32,256]{2,1,0:T(8,128)(2,1)S(1)}, u32[]{:S(2)}, u32[]{:S(2)}) collective-permute-start(bf16[2,32,256]{2,1,0:T(8,128)(2,1)S(1)} %get-tuple-element.66.refs_1_), channel_id=1, source_target_pairs={{0,3},{1,2},{2,1},{3,0},{4,7},{5,6},{6,5},{7,4},{8,11},{9,10},{10,... | collective-permute-start | bytes 98312 | tf_op jit(solution)/shard_map/ppermute | solution.py:313
  97.3 1.6 %collective-permute-done.38.refs_1_.refs_15_ = bf16[2,32,256]{2,1,0:T(8,128)(2,1)S(1)} collective-permute-done((bf16[2,32,256]{2,1,0:T(8,128)(2,1)S(1)}, bf16[2,32,256]{2,1,0:T(8,128)(2,1)S(1)}, u32[]{:S(2)}, u32[]{:S(2)}) %collective-permute-start.38) | collective-permute-done | bytes 32800 | tf_op jit(solution)/shard_map/ppermute | solution.py:313
  104.7 2.1 %collective-permute-done.42.refs_3_ = bf16[2,32,256]{2,1,0:T(8,128)(2,1)S(1)} collective-permute-done((bf16[2,32,256]{2,1,0:T(8,128)(2,1)S(1)}, bf16[2,32,256]{2,1,0:T(8,128)(2,1)S(1)}, u32[]{:S(2)}, u32[]{:S(2)}) %collective-permute-start.42) | collective-permute-done | bytes 32800 | tf_op jit(solution)/shard_map/ppermute | solution.py:303
  108.0 3.3 %collective-permute-start.44 = (bf16[2,32,256]{2,1,0:T(8,128)(2,1)S(1)}, bf16[2,32,256]{2,1,0:T(8,128)(2,1)S(1)}, u32[]{:S(2)}, u32[]{:S(2)}) collective-permute-start(bf16[2,32,256]{2,1,0:T(8,128)(2,1)S(1)} %get-tuple-element.69), channel_id=1, source_target_pairs={{0,3},{1,2},{2,1},{3,0},{4,7},{5,6},{6,5},{7,4},{8,11},{9,10},{10,... | collective-permute-start | bytes 98312 | tf_op jit(solution)/shard_map/ppermute | solution.py:313
  111.8 2.0 %collective-permute-done.44.refs_1_.refs_19_ = bf16[2,32,256]{2,1,0:T(8,128)(2,1)S(1)} collective-permute-done((bf16[2,32,256]{2,1,0:T(8,128)(2,1)S(1)}, bf16[2,32,256]{2,1,0:T(8,128)(2,1)S(1)}, u32[]{:S(2)}, u32[]{:S(2)}) %collective-permute-start.44) | collective-permute-done | bytes 32800 | tf_op jit(solution)/shard_map/ppermute | solution.py:313
  116.9 2.0 %collective-permute-start.52 = (bf16[2,32,256]{2,1,0:T(8,128)(2,1)S(1)}, bf16[2,32,256]{2,1,0:T(8,128)(2,1)S(1)}, u32[]{:S(2)}, u32[]{:S(2)}) collective-permute-start(bf16[2,32,256]{2,1,0:T(8,128)(2,1)S(1)} %shard_map.82.refs_20_.refs_0_), channel_id=1, source_target_pairs={{0,24},{4,28},{8,16},{12,20},{16,8},{20,12},{24,0},{28,4},{1,25},{... | collective-permute-start | bytes 98312 | tf_op jit(solution)/shard_map/ppermute | solution.py:303
  119.9 1.8 %collective-permute-done.52.refs_3_ = bf16[2,32,256]{2,1,0:T(8,128)(2,1)S(1)} collective-permute-done((bf16[2,32,256]{2,1,0:T(8,128)(2,1)S(1)}, bf16[2,32,256]{2,1,0:T(8,128)(2,1)S(1)}, u32[]{:S(2)}, u32[]{:S(2)}) %collective-permute-start.52) | collective-permute-done | bytes 32800 | tf_op jit(solution)/shard_map/ppermute | solution.py:303
  123.1 1.6 %collective-permute-start.54 = (bf16[2,2,32,256]{3,2,1,0:T(8,128)(2,1)S(1)}, bf16[2,2,32,256]{3,2,1,0:T(8,128)(2,1)S(1)}, u32[]{:S(2)}, u32[]{:S(2)}) collective-permute-start(bf16[2,2,32,256]{3,2,1,0:T(8,128)(2,1)S(1)} %get-tuple-element.72.refs_0_), channel_id=1, source_target_pairs={{0,2},{1,3},{2,0},{3,1},{4,6},{5,7},{6,4},{7,5},{8,10},{9,11},{10,... | collective-permute-start | bytes 196616 | tf_op jit(solution)/shard_map/ppermute | solution.py:306
  124.7 2.1 %collective-permute-start.55 = (bf16[2,2,32,256]{3,2,1,0:T(8,128)(2,1)S(1)}, bf16[2,2,32,256]{3,2,1,0:T(8,128)(2,1)S(1)}, u32[]{:S(2)}, u32[]{:S(2)}) collective-permute-start(bf16[2,2,32,256]{3,2,1,0:T(8,128)(2,1)S(1)} %get-tuple-element.72.refs_0_), channel_id=1, source_target_pairs={{0,3},{1,2},{2,1},{3,0},{4,7},{5,6},{6,5},{7,4},{8,11},{9,10},{10,... | collective-permute-start | bytes 196616 | tf_op jit(solution)/shard_map/ppermute | solution.py:306
  126.9 2.3 %collective-permute-start.47 = (bf16[2,32,256]{2,1,0:T(8,128)(2,1)S(1)}, bf16[2,32,256]{2,1,0:T(8,128)(2,1)S(1)}, u32[]{:S(2)}, u32[]{:S(2)}) collective-permute-start(bf16[2,32,256]{2,1,0:T(8,128)(2,1)S(1)} %shard_map.84.refs_20_.refs_21_), channel_id=1, source_target_pairs={{0,2},{1,3},{2,0},{3,1},{4,6},{5,7},{6,4},{7,5},{8,10},{9,11},{10,... | collective-permute-start | bytes 98312 | tf_op jit(solution)/shard_map/ppermute | solution.py:306
  129.1 2.1 %collective-permute-start.48 = (bf16[2,32,256]{2,1,0:T(8,128)(2,1)S(1)}, bf16[2,32,256]{2,1,0:T(8,128)(2,1)S(1)}, u32[]{:S(2)}, u32[]{:S(2)}) collective-permute-start(bf16[2,32,256]{2,1,0:T(8,128)(2,1)S(1)} %shard_map.84.refs_20_.refs_21_), channel_id=1, source_target_pairs={{0,3},{1,2},{2,1},{3,0},{4,7},{5,6},{6,5},{7,4},{8,11},{9,10},{10,... | collective-permute-start | bytes 98312 | tf_op jit(solution)/shard_map/ppermute | solution.py:306
  132.7 2.1 %collective-permute-done.48.refs_26_.refs_27_ = bf16[2,32,256]{2,1,0:T(8,128)(2,1)S(1)} collective-permute-done((bf16[2,32,256]{2,1,0:T(8,128)(2,1)S(1)}, bf16[2,32,256]{2,1,0:T(8,128)(2,1)S(1)}, u32[]{:S(2)}, u32[]{:S(2)}) %collective-permute-start.48) | collective-permute-done | bytes 32800 | tf_op jit(solution)/shard_map/ppermute | solution.py:306
  (123 shorter events, 56.8 us)
Async XLA Ops:
  1.3 19.2 %collective-permute-start.1 = (bf16[2,5,256,256]{3,2,1,0:T(8,128)(2,1)S(1)}, bf16[2,5,256,256]{3,2,1,0:T(8,128)(2,1)S(1)}, u32[]{:S(2)}, u32[]{:S(2)}) collective-permute-start(bf16[2,5,256,256]{3,2,1,0:T(8,128)(2,1)S(1)} %shard_map.56.own_ref.io), channel_id=1, source_target_pairs={{0,4},{4,0},{8,12},{12,8},{16,20},{20,16},{24,28},{28,24},{1,5},{5... | collective-permute-start | bytes 3932168 | tf_op jit(solution)/shard_map/ppermute | solution.py:303
  2.9 22.8 %collective-permute-start = (bf16[16,32,256]{2,1,0:T(8,128)(2,1)S(1)}, bf16[16,32,256]{2,1,0:T(8,128)(2,1)S(1)}, u32[]{:S(2)}, u32[]{:S(2)}) collective-permute-start(bf16[16,32,256]{2,1,0:T(8,128)(2,1)S(1)} %get-tuple-element.41), channel_id=1, source_target_pairs={{0,4},{4,0},{8,12},{12,8},{16,20},{20,16},{24,28},{28,24},{1,5},{5... | collective-permute-start | bytes 786440 | tf_op jit(solution)/shard_map/ppermute | solution.py:303
  7.8 26.5 %collective-permute-start.9 = (bf16[2,5,256,256]{3,2,1,0:T(8,128)(2,1)S(1)}, bf16[2,5,256,256]{3,2,1,0:T(8,128)(2,1)S(1)}, u32[]{:S(2)}, u32[]{:S(2)}) collective-permute-start(bf16[2,5,256,256]{3,2,1,0:T(8,128)(2,1)S(1)} %shard_map.63.own_ref.io), channel_id=1, source_target_pairs={{0,4},{4,0},{8,12},{12,8},{16,20},{20,16},{24,28},{28,24},{1,5},{5... | collective-permute-start | bytes 3932168 | tf_op jit(solution)/shard_map/ppermute | solution.py:303
  13.8 4.9 %collective-permute-start.5 = (bf16[2,32,256]{2,1,0:T(8,128)(2,1)S(1)}, bf16[2,32,256]{2,1,0:T(8,128)(2,1)S(1)}, u32[]{:S(2)}, u32[]{:S(2)}) collective-permute-start(bf16[2,32,256]{2,1,0:T(8,128)(2,1)S(1)} %shard_map.58.refs_0_.old.solved_ref), channel_id=1, source_target_pairs={{0,16},{4,20},{8,24},{12,28},{16,0},{20,4},{24,8},{28,12},{1,17},{... | collective-permute-start | bytes 98312 | tf_op jit(solution)/shard_map/ppermute | solution.py:303
  15.7 4.9 %collective-permute-start.6 = (bf16[2,32,256]{2,1,0:T(8,128)(2,1)S(1)}, bf16[2,32,256]{2,1,0:T(8,128)(2,1)S(1)}, u32[]{:S(2)}, u32[]{:S(2)}) collective-permute-start(bf16[2,32,256]{2,1,0:T(8,128)(2,1)S(1)} %shard_map.58.refs_0_.old.solved_ref), channel_id=1, source_target_pairs={{0,24},{4,28},{8,16},{12,20},{16,8},{20,12},{24,0},{28,4},{1,25},{... | collective-permute-start | bytes 98312 | tf_op jit(solution)/shard_map/ppermute | solution.py:303
  21.3 5.1 %collective-permute-start.7 = (bf16[2,32,256]{2,1,0:T(8,128)(2,1)S(1)}, bf16[2,32,256]{2,1,0:T(8,128)(2,1)S(1)}, u32[]{:S(2)}, u32[]{:S(2)}) collective-permute-start(bf16[2,32,256]{2,1,0:T(8,128)(2,1)S(1)} %get-tuple-element.44), channel_id=1, source_target_pairs={{0,2},{1,3},{2,0},{3,1},{4,6},{5,7},{6,4},{7,5},{8,10},{9,11},{10,... | collective-permute-start | bytes 98312 | tf_op jit(solution)/shard_map/ppermute | solution.py:313
  23.7 5.7 %collective-permute-start.8 = (bf16[2,32,256]{2,1,0:T(8,128)(2,1)S(1)}, bf16[2,32,256]{2,1,0:T(8,128)(2,1)S(1)}, u32[]{:S(2)}, u32[]{:S(2)}) collective-permute-start(bf16[2,32,256]{2,1,0:T(8,128)(2,1)S(1)} %get-tuple-element.45), channel_id=1, source_target_pairs={{0,3},{1,2},{2,1},{3,0},{4,7},{5,6},{6,5},{7,4},{8,11},{9,10},{10,... | collective-permute-start | bytes 98312 | tf_op jit(solution)/shard_map/ppermute | solution.py:313
  30.7 22.3 %collective-permute-start.13 = (bf16[2,5,256,256]{3,2,1,0:T(8,128)(2,1)S(1)}, bf16[2,5,256,256]{3,2,1,0:T(8,128)(2,1)S(1)}, u32[]{:S(2)}, u32[]{:S(2)}) collective-permute-start(bf16[2,5,256,256]{3,2,1,0:T(8,128)(2,1)S(1)} %shard_map.65.own_ref.io), channel_id=1, source_target_pairs={{0,4},{4,0},{8,12},{12,8},{16,20},{20,16},{24,28},{28,24},{1,5},{5... | collective-permute-start | bytes 3932168 | tf_op jit(solution)/shard_map/ppermute | solution.py:303
  33.9 4.8 %collective-permute-start.12 = (bf16[2,32,256]{2,1,0:T(8,128)(2,1)S(1)}, bf16[2,32,256]{2,1,0:T(8,128)(2,1)S(1)}, u32[]{:S(2)}, u32[]{:S(2)}) collective-permute-start(bf16[2,32,256]{2,1,0:T(8,128)(2,1)S(1)} %shard_map.62.refs_0_.solved_ref.old), channel_id=1, source_target_pairs={{0,24},{4,28},{8,16},{12,20},{16,8},{20,12},{24,0},{28,4},{1,25},{... | collective-permute-start | bytes 98312 | tf_op jit(solution)/shard_map/ppermute | solution.py:303
  40.0 27.7 %collective-permute-start.21 = (bf16[2,5,256,256]{3,2,1,0:T(8,128)(2,1)S(1)}, bf16[2,5,256,256]{3,2,1,0:T(8,128)(2,1)S(1)}, u32[]{:S(2)}, u32[]{:S(2)}) collective-permute-start(bf16[2,5,256,256]{3,2,1,0:T(8,128)(2,1)S(1)} %shard_map.70.own_ref.io), channel_id=1, source_target_pairs={{0,4},{4,0},{8,12},{12,8},{16,20},{20,16},{24,28},{28,24},{1,5},{5... | collective-permute-start | bytes 3932168 | tf_op jit(solution)/shard_map/ppermute | solution.py:303
  40.1 5.8 %collective-permute-start.15 = (bf16[2,32,256]{2,1,0:T(8,128)(2,1)S(1)}, bf16[2,32,256]{2,1,0:T(8,128)(2,1)S(1)}, u32[]{:S(2)}, u32[]{:S(2)}) collective-permute-start(bf16[2,32,256]{2,1,0:T(8,128)(2,1)S(1)} %get-tuple-element.49.refs_0_), channel_id=1, source_target_pairs={{0,2},{1,3},{2,0},{3,1},{4,6},{5,7},{6,4},{7,5},{8,10},{9,11},{10,... | collective-permute-start | bytes 98312 | tf_op jit(solution)/shard_map/ppermute | solution.py:313
  43.6 5.7 %collective-permute-start.16 = (bf16[2,32,256]{2,1,0:T(8,128)(2,1)S(1)}, bf16[2,32,256]{2,1,0:T(8,128)(2,1)S(1)}, u32[]{:S(2)}, u32[]{:S(2)}) collective-permute-start(bf16[2,32,256]{2,1,0:T(8,128)(2,1)S(1)} %get-tuple-element.50.refs_1_), channel_id=1, source_target_pairs={{0,3},{1,2},{2,1},{3,0},{4,7},{5,6},{6,5},{7,4},{8,11},{9,10},{10,... | collective-permute-start | bytes 98312 | tf_op jit(solution)/shard_map/ppermute | solution.py:313
  57.4 30.4 %collective-permute-start.28 = (bf16[2,5,256,256]{3,2,1,0:T(8,128)(2,1)S(1)}, bf16[2,5,256,256]{3,2,1,0:T(8,128)(2,1)S(1)}, u32[]{:S(2)}, u32[]{:S(2)}) collective-permute-start(bf16[2,5,256,256]{3,2,1,0:T(8,128)(2,1)S(1)} %shard_map.74.own_ref.io), channel_id=1, source_target_pairs={{0,4},{4,0},{8,12},{12,8},{16,20},{20,16},{24,28},{28,24},{1,5},{5... | collective-permute-start | bytes 3932168 | tf_op jit(solution)/shard_map/ppermute | solution.py:303
  57.6 5.0 %collective-permute-start.23 = (bf16[2,32,256]{2,1,0:T(8,128)(2,1)S(1)}, bf16[2,32,256]{2,1,0:T(8,128)(2,1)S(1)}, u32[]{:S(2)}, u32[]{:S(2)}) collective-permute-start(bf16[2,32,256]{2,1,0:T(8,128)(2,1)S(1)} %get-tuple-element.55.refs_0_), channel_id=1, source_target_pairs={{0,2},{1,3},{2,0},{3,1},{4,6},{5,7},{6,4},{7,5},{8,10},{9,11},{10,... | collective-permute-start | bytes 98312 | tf_op jit(solution)/shard_map/ppermute | solution.py:313
  58.1 6.1 %collective-permute-start.24 = (bf16[2,32,256]{2,1,0:T(8,128)(2,1)S(1)}, bf16[2,32,256]{2,1,0:T(8,128)(2,1)S(1)}, u32[]{:S(2)}, u32[]{:S(2)}) collective-permute-start(bf16[2,32,256]{2,1,0:T(8,128)(2,1)S(1)} %get-tuple-element.56.refs_1_), channel_id=1, source_target_pairs={{0,3},{1,2},{2,1},{3,0},{4,7},{5,6},{6,5},{7,4},{8,11},{9,10},{10,... | collective-permute-start | bytes 98312 | tf_op jit(solution)/shard_map/ppermute | solution.py:313
  73.3 29.2 %collective-permute-start.35 = (bf16[2,5,256,256]{3,2,1,0:T(8,128)(2,1)S(1)}, bf16[2,5,256,256]{3,2,1,0:T(8,128)(2,1)S(1)}, u32[]{:S(2)}, u32[]{:S(2)}) collective-permute-start(bf16[2,5,256,256]{3,2,1,0:T(8,128)(2,1)S(1)} %shard_map.78.own_ref.io), channel_id=1, source_target_pairs={{0,4},{4,0},{8,12},{12,8},{16,20},{20,16},{24,28},{28,24},{1,5},{5... | collective-permute-start | bytes 3932168 | tf_op jit(solution)/shard_map/ppermute | solution.py:303
  73.4 5.0 %collective-permute-start.22 = (bf16[2,32,256]{2,1,0:T(8,128)(2,1)S(1)}, bf16[2,32,256]{2,1,0:T(8,128)(2,1)S(1)}, u32[]{:S(2)}, u32[]{:S(2)}) collective-permute-start(bf16[2,32,256]{2,1,0:T(8,128)(2,1)S(1)} %get-tuple-element.54), channel_id=1, source_target_pairs={{0,1},{1,0},{2,3},{3,2},{4,5},{5,4},{6,7},{7,6},{8,9},{9,8},{10,11... | collective-permute-start | bytes 98312 | tf_op jit(solution)/shard_map/ppermute | solution.py:306
  74.2 6.8 %collective-permute-start.30 = (bf16[2,32,256]{2,1,0:T(8,128)(2,1)S(1)}, bf16[2,32,256]{2,1,0:T(8,128)(2,1)S(1)}, u32[]{:S(2)}, u32[]{:S(2)}) collective-permute-start(bf16[2,32,256]{2,1,0:T(8,128)(2,1)S(1)} %get-tuple-element.60.refs_0_), channel_id=1, source_target_pairs={{0,2},{1,3},{2,0},{3,1},{4,6},{5,7},{6,4},{7,5},{8,10},{9,11},{10,... | collective-permute-start | bytes 98312 | tf_op jit(solution)/shard_map/ppermute | solution.py:313
  78.4 5.7 %collective-permute-start.31 = (bf16[2,32,256]{2,1,0:T(8,128)(2,1)S(1)}, bf16[2,32,256]{2,1,0:T(8,128)(2,1)S(1)}, u32[]{:S(2)}, u32[]{:S(2)}) collective-permute-start(bf16[2,32,256]{2,1,0:T(8,128)(2,1)S(1)} %get-tuple-element.61.refs_1_), channel_id=1, source_target_pairs={{0,3},{1,2},{2,1},{3,0},{4,7},{5,6},{6,5},{7,4},{8,11},{9,10},{10,... | collective-permute-start | bytes 98312 | tf_op jit(solution)/shard_map/ppermute | solution.py:313
  92.2 29.5 %collective-permute-start.49 = (bf16[2,5,256,256]{3,2,1,0:T(8,128)(2,1)S(1)}, bf16[2,5,256,256]{3,2,1,0:T(8,128)(2,1)S(1)}, u32[]{:S(2)}, u32[]{:S(2)}) collective-permute-start(bf16[2,5,256,256]{3,2,1,0:T(8,128)(2,1)S(1)} %shard_map.85.own_ref.io), channel_id=1, source_target_pairs={{0,4},{4,0},{8,12},{12,8},{16,20},{20,16},{24,28},{28,24},{1,5},{5... | collective-permute-start | bytes 3932168 | tf_op jit(solution)/shard_map/ppermute | solution.py:303
  92.3 5.0 %collective-permute-start.37 = (bf16[2,32,256]{2,1,0:T(8,128)(2,1)S(1)}, bf16[2,32,256]{2,1,0:T(8,128)(2,1)S(1)}, u32[]{:S(2)}, u32[]{:S(2)}) collective-permute-start(bf16[2,32,256]{2,1,0:T(8,128)(2,1)S(1)} %get-tuple-element.65.refs_0_), channel_id=1, source_target_pairs={{0,2},{1,3},{2,0},{3,1},{4,6},{5,7},{6,4},{7,5},{8,10},{9,11},{10,... | collective-permute-start | bytes 98312 | tf_op jit(solution)/shard_map/ppermute | solution.py:313
  92.4 6.5 %collective-permute-start.38 = (bf16[2,32,256]{2,1,0:T(8,128)(2,1)S(1)}, bf16[2,32,256]{2,1,0:T(8,128)(2,1)S(1)}, u32[]{:S(2)}, u32[]{:S(2)}) collective-permute-start(bf16[2,32,256]{2,1,0:T(8,128)(2,1)S(1)} %get-tuple-element.66.refs_1_), channel_id=1, source_target_pairs={{0,3},{1,2},{2,1},{3,0},{4,7},{5,6},{6,5},{7,4},{8,11},{9,10},{10,... | collective-permute-start | bytes 98312 | tf_op jit(solution)/shard_map/ppermute | solution.py:313
  99.0 4.9 %collective-permute-start.40 = (bf16[2,32,256]{2,1,0:T(8,128)(2,1)S(1)}, bf16[2,32,256]{2,1,0:T(8,128)(2,1)S(1)}, u32[]{:S(2)}, u32[]{:S(2)}) collective-permute-start(bf16[2,32,256]{2,1,0:T(8,128)(2,1)S(1)} %shard_map.80.refs_0_.old.refs_16_), channel_id=1, source_target_pairs={{0,8},{4,12},{8,0},{12,4},{16,24},{20,28},{24,16},{28,20},{1,9},{5... | collective-permute-start | bytes 98312 | tf_op jit(solution)/shard_map/ppermute | solution.py:303
  103.2 8.6 %collective-permute-start.36 = (bf16[2,32,256]{2,1,0:T(8,128)(2,1)S(1)}, bf16[2,32,256]{2,1,0:T(8,128)(2,1)S(1)}, u32[]{:S(2)}, u32[]{:S(2)}) collective-permute-start(bf16[2,32,256]{2,1,0:T(8,128)(2,1)S(1)} %get-tuple-element.64), channel_id=1, source_target_pairs={{0,1},{1,0},{2,3},{3,2},{4,5},{5,4},{6,7},{7,6},{8,9},{9,8},{10,11... | collective-permute-start | bytes 98312 | tf_op jit(solution)/shard_map/ppermute | solution.py:306
  106.8 5.0 %collective-permute-start.43 = (bf16[2,32,256]{2,1,0:T(8,128)(2,1)S(1)}, bf16[2,32,256]{2,1,0:T(8,128)(2,1)S(1)}, u32[]{:S(2)}, u32[]{:S(2)}) collective-permute-start(bf16[2,32,256]{2,1,0:T(8,128)(2,1)S(1)} %get-tuple-element.68), channel_id=1, source_target_pairs={{0,2},{1,3},{2,0},{3,1},{4,6},{5,7},{6,4},{7,5},{8,10},{9,11},{10,... | collective-permute-start | bytes 98312 | tf_op jit(solution)/shard_map/ppermute | solution.py:313
  108.0 5.7 %collective-permute-start.44 = (bf16[2,32,256]{2,1,0:T(8,128)(2,1)S(1)}, bf16[2,32,256]{2,1,0:T(8,128)(2,1)S(1)}, u32[]{:S(2)}, u32[]{:S(2)}) collective-permute-start(bf16[2,32,256]{2,1,0:T(8,128)(2,1)S(1)} %get-tuple-element.69), channel_id=1, source_target_pairs={{0,3},{1,2},{2,1},{3,0},{4,7},{5,6},{6,5},{7,4},{8,11},{9,10},{10,... | collective-permute-start | bytes 98312 | tf_op jit(solution)/shard_map/ppermute | solution.py:313
  115.3 11.6 %collective-permute-start.45 = (bf16[11,32,256]{2,1,0:T(8,128)(2,1)S(1)}, bf16[11,32,256]{2,1,0:T(8,128)(2,1)S(1)}, u32[]{:S(2)}, u32[]{:S(2)}) collective-permute-start(bf16[11,32,256]{2,1,0:T(8,128)(2,1)S(1)} %shard_map.83), channel_id=1, source_target_pairs={{0,4},{4,0},{8,12},{12,8},{16,20},{20,16},{24,28},{28,24},{1,5},{5... | collective-permute-start | bytes 540680 | tf_op jit(solution)/shard_map/ppermute | solution.py:303
  122.4 6.7 %collective-permute-start.53 = (bf16[2,2,32,256]{3,2,1,0:T(8,128)(2,1)S(1)}, bf16[2,2,32,256]{3,2,1,0:T(8,128)(2,1)S(1)}, u32[]{:S(2)}, u32[]{:S(2)}) collective-permute-start(bf16[2,2,32,256]{3,2,1,0:T(8,128)(2,1)S(1)} %get-tuple-element.72.refs_0_), channel_id=1, source_target_pairs={{0,1},{1,0},{2,3},{3,2},{4,5},{5,4},{6,7},{7,6},{8,9},{9,8},{10,11... | collective-permute-start | bytes 196616 | tf_op jit(solution)/shard_map/ppermute | solution.py:306
  123.1 8.1 %collective-permute-start.54 = (bf16[2,2,32,256]{3,2,1,0:T(8,128)(2,1)S(1)}, bf16[2,2,32,256]{3,2,1,0:T(8,128)(2,1)S(1)}, u32[]{:S(2)}, u32[]{:S(2)}) collective-permute-start(bf16[2,2,32,256]{3,2,1,0:T(8,128)(2,1)S(1)} %get-tuple-element.72.refs_0_), channel_id=1, source_target_pairs={{0,2},{1,3},{2,0},{3,1},{4,6},{5,7},{6,4},{7,5},{8,10},{9,11},{10,... | collective-permute-start | bytes 196616 | tf_op jit(solution)/shard_map/ppermute | solution.py:306
  124.7 6.5 %collective-permute-start.55 = (bf16[2,2,32,256]{3,2,1,0:T(8,128)(2,1)S(1)}, bf16[2,2,32,256]{3,2,1,0:T(8,128)(2,1)S(1)}, u32[]{:S(2)}, u32[]{:S(2)}) collective-permute-start(bf16[2,2,32,256]{3,2,1,0:T(8,128)(2,1)S(1)} %get-tuple-element.72.refs_0_), channel_id=1, source_target_pairs={{0,3},{1,2},{2,1},{3,0},{4,7},{5,6},{6,5},{7,4},{8,11},{9,10},{10,... | collective-permute-start | bytes 196616 | tf_op jit(solution)/shard_map/ppermute | solution.py:306
  126.9 5.8 %collective-permute-start.47 = (bf16[2,32,256]{2,1,0:T(8,128)(2,1)S(1)}, bf16[2,32,256]{2,1,0:T(8,128)(2,1)S(1)}, u32[]{:S(2)}, u32[]{:S(2)}) collective-permute-start(bf16[2,32,256]{2,1,0:T(8,128)(2,1)S(1)} %shard_map.84.refs_20_.refs_21_), channel_id=1, source_target_pairs={{0,2},{1,3},{2,0},{3,1},{4,6},{5,7},{6,4},{7,5},{8,10},{9,11},{10,... | collective-permute-start | bytes 98312 | tf_op jit(solution)/shard_map/ppermute | solution.py:306
  129.1 5.7 %collective-permute-start.48 = (bf16[2,32,256]{2,1,0:T(8,128)(2,1)S(1)}, bf16[2,32,256]{2,1,0:T(8,128)(2,1)S(1)}, u32[]{:S(2)}, u32[]{:S(2)}) collective-permute-start(bf16[2,32,256]{2,1,0:T(8,128)(2,1)S(1)} %shard_map.84.refs_20_.refs_21_), channel_id=1, source_target_pairs={{0,3},{1,2},{2,1},{3,0},{4,7},{5,6},{6,5},{7,4},{8,11},{9,10},{10,... | collective-permute-start | bytes 98312 | tf_op jit(solution)/shard_map/ppermute | solution.py:306
  (27 other events, 108.2 us)
